TPU v7x, 256 devices: a whole 4x4x8 slice. The times are simulated.
256 devices in a mesh: dp: 32 (over y, z), vocab: 8 (over x, core).
Axes of the slice: x: 4, y: 4, z: 8, core: 2. Of those that a mesh axis runs over, the one named last changes fastest.
Arguments:
- hidden_states: bfloat16 [16384, 2048], P('dp', 'vocab'), may hold values from -12 to 12
- teacher_logits: bfloat16 [16384, 16384], P('dp', 'vocab'), may hold values from -24 to 240
- head_weight: bfloat16 [2048, 16384], P(None, 'vocab'), as said below
Outputs:
- kl_per_token: float32 [16384], P('dp')
- hidden_grad: bfloat16 [16384, 2048], P('dp', 'vocab')
- head_grad: float32 [2048, 16384], P('dp', 'vocab')
Inputs may be any that keep to these rules, and one draw needn't show every extreme that they name: `head_weight`: every entry's magnitude is at most 18 / sqrt(2048).
All inputs are finite; a program needn't handle non-finite values.
Results may differ from a plain program's by a relative error of at most 0.014.
Values may be sent and summed in bfloat16 or wider, within the bound.
No kernel may reach another device: no remote copies, remote signals or barrier semaphores. Data moves between devices by JAX's collectives and lax.ppermute only.
A program may use at most 128 MiB of HBM per device.

v0:
```python
import jax
import jax.numpy as jnp
from jax import lax
from jax.sharding import Mesh
from jax.sharding import PartitionSpec as P

MICRO = 2
DP = ("dp_0", "dp_1")


grad_scale = 8.0


def in_order(pieces, dim):
    lengths = list(pieces.shape[1:])
    lengths[dim] *= pieces.shape[0]
    return jnp.moveaxis(pieces, 0, dim).reshape(lengths)


def sent_to_all(array, axis):
    copies = jnp.broadcast_to(array, (lax.axis_size(axis), *array.shape))
    return lax.all_to_all(copies, axis, split_axis=0, concat_axis=0, tiled=True)


def gathered_copies(array, axis, dim):
    return in_order(sent_to_all(array, axis), dim)


def gathered_once(array, axis):
    leaves = jax.tree.leaves(array)
    turns = sorted(range(len(leaves)), key=lambda k: -leaves[k].size)
    width = (1, *leaves[turns[0]].shape)[-1]
    lines = [
        jnp.pad(leaves[k].reshape(-1), (0, -leaves[k].size % width)).reshape(-1, width)
        for k in turns
    ]
    both, at, found = (sent_to_all(jnp.concatenate(lines), axis), 0, {})
    for k, line in zip(turns, lines):
        share = both[:, at : at + len(line)].reshape(len(both), -1)
        found[k] = share[:, : leaves[k].size].reshape(-1, *leaves[k].shape)
        at += len(line)
    numbers = iter(range(len(leaves)))
    return jax.tree.map(lambda _: found[next(numbers)], array)


def folded_in_pairs(pieces, combine):
    while len(jax.tree.leaves(pieces)[0]) > 1:
        pieces = jax.vmap(combine)(
            *(jax.tree.map(lambda part: part[side::2], pieces) for side in (0, 1))
        )
    return jax.tree.map(lambda part: part[0], pieces)


def merged_2(array, axis, combine):
    pieces = gathered_once(array, axis)
    return folded_in_pairs(pieces, combine)


def in_blocks(array, dim, size):
    before, after = (array.shape[:dim], array.shape[dim + 1 :])
    return jnp.moveaxis(array.reshape(*before, size, -1, *after), dim, 0)


def summed_on_arrival(array, axis, dim):
    size = lax.axis_size(axis)
    pieces = lax.all_to_all(in_blocks(array, dim, size), axis, 0, 0, tiled=True)
    return jnp.sum(pieces.astype(jnp.float32), axis=0)


def sum_by_axis(array, axes, dim):
    if not axes:
        return array
    nearer = lax.psum_scatter(array, axes[0], scatter_dimension=dim, tiled=True)
    return sum_by_axis(nearer, axes[1:], dim)


def combine_rows(left_stats, right_stats):
    student_peak = jnp.maximum(left_stats[0], right_stats[0])
    left_scale = jnp.exp(left_stats[0] - student_peak)
    right_scale = jnp.exp(right_stats[0] - student_peak)
    student_total = left_stats[1] * left_scale + right_stats[1] * right_scale
    teacher_peak = jnp.maximum(left_stats[2], right_stats[2])
    left_weight = jnp.exp(left_stats[2] - teacher_peak)
    right_weight = jnp.exp(right_stats[2] - teacher_peak)
    teacher_total = left_stats[3] * left_weight + right_stats[3] * right_weight
    cross_term = left_stats[4] * left_weight + right_stats[4] * right_weight
    return (student_peak, student_total, teacher_peak, teacher_total, cross_term)


def micro_batch(hidden_part, teacher_part, head_weight):
    gathered = gathered_copies(hidden_part, "vocab", 1)
    student = jnp.dot(gathered, head_weight, preferred_element_type=jnp.float32)
    teacher = teacher_part.astype(jnp.float32)
    student_peak = jnp.max(student, axis=1)
    teacher_peak = jnp.max(teacher, axis=1)
    student_terms = jnp.exp(student - student_peak[:, None])
    teacher_terms = jnp.exp(teacher - teacher_peak[:, None])
    merged = merged_2(
        (
            student_peak,
            jnp.sum(student_terms, axis=1),
            teacher_peak,
            jnp.sum(teacher_terms, axis=1),
            jnp.sum(teacher_terms * (teacher - student), axis=1),
        ),
        "vocab",
        combine_rows,
    )
    student_max, student_total, teacher_max, teacher_total, cross_term = merged
    student_terms = student_terms * jnp.exp(student_peak - student_max)[:, None]
    teacher_terms = teacher_terms * jnp.exp(teacher_peak - teacher_max)[:, None]
    divergence = (
        cross_term / teacher_total
        - teacher_max
        - jnp.log(teacher_total)
        + student_max
        + jnp.log(student_total)
    )
    logit_grad = (
        grad_scale
        * (student_terms / student_total[:, None] - teacher_terms / teacher_total[:, None])
    ).astype(jnp.bfloat16)
    partial_value = lax.dot_general(
        logit_grad, head_weight, (((1,), (1,)), ((), ())), preferred_element_type=jnp.float32
    )
    hidden_grad = summed_on_arrival(partial_value.astype(jnp.bfloat16), "vocab", 1).astype(
        jnp.bfloat16
    )
    return (gathered, logit_grad, hidden_grad, divergence)


def per_device(hidden_states, teacher_logits, head_weight):
    device_rows = hidden_states.shape[0]
    micro_rows = device_rows // MICRO
    model_width = head_weight.shape[0]
    local_vocab = head_weight.shape[1]
    initial = jnp.zeros((model_width, local_vocab), jnp.float32)
    running = initial
    collected = []
    for number in range(MICRO):
        row_begin = number * micro_rows
        row_end = row_begin + micro_rows
        accumulate_running = running
        gathered, logit_grad, accumulate_hidden_grad, accumulate_divergence = micro_batch(
            hidden_states[row_begin:row_end], teacher_logits[row_begin:row_end], head_weight
        )
        accumulate_running = accumulate_running + lax.dot_general(
            gathered, logit_grad, (((0,), (0,)), ((), ())), preferred_element_type=jnp.float32
        )
        running = accumulate_running
        produced = (accumulate_hidden_grad, accumulate_divergence)
        collected.append(produced)
    results = tuple((jnp.concatenate(column, axis=0) for column in zip(*collected)))
    hidden_grad = results[0]
    divergence = results[1]
    head_grad = sum_by_axis(running.astype(jnp.bfloat16), DP, 0).astype(jnp.float32)
    return (divergence, hidden_grad, head_grad)


def solution(mesh):
    split = Mesh(mesh.devices.reshape(4, 8, mesh.shape["vocab"]), ("dp_0", "dp_1", "vocab"))
    placed = (P(DP, "vocab"), P(DP, "vocab"), P(None, "vocab"))
    return jax.shard_map(
        per_device,
        mesh=split,
        in_specs=placed,
        out_specs=(P(DP), P(DP, "vocab"), P(DP, "vocab")),
        check_vma=False,
    )
```

profile of v0, /device:TPU:1, one launch (start us, length us, event | category | flops | bytes accessed | tf_op | source)
XLA Modules:
  0.0 246.2 jit_solution(8956937565162320804)
XLA Ops:
  7.2 1.0 fusion.32
  8.2 0.1 copy.22
  8.3 1.1 broadcast_in_dim.8
  9.3 6.7 %all-to-all-start = ((bf16[8,256,256]{1,2,0:T(8,128)(2,1)}), bf16[8,256,256]{1,2,0:T(8,128)(2,1)S(1)}, u32[]{:S(2)}, u32[]{:S(2)}) async-start(bf16[8,256,256]{1,2,0:T(8,128)(2,1)} %broadcast_in_dim.8), calls=%async_computation | async-start | bytes 2097152 | tf_op jit(solution)/shard_map/all_to_all | solution.py:22
  16.0 0.0 copy-start
  16.0 0.1 copy.26
  16.1 14.9 %all-to-all-done = bf16[8,256,256]{1,2,0:T(8,128)(2,1)S(1)} async-done(((bf16[8,256,256]{1,2,0:T(8,128)(2,1)}), bf16[8,256,256]{1,2,0:T(8,128)(2,1)S(1)}, u32[]{:S(2)}, u32[]{:S(2)}) %all-to-all-start) | async-done | bytes 1048608 | tf_op jit(solution)/shard_map/all_to_all | solution.py:22
  31.0 1.0 broadcast_in_dim.10
  32.0 5.1 %all-to-all-start.2 = ((bf16[8,256,256]{1,2,0:T(8,128)(2,1)}), bf16[8,256,256]{1,2,0:T(8,128)(2,1)}, u32[]{:S(2)}, u32[]{:S(2)}) async-start(bf16[8,256,256]{1,2,0:T(8,128)(2,1)} %broadcast_in_dim.10), calls=%async_computation.2 | async-start | bytes 2097152 | tf_op jit(solution)/shard_map/all_to_all | solution.py:22
  37.1 0.0 copy-done
  37.1 0.4 slice_reduce_fusion.1
  37.5 7.1 %fusion.36 = (f32[256]{0:T(256)S(1)}, f32[256,2048]{1,0:T(8,128)}) fusion(bf16[256,2048]{0,1:T(8,128)(2,1)S(1)} %bitcast.81, bf16[2048,2048]{1,0:T(8,128)(2,1)} %param.5), kind=kOutput, calls=%fused_computation.103 | convolution fusion | flops 2148007680 | bytes 11535360 | tf_op jit(solution)/shard_map/dot_general | solution.py:92
  44.6 7.6 %all-to-all-done.2 = bf16[8,256,256]{1,2,0:T(8,128)(2,1)} async-done(((bf16[8,256,256]{1,2,0:T(8,128)(2,1)}), bf16[8,256,256]{1,2,0:T(8,128)(2,1)}, u32[]{:S(2)}, u32[]{:S(2)}) %all-to-all-start.2) | async-done | bytes 1048608 | tf_op jit(solution)/shard_map/all_to_all | solution.py:22
  52.2 0.0 copy-start.1
  52.2 6.3 %fusion.35 = (f32[256]{0:T(256)S(1)}, f32[256,2048]{1,0:T(8,128)S(1)}) fusion(bf16[256,2048]{0,1:T(8,128)(2,1)} %bitcast.16, bf16[2048,2048]{1,0:T(8,128)(2,1)} %param.5), kind=kOutput, calls=%fused_computation.102 | convolution fusion | flops 2148007680 | bytes 11535360 | tf_op jit(solution)/shard_map/dot_general | solution.py:92
  58.5 0.0 copy-done.1
  58.5 2.2 fusion.5
  60.7 0.0 copy-done.2
  60.8 0.6 broadcast_in_dim.11
  61.4 4.2 %all-to-all-start.3 = ((f32[8,5,256]{2,1,0:T(8,128)}), f32[8,5,256]{2,1,0:T(8,128)S(1)}, u32[]{:S(2)}, u32[]{:S(2)}) async-start(f32[8,5,256]{2,1,0:T(8,128)} %broadcast_in_dim.11), calls=%async_computation.3 | async-start | bytes 131072 | tf_op jit(solution)/shard_map/all_to_all | solution.py:22
  65.6 4.8 %all-to-all-done.3 = f32[8,5,256]{2,1,0:T(8,128)S(1)} async-done(((f32[8,5,256]{2,1,0:T(8,128)}), f32[8,5,256]{2,1,0:T(8,128)S(1)}, u32[]{:S(2)}, u32[]{:S(2)}) %all-to-all-start.3) | async-done | bytes 40992 | tf_op jit(solution)/shard_map/all_to_all | solution.py:22
  70.5 0.6 broadcast_in_dim.9
  71.1 4.0 %all-to-all-start.1 = ((f32[8,5,256]{2,1,0:T(8,128)}), f32[8,5,256]{2,1,0:T(8,128)S(1)}, u32[]{:S(2)}, u32[]{:S(2)}) async-start(f32[8,5,256]{2,1,0:T(8,128)} %broadcast_in_dim.9), calls=%async_computation.1 | async-start | bytes 131072 | tf_op jit(solution)/shard_map/all_to_all | solution.py:22
  75.2 0.0 reduce-scatter.5.cloned.1.call-start
  75.7 4.3 %all-to-all-done.1 = f32[8,5,256]{2,1,0:T(8,128)S(1)} async-done(((f32[8,5,256]{2,1,0:T(8,128)}), f32[8,5,256]{2,1,0:T(8,128)S(1)}, u32[]{:S(2)}, u32[]{:S(2)}) %all-to-all-start.1) | async-done | bytes 40992 | tf_op jit(solution)/shard_map/all_to_all | solution.py:22
  80.9 0.0 copy-start.3
  80.9 10.6 %fusion.27 = f32[2048,2048]{1,0:T(8,128)} fusion(bf16[256,2048]{0,1:T(8,128)(2,1)S(1)} %bitcast.82, f32[256,2048]{1,0:T(8,128)} %get-tuple-element.67, f32[256]{0:T(256)S(1)} %bitcast.125, f32[256]{0:T(256)S(1)} %get-tuple-element.68, f32[256]{0:T(256)S(1)} %bitcast.128, f32[256]{0:T(256)S(1)} %get-tuple-element.70, f32[256]{0:T(256)S(1)} %reduce_max.64, ...), kind=kOutput, calls=%fused_computation.98 | convolution fusion | flops 2152726528 | bytes 20977664 | tf_op jit(solution)/shard_map/dot_general | solution.py:147
  91.5 0.0 copy-done.3
  91.5 9.9 %fusion = bf16[2048,2048]{0,1:T(8,128)(2,1)} fusion(f32[2048,2048]{1,0:T(8,128)} %fusion.27, bf16[256,2048]{0,1:T(8,128)(2,1)} %bitcast.16, f32[256,2048]{1,0:T(8,128)S(1)} %copy-done.3, f32[256]{0:T(256)S(1)} %bitcast.119, f32[256]{0:T(256)S(1)} %get-tuple-element.63, f32[256]{0:T(256)S(1)} %bitcast.122, f32[256]{0:T(256)S(1)} %get-tuple-element.61, ...), kind=kOutput, calls=%fused_computation.1 | convolution fusion | flops 2161115136 | bytes 29366272 | tf_op jit(solution)/shard_map/dot_general | solution.py:147
  101.4 0.0 reduce-scatter.5.cloned.1.call-update
  101.4 0.0 reduce-scatter.7.cloned.1.call-start
  101.4 83.5 %reduce-scatter.5.cloned.1.call-done = bf16[512,2048]{0,1:T(8,128)(2,1)} async-done(((bf16[2048,2048]{0,1:T(8,128)(2,1)}), bf16[512,2048]{0,1:T(8,128)(2,1)}) %reduce-scatter.5.cloned.1.call-update) | async-done | bytes 2097168 | tf_op jit(solution)/shard_map/reduce_scatter | solution.py:73
  184.9 4.0 %copy.33 = bf16[512,2048]{1,0:T(8,128)(2,1)} copy(bf16[512,2048]{0,1:T(8,128)(2,1)} %reduce-scatter.5.cloned.1.call-done) | data formatting | bytes 4194304
  188.9 0.0 reduce-scatter.7.cloned.1.call-update
  188.9 6.9 %convolution_convert_fusion = bf16[256,2048]{1,0:T(8,128)(2,1)S(1)} fusion(bf16[2048,2048]{1,0:T(8,128)(2,1)} %param.5, f32[256,2048]{1,0:T(8,128)} %copy-done.2, f32[256]{0:T(256)S(1)} %bitcast.120, f32[256]{0:T(256)S(1)} %get-tuple-element.63, f32[256]{0:T(256)S(1)} %bitcast.123, f32[256]{0:T(256)S(1)} %get-tuple-element.61, f32[256]{0:T(256)S(1)} %reduce_max.65, ...), kind=kOutput, calls=%fused_computation.6 | convolution fusion | flops 2153250816 | bytes 12589056 | tf_op jit(solution)/shard_map/dot_general | solution.py:123
  195.8 1.1 copy.59
  196.9 5.0 %all-to-all-start.5 = ((bf16[8,256,256]{2,1,0:T(8,128)(2,1)}), bf16[8,256,256]{2,1,0:T(8,128)(2,1)S(1)}, u32[]{:S(2)}, u32[]{:S(2)}) async-start(bf16[8,256,256]{2,1,0:T(8,128)(2,1)} %bitcast.83), calls=%async_computation.5 | async-start | bytes 2097152 | tf_op jit(solution)/shard_map/all_to_all | solution.py:66
  201.9 6.9 %convolution_convert_fusion.1 = bf16[256,2048]{1,0:T(8,128)(2,1)S(1)} fusion(bf16[2048,2048]{1,0:T(8,128)(2,1)} %param.5, f32[256,2048]{1,0:T(8,128)} %get-tuple-element.67, f32[256]{0:T(256)S(1)} %bitcast.126, f32[256]{0:T(256)S(1)} %get-tuple-element.68, f32[256]{0:T(256)S(1)} %bitcast.129, f32[256]{0:T(256)S(1)} %get-tuple-element.70, ...), kind=kOutput, calls=%fused_computation.7 | convolution fusion | flops 2153250816 | bytes 12589056 | tf_op jit(solution)/shard_map/dot_general | solution.py:123
  208.8 1.1 copy.60
  209.8 7.0 %all-to-all-done.5 = bf16[8,256,256]{2,1,0:T(8,128)(2,1)S(1)} async-done(((bf16[8,256,256]{2,1,0:T(8,128)(2,1)}), bf16[8,256,256]{2,1,0:T(8,128)(2,1)S(1)}, u32[]{:S(2)}, u32[]{:S(2)}) %all-to-all-start.5) | async-done | bytes 1048608 | tf_op jit(solution)/shard_map/all_to_all | solution.py:66
  216.8 4.4 %all-to-all-start.4 = ((bf16[8,256,256]{2,1,0:T(8,128)(2,1)}), bf16[8,256,256]{2,1,0:T(8,128)(2,1)S(1)}, u32[]{:S(2)}, u32[]{:S(2)}) async-start(bf16[8,256,256]{2,1,0:T(8,128)(2,1)} %bitcast.70), calls=%async_computation.4 | async-start | bytes 2097152 | tf_op jit(solution)/shard_map/all_to_all | solution.py:66
  221.3 0.6 pad_maximum_fusion.1
  221.8 0.1 reduce_sum.85
  222.0 14.3 %all-to-all-done.4 = bf16[8,256,256]{2,1,0:T(8,128)(2,1)S(1)} async-done(((bf16[8,256,256]{2,1,0:T(8,128)(2,1)}), bf16[8,256,256]{2,1,0:T(8,128)(2,1)S(1)}, u32[]{:S(2)}, u32[]{:S(2)}) %all-to-all-start.4) | async-done | bytes 1048608 | tf_op jit(solution)/shard_map/all_to_all | solution.py:66
  236.3 0.1 reduce_sum.84
  236.4 0.7 pad_maximum_fusion
  237.1 1.2 copy.34
  238.4 1.0 copy.32
  (77 shorter events, 1.3 us)
Async XLA Ops:
  9.3 21.7 %all-to-all-start = ((bf16[8,256,256]{1,2,0:T(8,128)(2,1)}), bf16[8,256,256]{1,2,0:T(8,128)(2,1)S(1)}, u32[]{:S(2)}, u32[]{:S(2)}) async-start(bf16[8,256,256]{1,2,0:T(8,128)(2,1)} %broadcast_in_dim.8), calls=%async_computation | async-start | bytes 2097152 | tf_op jit(solution)/shard_map/all_to_all | solution.py:22
  16.0 21.1 %copy-start = (bf16[512,2048]{1,0:T(8,128)(2,1)S(1)}, bf16[512,2048]{1,0:T(8,128)(2,1)}, u32[]{:S(2)}) copy-start(bf16[512,2048]{1,0:T(8,128)(2,1)} %param.4) | copy-start | bytes 6291460
  32.0 20.2 %all-to-all-start.2 = ((bf16[8,256,256]{1,2,0:T(8,128)(2,1)}), bf16[8,256,256]{1,2,0:T(8,128)(2,1)}, u32[]{:S(2)}, u32[]{:S(2)}) async-start(bf16[8,256,256]{1,2,0:T(8,128)(2,1)} %broadcast_in_dim.10), calls=%async_computation.2 | async-start | bytes 2097152 | tf_op jit(solution)/shard_map/all_to_all | solution.py:22
  52.2 6.3 %copy-start.1 = (f32[256,2048]{1,0:T(8,128)S(1)}, f32[256,2048]{1,0:T(8,128)}, u32[]{:S(2)}) copy-start(f32[256,2048]{1,0:T(8,128)} %get-tuple-element.67) | copy-start | bytes 6291460
  58.5 2.2 copy-start.2
  61.4 9.1 %all-to-all-start.3 = ((f32[8,5,256]{2,1,0:T(8,128)}), f32[8,5,256]{2,1,0:T(8,128)S(1)}, u32[]{:S(2)}, u32[]{:S(2)}) async-start(f32[8,5,256]{2,1,0:T(8,128)} %broadcast_in_dim.11), calls=%async_computation.3 | async-start | bytes 131072 | tf_op jit(solution)/shard_map/all_to_all | solution.py:22
  71.1 8.9 %all-to-all-start.1 = ((f32[8,5,256]{2,1,0:T(8,128)}), f32[8,5,256]{2,1,0:T(8,128)S(1)}, u32[]{:S(2)}, u32[]{:S(2)}) async-start(f32[8,5,256]{2,1,0:T(8,128)} %broadcast_in_dim.9), calls=%async_computation.1 | async-start | bytes 131072 | tf_op jit(solution)/shard_map/all_to_all | solution.py:22
  75.2 109.8 %reduce-scatter.5.cloned.1.call-start = ((), (), s32[]{:S(2)}) async-start(), calls=%async_computation.8 | async-start | bytes 10485760 | tf_op jit(solution)/shard_map/reduce_scatter | solution.py:73
  80.9 10.6 %copy-start.3 = (f32[256,2048]{1,0:T(8,128)S(1)}, f32[256,2048]{1,0:T(8,128)}, u32[]{:S(2)}) copy-start(f32[256,2048]{1,0:T(8,128)} %copy-done.2) | copy-start | bytes 6291460
  101.4 135.7 %reduce-scatter.7.cloned.1.call-start = ((), (), s32[]{:S(2)}) async-start(), calls=%async_computation.9 | async-start | bytes 2359296
  196.9 20.0 %all-to-all-start.5 = ((bf16[8,256,256]{2,1,0:T(8,128)(2,1)}), bf16[8,256,256]{2,1,0:T(8,128)(2,1)S(1)}, u32[]{:S(2)}, u32[]{:S(2)}) async-start(bf16[8,256,256]{2,1,0:T(8,128)(2,1)} %bitcast.83), calls=%async_computation.5 | async-start | bytes 2097152 | tf_op jit(solution)/shard_map/all_to_all | solution.py:66
  216.8 19.4 %all-to-all-start.4 = ((bf16[8,256,256]{2,1,0:T(8,128)(2,1)}), bf16[8,256,256]{2,1,0:T(8,128)(2,1)S(1)}, u32[]{:S(2)}, u32[]{:S(2)}) async-start(bf16[8,256,256]{2,1,0:T(8,128)(2,1)} %bitcast.70), calls=%async_computation.4 | async-start | bytes 2097152 | tf_op jit(solution)/shard_map/all_to_all | solution.py:66
Sparse Core Ops, SparseCore 0:
  101.5 83.3 reduce-scatter.4
  189.0 38.3 reduce-scatter.6
where the time goes:
time: 247 us; the launch traced here: 246 us
  waiting for transfers between devices  136 us (55%)
  matrix products  47.7 us (19%)
  starting transfers between devices  29.5 us (12%)
  between operations  14.3 us (6%)
  local copies, waits for them, and re-layouts  13.9 us (6%)
  other arithmetic  4.43 us (2%)
    reduce_scatter x1, waiting for transfers between devices, sum_by_axis(): nearer = lax.psum_scatter(array, axes[0], scatter_dimension=dim, tiled=True)  83.5 us
    all_to_all x4, waiting for transfers between devices, sent_to_all(): return lax.all_to_all(copies, axis, split_axis=0, concat_axis=0, tiled=True)  31.6 us
    all_to_all x2, waiting for transfers between devices, summed_on_arrival(): pieces = lax.all_to_all(in_blocks(array, dim, size), axis, 0, 0, tiled=True)  21.2 us
    dot_general x2, matrix products, per_device(): lax.dot_general(gathered, logit_grad, (((0,), (0,)), ((), ())), preferred...  20.5 us
    all_to_all x4, starting transfers between devices, sent_to_all(): return lax.all_to_all(copies, axis, split_axis=0, concat_axis=0, tiled=True)  20 us
    dot_general x2, matrix products, micro_batch(): lax.dot_general(logit_grad, head_weight, (((1,), (1,)), ((), ())), prefer...  13.8 us
    dot_general x2, matrix products, micro_batch(): student = jnp.dot(gathered, head_weight, preferred_element_type=jnp.float32)  13.4 us
    all_to_all x2, starting transfers between devices, summed_on_arrival(): pieces = lax.all_to_all(in_blocks(array, dim, size), axis, 0, 0, tiled=True)  9.43 us
  transfers between devices with their start and end apart: 8, of which 7 were waited for; matrix products, arithmetic and copies ran while one was open for 10% of the time, Pallas kernels for 0%

commit v1 on v0

v1 whole, which is shorter than its diff:
```python
import functools

import jax
import jax.numpy as jnp
from jax import lax
from jax.experimental import pallas as pl
from jax.experimental.pallas import tpu as pltpu
from jax.sharding import Mesh
from jax.sharding import PartitionSpec as P


DP = ("y", "p", "q")
VOCAB = ("x", "c")
WHOLE_VOCAB = ("q", "x", "c")
SWAP = ((0, 1), (1, 0))
CHUNKS = (512, 512)


grad_scale = 8.0
BF = jnp.bfloat16
F32 = jnp.float32


def sent(array, axis, by):
    size = lax.axis_size(axis)
    return lax.ppermute(array, axis, [(k, (k + by) % size) for k in range(size)])


def swapped(array, axis):
    return lax.ppermute(array, axis, SWAP)


def sent_to_all(array, axis):
    copies = jnp.broadcast_to(array, (lax.axis_size(axis), *array.shape))
    return lax.all_to_all(copies, axis, 0, 0, tiled=True)


def whole(shape):
    return pl.BlockSpec(shape, lambda *_: (0,) * len(shape))


def after(array, *others):
    return lax.optimization_barrier((array, *others))[0]


def call(body, where, operands, in_specs, out_shapes, out_specs, grid=(1,), scratch=(), micros=2, vmem=20):
    operands = [
        pltpu.with_memory_space_constraint(array, pltpu.HBM) if array.size >= 2**17 else array
        for array in operands
    ]
    out_shapes = jax.tree.map(
        lambda s: pltpu.HBM(s.shape, s.dtype) if s.size >= 2**17 else s, out_shapes
    )
    cost = pl.CostEstimate(flops=int(micros * 4.5e8), bytes_accessed=2**20, transcendentals=0)
    return pl.pallas_call(
        body,
        cost_estimate=cost,
        out_shape=out_shapes,
        grid_spec=pltpu.PrefetchScalarGridSpec(
            num_scalar_prefetch=1,
            grid=grid,
            in_specs=in_specs,
            out_specs=out_specs,
            scratch_shapes=scratch,
        ),
        compiler_params=pltpu.CompilerParams(vmem_limit_bytes=vmem * 2**20),
    )(where, *operands)


def as_row(column):
    return jnp.transpose(jnp.broadcast_to(column, (column.shape[0], 128)))[0:1]


def lane_sums(value):
    lanes = value[:, 0:128]
    for k in range(128, value.shape[1], 128):
        lanes = lanes + value[:, k : k + 128]
    return jnp.sum(lanes, axis=1, keepdims=True)


def totals(stats, value, row_block=128):
    rows, columns = value.shape
    found = ([], [])
    for at in range(0, rows, row_block):
        part = value[at : at + row_block, :].astype(F32)
        lanes = part[:, 0:128]
        for k in range(128, columns, 128):
            lanes = jnp.maximum(lanes, part[:, k : k + 128])
        peak = jnp.max(lanes, axis=1, keepdims=True)
        found[0].append(peak)
        found[1].append(lane_sums(jnp.exp(part - peak)))
    for k, part in enumerate(found):
        stats[k : k + 1, :] = as_row(jnp.concatenate(part, axis=0))


def join_body(where, *refs):
    rows = refs[0].shape[0]
    for k, ref in enumerate(refs[:-1]):
        refs[-1][k * rows : (k + 1) * rows, :] = ref[...]


def student_body(block, where, mine, other, *refs):
    weights, (total, stats) = refs[:4], refs[4:]
    c = where[4]
    width = mine.shape[1]
    rows = mine.shape[0] // 4
    step = pl.program_id(0)
    value = None
    for k in range(4):
        for side, slices in enumerate((mine, other)):
            at = pl.multiple_of((c if side == 0 else 1 - c) * width, width)
            got = jnp.dot(
                slices[k * rows : (k + 1) * rows, :],
                weights[k][pl.ds(at, width), :],
                preferred_element_type=F32,
            )
            value = got if value is None else value + got
    total[:, pl.ds(pl.multiple_of(step * block, block), block)] = value

    @pl.when(step == pl.num_programs(0) - 1)
    def _():
        totals(stats, total)


def student_part(where, pair, weight, block=256):
    rows = pair[0].shape[0] // 4
    columns = weight.shape[1] // 2
    width = pair[0].shape[1]
    steps = columns // block
    in_specs = [whole(pair[0].shape)] * 2
    for by in range(4):
        in_specs.append(
            pl.BlockSpec(
                (2 * width, block),
                lambda j, at, by=by: (lax.rem(at[3] + by, 4), at[2] * steps + j),
            )
        )
    return call(
        functools.partial(student_body, block),
        where,
        [*pair, *[weight] * 4],
        in_specs,
        [jax.ShapeDtypeStruct((rows, columns), F32), jax.ShapeDtypeStruct((2, rows), F32)],
        [whole((rows, columns)), whole((2, rows))],
        (steps,),
        micros=8,
        vmem=28,
    )


def teacher_body(where, teacher, stats):
    totals(stats, teacher)


def arrange_body(where, *refs):
    pairs, outs = refs[:-4], refs[-4:]
    y, x, c = where[0], where[3], where[4]
    width = pairs[0].shape[1]
    rows = outs[0].shape[0] // 2
    for r in range(4):
        d = lax.rem(x + r - y + 4, 4)
        for side in range(4):

            @pl.when(d == side)
            def _(r=r, side=side):
                for group in range(2):
                    mine = pairs[2 * group][r * rows : (r + 1) * rows, :]
                    other = pairs[2 * group + 1][r * rows : (r + 1) * rows, :]
                    to = slice(group * rows, (group + 1) * rows)
                    outs[side][to, 0:width] = jnp.where(c == 0, mine, other)
                    outs[side][to, width : 2 * width] = jnp.where(c == 0, other, mine)


def merged(parts):
    top = jnp.max(parts[0][:, 0], axis=0, keepdims=True)
    for part in parts[1:]:
        top = jnp.maximum(top, jnp.max(part[:, 0], axis=0, keepdims=True))
    total = sum(
        jnp.sum(part[:, 1] * jnp.exp(part[:, 0] - top), axis=0, keepdims=True) for part in parts
    )
    return top, total


def grad_body(first, where, s_own, s_other, t_own, t_other, every_s, every_t, out, *refs):
    if first:
        scales = refs
    else:
        tops, cross, *scales = refs
    q = where[2]
    step = pl.program_id(0)
    steps = pl.num_programs(0)
    block = s_own.shape[0]
    rows = every_t.shape[2]
    half = every_s.shape[0] // 2

    @pl.when(step == 0)
    def _():
        for group in range(2):
            at = slice(group * rows, (group + 1) * rows)
            to = slice((1 - group) * rows, (2 - group) * rows)
            mine = every_s[pl.ds(q * half, half), :, at]
            other = every_s[pl.ds((1 - q) * half, half), :, to]
            s_top, s_total = merged((mine, other))
            source = q if group == 0 else 1 - q
            t_top, t_total = merged((every_t[pl.ds(source * half, half), :, :],))
            if group == 0 and not first:
                for k, row in enumerate((s_top, s_total, t_top, t_total)):
                    tops[k : k + 1, :] = row
            wanted = (s_top, grad_scale / s_total, t_top, grad_scale / t_total)
            for row, scale in zip(wanted, scales):
                scale[at, :] = jnp.transpose(jnp.broadcast_to(row, (128, rows)))

    def rows_of(student, teacher):
        at = pl.ds(pl.multiple_of(step * block, block), block)
        s_top, s_scale, t_top, t_scale = (scale[at, :] for scale in scales)
        begin = student.shape[1] - out.shape[1]
        lanes = None
        for k in range(0, student.shape[1], 128):
            s = student[:, k : k + 128]
            t = teacher[:, k : k + 128].astype(F32)
            t_term = jnp.exp(t - t_top)
            if k >= begin:
                out[:, k - begin : k - begin + 128] = (
                    jnp.exp(s - s_top) * s_scale - t_term * t_scale
                ).astype(BF)
            if not first:
                term = t_term * (t - s)
                lanes = term if lanes is None else lanes + term
        if not first:
            cross[0:1, at] = as_row(jnp.sum(lanes, axis=1, keepdims=True))

    @pl.when(step < steps // 2)
    def _():
        rows_of(s_own, t_own)

    @pl.when(step >= steps // 2)
    def _():
        rows_of(s_other, t_other)


def grad_part(where, values, every_s, every_t, count, first, block=256):
    rows, half = values[0].shape
    steps = 2 * rows // block
    read = count if first else half
    early = pl.BlockSpec((block, read), lambda j, at: (jnp.minimum(j, steps // 2 - 1), 0))
    late = pl.BlockSpec((block, read), lambda j, at: (jnp.maximum(j - steps // 2, 0), 0))
    shapes = [jax.ShapeDtypeStruct((2 * rows, count), BF)]
    specs = [pl.BlockSpec((block, count), lambda j, at: (j, 0))]
    if not first:
        more = ((4, rows), (1, 2 * rows))
        shapes += [jax.ShapeDtypeStruct(shape, F32) for shape in more]
        specs += [whole(shape) for shape in more]
    return call(
        functools.partial(grad_body, first),
        where,
        [*values, every_s, every_t],
        [early, late, early, late, whole(every_s.shape), whole(every_t.shape)],
        shapes,
        specs,
        (steps,),
        [pltpu.VMEM((2 * rows, 128), F32)] * 4,
        micros=4,
    )


def hidden_body(with_arrived, where, first, last, weight, *refs):
    split = first.shape[1]
    value = None
    for grad, columns in ((first, slice(0, split)), (last, slice(split, None))):
        part = lax.dot_general(
            grad[...], weight[:, columns], (((1,), (1,)), ((), ())), preferred_element_type=F32
        )
        value = part if value is None else value + part
    if with_arrived:
        value = value + refs[0][0].astype(F32)
    refs[-1][0] = value.astype(BF)


def hidden_part(where, grads, weight, this_core, arrived=None):
    tokens = grads[0].shape[0]
    half = weight.shape[1] // 2
    width = 256

    def block_of(j, at):
        core = at[4] if this_core else 1 - at[4]
        return (2 * lax.rem(at[3] + j, 4) + core, at[2])

    tile = pl.BlockSpec((1, tokens, width), lambda j, at: (j, 0, 0))
    operands = [*grads, weight]
    in_specs = [*(whole(grad.shape) for grad in grads), pl.BlockSpec((width, half), block_of)]
    if arrived is not None:
        operands.append(arrived)
        in_specs.append(tile)
    return call(
        functools.partial(hidden_body, arrived is not None),
        where,
        operands,
        in_specs,
        jax.ShapeDtypeStruct((4, tokens, width), BF),
        tile,
        (4,),
        micros=6,
    )


def final_body(where, *refs):
    out = refs[-1]
    half = out.shape[1] // 2
    begin = 0
    for piece in refs[:-1]:
        chunk = piece.shape[2]
        for side in (0, 1):
            at = side * half + begin
            out[:, at : at + chunk] = sum(piece[2 * p + side].astype(F32) for p in range(4))
        begin += chunk


def per_device(hidden_states, teacher_logits, head_weight):
    rows, width = hidden_states.shape
    _, columns = head_weight.shape
    half = columns // 2
    where = jnp.stack([lax.axis_index(name) for name in (*DP, *VOCAB)]).astype(jnp.int32)
    q = lax.axis_index("q")

    other_hidden = swapped(hidden_states, "q")
    (teacher_stats,) = call(
        teacher_body,
        where,
        [teacher_logits],
        [whole(teacher_logits.shape)],
        [jax.ShapeDtypeStruct((2, rows), F32)],
        [whole((2, rows))],
        micros=5,
    )
    every_teacher = sent_to_all(teacher_stats, WHOLE_VOCAB)
    pairs = []
    for piece in (hidden_states, other_hidden):
        moved = [sent(piece, "x", by) for by in (-1, 2, 1)]
        mine = call(
            join_body,
            where,
            [piece, *moved],
            [whole(piece.shape)] * 4,
            jax.ShapeDtypeStruct((4 * rows, width), BF),
            whole((4 * rows, width)),
            micros=1,
        )
        pairs.append((mine, swapped(mine, "c")))
    kept_teacher = lax.dynamic_slice_in_dim(teacher_logits, q * half, half, 1)
    later = after(teacher_logits, other_hidden)
    sent_teacher = lax.dynamic_slice_in_dim(later, (1 - q) * half, half, 1)
    arrived_teacher = swapped(sent_teacher, "q")

    student_own, stats_own = student_part(where, pairs[0], head_weight)
    student_other, stats_other = student_part(where, pairs[1], head_weight)
    every_student = sent_to_all(jnp.concatenate([stats_own, stats_other], axis=1), WHOLE_VOCAB)
    flat = [array for pair in pairs for array in pair]
    blocks = call(
        arrange_body,
        where,
        flat,
        [whole(array.shape) for array in flat],
        [jax.ShapeDtypeStruct((2 * rows, 2 * width), BF)] * 4,
        [whole((2 * rows, 2 * width))] * 4,
        micros=5,
    )
    values = (student_own, student_other, kept_teacher, arrived_teacher)
    (grad_first,) = grad_part(where, values, every_student, every_teacher, CHUNKS[0], True)

    pieces = []
    begin = -CHUNKS[0]
    grads = grad_first
    gate = None
    for k, chunk in enumerate(CHUNKS):
        if k:
            grads = after(grad_last, gate)[:, begin : begin + chunk]
        begin += chunk
        parts = []
        for d in (2, 1, 3):
            part = lax.dot_general(
                blocks[d], grads, (((0,), (0,)), ((), ())), preferred_element_type=F32
            ).astype(BF)
            parts.append(sent(part, "y", d))
        if k == 0:
            later = tuple(after(value, part) for value in values)
            grad_last, tops, cross = grad_part(
                where, later, every_student, every_teacher, half - CHUNKS[0], False
            )
            crosses = sent_to_all(cross, WHOLE_VOCAB)
            across_core = hidden_part(where, (grad_first, grad_last), head_weight, False)
            across_core = swapped(across_core, "c")
            gate = grad_last
        else:
            gate = part
        own = lax.dot_general(
            blocks[0], grads, (((0,), (0,)), ((), ())), preferred_element_type=F32
        )
        total = own + sum(part.astype(F32) for part in parts)
        total = total.astype(BF).reshape(8, -1, chunk)
        pieces.append(lax.all_to_all(total, ("p", "q"), 0, 0, tiled=True))
        if k == 0:
            value = hidden_part(
                where, (grad_first, after(grad_last, total)), head_weight, True, across_core
            )
    head_grad = call(
        final_body,
        where,
        pieces,
        [whole(piece.shape) for piece in pieces],
        jax.ShapeDtypeStruct((pieces[0].shape[1], columns), F32),
        whole((pieces[0].shape[1], columns)),
    )
    moved = [sent(value[d], "x", d) for d in (2, 1, 3)]
    value = value[0].astype(F32) + sum(part.astype(F32) for part in moved)
    partner = swapped(value[rows:].astype(BF), "q")
    hidden_grad = (value[:rows] + partner.astype(F32)).astype(BF)

    crosses = jnp.sum(crosses[:, 0].reshape(2, -1, 2, rows), axis=1)
    cross_term = jnp.where(q == 0, crosses[0, 0] + crosses[1, 1], crosses[1, 0] + crosses[0, 1])
    student_max, student_total, teacher_max, teacher_total = tops
    divergence = (
        cross_term / teacher_total
        - teacher_max
        - jnp.log(teacher_total)
        + student_max
        + jnp.log(student_total)
    )
    return divergence, hidden_grad, head_grad


def solution(mesh):
    split = Mesh(mesh.devices.reshape(4, 4, 2, 4, 2), (*DP, *VOCAB))
    placed = (P(DP, VOCAB), P(DP, VOCAB), P(None, VOCAB))

    return jax.shard_map(
        per_device,
        mesh=split,
        in_specs=placed,
        out_specs=(P(DP), P(DP, VOCAB), P(DP, VOCAB)),
        check_vma=False,
    )
```

time: 247 us -> 205 us (0.83)
  waiting for transfers between devices: 136 us -> 55.3 us
  Pallas kernels: 0 us -> 59.2 us
  matrix products: 47.7 us -> 14.5 us
  starting transfers between devices: 29.5 us -> 59.3 us
  between operations: 14.3 us -> 0.79 us
  local copies, waits for them, and re-layouts: 13.9 us -> 11.4 us
    reduce_scatter x1 -> x0, waiting for transfers between devices: 83.5 us -> none  [sum_by_axis(): nearer = lax.psum_scatter(array, axes[0], scatter_dimension=dim, tiled=True)]
    pallas_call x0 -> x11, Pallas kernels: none -> 59.2 us  [call(): pl.pallas_call(body, cost_estimate=cost, out_shape=out_shapes, grid_spec=...]
    ppermute x0 -> x21, waiting for transfers between devices: none -> 52.7 us  [the longest x15 50.9 us: sent(): lax.ppermute(array, axis, [(k, (k + by) % size) for k in range(size)])]
    all_to_all x6 -> x5, waiting for transfers between devices: 52.9 us -> 2.55 us  [the longest x3 2.54 us: sent_to_all(): return lax.all_to_all(copies, axis, 0, 0, tiled=True)]
    dot_general x6 -> x8, matrix products: 47.7 us -> 14.5 us  [the longest x6 8.14 us: per_device(): lax.dot_general(blocks[d], grads, (((0,), (0,)), ((), ())), preferred_ele...]
    ppermute x0 -> x21, starting transfers between devices: none -> 28.6 us  [the longest x15 20.9 us: sent(): lax.ppermute(array, axis, [(k, (k + by) % size) for k in range(size)])]
    unnamed x21 -> x36, local copies, waits for them, and re-layouts: 6.21 us -> 4.81 us
    all_to_all x6 -> x5, starting transfers between devices: 29.4 us -> 30.8 us  [the longest x3 16.2 us: sent_to_all(): return lax.all_to_all(copies, axis, 0, 0, tiled=True)]
  transfers between devices with their start and end apart: 8 -> 26, of which waited for: 7 -> 12; matrix products, arithmetic and copies ran while one was open for 10% -> 11% of each run, Pallas kernels for 0% -> 20%
where the time goes in v1:
time: 205 us; the launch traced here: 204 us
  starting transfers between devices  59.3 us (29%)
  Pallas kernels  59.2 us (29%)
  waiting for transfers between devices  55.3 us (27%)
  matrix products  14.5 us (7%)
  local copies, waits for them, and re-layouts  11.4 us (6%)
  other arithmetic  3 us (1%)
    pallas_call x11, Pallas kernels, call(): pl.pallas_call(body, cost_estimate=cost, out_shape=out_shapes, grid_spec=...  59.2 us
    ppermute x15, waiting for transfers between devices, sent(): lax.ppermute(array, axis, [(k, (k + by) % size) for k in range(size)])  50.9 us
    ppermute x15, starting transfers between devices, sent(): lax.ppermute(array, axis, [(k, (k + by) % size) for k in range(size)])  20.9 us
    all_to_all x3, starting transfers between devices, sent_to_all(): return lax.all_to_all(copies, axis, 0, 0, tiled=True)  16.2 us
    all_to_all x2, starting transfers between devices, per_device(): pieces.append(lax.all_to_all(total, ('p', 'q'), 0, 0, tiled=True))  14.6 us
    dot_general x6, matrix products, per_device(): lax.dot_general(blocks[d], grads, (((0,), (0,)), ((), ())), preferred_ele...  8.14 us
    ppermute x6, starting transfers between devices, swapped(): return lax.ppermute(array, axis, SWAP)  7.66 us
    dot_general x2, matrix products, per_device(): lax.dot_general(blocks[0], grads, (((0,), (0,)), ((), ())), preferred_ele...  6.4 us
  transfers between devices with their start and end apart: 26, of which 12 were waited for; matrix products, arithmetic and copies ran while one was open for 11% of the time, Pallas kernels for 20%

profile of v1, /device:TPU:1, one launch (start us, length us, event | category | flops | bytes accessed | tf_op | source)
XLA Modules:
  0.0 203.6 jit_solution(1442111615197545929)
XLA Ops:
  0.6 2.1 %collective-permute-start.2 = (bf16[512,256]{1,0:T(8,128)(2,1)}, bf16[512,256]{1,0:T(8,128)(2,1)S(1)}, u32[]{:S(2)}, u32[]{:S(2)}) collective-permute-start(bf16[512,256]{1,0:T(8,128)(2,1)} %refs_0_.3), channel_id=1, source_target_pairs={{0,2},{2,4},{4,6},{6,0},{1,3},{3,5},{5,7},{7,1},{8,10},{10,12},{12... | collective-permute-start | bytes 786440 | tf_op jit(solution)/shard_map/ppermute | solution.py:26
  2.7 2.5 %collective-permute-start.1 = (bf16[512,256]{1,0:T(8,128)(2,1)}, bf16[512,256]{1,0:T(8,128)(2,1)S(1)}, u32[]{:S(2)}, u32[]{:S(2)}) collective-permute-start(bf16[512,256]{1,0:T(8,128)(2,1)} %refs_0_.3), channel_id=1, source_target_pairs={{0,4},{2,6},{4,0},{6,2},{1,5},{3,7},{5,1},{7,3},{8,12},{10,14},{12... | collective-permute-start | bytes 786440 | tf_op jit(solution)/shard_map/ppermute | solution.py:26
  5.2 1.2 collective-permute-start
  6.3 1.6 collective-permute-start.4
  8.1 8.7 %collective-permute-done.1.refs_2_ = bf16[512,256]{1,0:T(8,128)(2,1)S(1)} collective-permute-done((bf16[512,256]{1,0:T(8,128)(2,1)}, bf16[512,256]{1,0:T(8,128)(2,1)S(1)}, u32[]{:S(2)}, u32[]{:S(2)}) %collective-permute-start.1) | collective-permute-done | bytes 262176 | tf_op jit(solution)/shard_map/ppermute | solution.py:26
  18.1 2.8 %shard_map.58.mine.refs_0_ = bf16[2048,256]{1,0:T(8,128)(2,1)} custom-call(s32[5]{0:T(128)S(1)} %stack.23.where, bf16[512,256]{1,0:T(8,128)(2,1)} %refs_0_.3, bf16[512,256]{1,0:T(8,128)(2,1)} %copy-done.9, bf16[512,256]{1,0:T(8,128)(2,1)} %copy-done.8, bf16[512,256]{1,0:T(8,128)(2,1)} %copy-done.7), custom_call_target="tpu_custom_call" | custom-call | flops 450000000 | bytes 1048576 | tf_op jit(solution)/shard_map/pallas_call | solution.py:55
  20.9 1.5 collective-permute-start.3
  22.7 2.1 %collective-permute-start.6 = (bf16[512,256]{1,0:T(8,128)(2,1)S(1)}, bf16[512,256]{1,0:T(8,128)(2,1)S(1)}, u32[]{:S(2)}, u32[]{:S(2)}) collective-permute-start(bf16[512,256]{1,0:T(8,128)(2,1)S(1)} %collective-permute-done.4.refs_0_), channel_id=1, source_target_pairs={{0,4},{2,6},{4,0},{6,2},{1,5},{3,7},{5,1},{7,3},{8,12},{10,14},{12... | collective-permute-start | bytes 786440 | tf_op jit(solution)/shard_map/ppermute | solution.py:26
  24.8 1.4 collective-permute-start.5
  26.2 5.5 %collective-permute-done.7.refs_3_ = bf16[512,256]{1,0:T(8,128)(2,1)S(1)} collective-permute-done((bf16[512,256]{1,0:T(8,128)(2,1)S(1)}, bf16[512,256]{1,0:T(8,128)(2,1)S(1)}, u32[]{:S(2)}, u32[]{:S(2)}) %collective-permute-start.7) | collective-permute-done | bytes 262176 | tf_op jit(solution)/shard_map/ppermute | solution.py:26
  31.7 5.1 %collective-permute-done.6.refs_2_ = bf16[512,256]{1,0:T(8,128)(2,1)S(1)} collective-permute-done((bf16[512,256]{1,0:T(8,128)(2,1)S(1)}, bf16[512,256]{1,0:T(8,128)(2,1)S(1)}, u32[]{:S(2)}, u32[]{:S(2)}) %collective-permute-start.6) | collective-permute-done | bytes 262176 | tf_op jit(solution)/shard_map/ppermute | solution.py:26
  38.2 2.8 %shard_map.60.refs_2_.mine = bf16[2048,256]{1,0:T(8,128)(2,1)} custom-call(s32[5]{0:T(128)S(1)} %stack.23.where, bf16[512,256]{1,0:T(8,128)(2,1)} %copy-done.6, bf16[512,256]{1,0:T(8,128)(2,1)} %copy-done.12, bf16[512,256]{1,0:T(8,128)(2,1)} %copy-done.11, bf16[512,256]{1,0:T(8,128)(2,1)} %copy-done.10), custom_call_target="tpu_custom_call" | custom-call | flops 450000000 | bytes 1048576 | tf_op jit(solution)/shard_map/pallas_call | solution.py:55
  41.0 1.3 collective-permute-start.8
  42.3 3.4 %shard_map.63 = f32[2,512]{1,0:T(2,128)S(1)} custom-call(s32[5]{0:T(128)S(1)} %stack.23.where, bf16[512,2048]{1,0:T(8,128)(2,1)} %teacher.1), custom_call_target="tpu_custom_call" | custom-call | flops 2249999872 | bytes 1048576 | tf_op jit(solution)/shard_map/pallas_call | solution.py:55
  46.3 5.2 %all-to-all-start.1 = ((f32[16,2,512]{2,1,0:T(2,128)}), f32[16,2,512]{2,1,0:T(2,128)S(1)}, u32[]{:S(2)}, u32[]{:S(2)}) async-start(f32[16,2,512]{2,1,0:T(2,128)} %broadcast_in_dim.10), calls=%async_computation.1 | async-start | bytes 131072 | tf_op jit(solution)/shard_map/all_to_all | solution.py:35
  52.7 1.4 collective-permute-start.9
  55.0 8.2 %shard_map.59 = (f32[512,1024]{1,0:T(8,128)}, f32[2,512]{1,0:T(2,128)S(1)}) custom-call(s32[5]{0:T(128)S(1)} %stack.23.where, bf16[2048,256]{1,0:T(8,128)(2,1)} %shard_map.58.mine.refs_0_, bf16[2048,256]{1,0:T(8,128)(2,1)} %copy-done.3, bf16[2048,2048]{1,0:T(8,128)(2,1)} %weight.3, bf16[2048,2048]{1,0:T(8,128)(2,1)} %weight.3, bf16[2048,2048]{1,0:T(8,128)(2,1)} %weight.3, ...), custom_call_target="tpu_custom_call" | custom-call | flops 3600000000 | bytes 1048576 | tf_op jit(solution)/shard_map/pallas_call | solution.py:55
  63.2 8.2 %shard_map.62 = (f32[512,1024]{1,0:T(8,128)}, f32[2,512]{1,0:T(2,128)S(1)}) custom-call(s32[5]{0:T(128)S(1)} %stack.23.where, bf16[2048,256]{1,0:T(8,128)(2,1)} %shard_map.60.refs_2_.mine, bf16[2048,256]{1,0:T(8,128)(2,1)} %collective-permute-done.8.refs_3_.other, bf16[2048,2048]{1,0:T(8,128)(2,1)} %weight.3, bf16[2048,2048]{1,0:T(8,128)(2,1)} %weight.3, ...), custom_call_target="tpu_custom_call" | custom-call | flops 3600000000 | bytes 1048576 | tf_op jit(solution)/shard_map/pallas_call | solution.py:55
  72.1 4.9 %all-to-all-start = ((f32[16,2,1024]{2,1,0:T(2,128)}), f32[16,2,1024]{2,1,0:T(2,128)S(1)}, u32[]{:S(2)}, u32[]{:S(2)}) async-start(f32[16,2,1024]{2,1,0:T(2,128)} %broadcast_in_dim.9), calls=%async_computation | async-start | bytes 262144 | tf_op jit(solution)/shard_map/all_to_all | solution.py:35
  78.0 5.3 %shard_map.61 = (bf16[1024,512]{1,0:T(8,128)(2,1)}, bf16[1024,512]{1,0:T(8,128)(2,1)}, bf16[1024,512]{1,0:T(8,128)(2,1)}, bf16[1024,512]{1,0:T(8,128)(2,1)}) custom-call(s32[5]{0:T(128)S(1)} %stack.23.where, bf16[2048,256]{1,0:T(8,128)(2,1)} %shard_map.58.mine.refs_0_, bf16[2048,256]{1,0:T(8,128)(2,1)} %copy-done.3, ...), custom_call_target="tpu_custom_call" | custom-call | flops 2249999872 | bytes 1048576 | tf_op jit(solution)/shard_map/pallas_call | solution.py:55
  83.4 5.5 %shard_map.64.first = bf16[1024,512]{1,0:T(8,128)(2,1)} custom-call(s32[5]{0:T(128)S(1)} %stack.23.where, f32[512,1024]{1,0:T(8,128)} %get-tuple-element.27.s_own, f32[512,1024]{1,0:T(8,128)} %get-tuple-element.28.s_other, bf16[512,1024]{1,0:T(8,128)(2,1)} %constant_dynamic-slice_fusion.1.t_own, bf16[512,1024]{1,0:T(8,128)(2,1)} %collective-permute-done.9.t_other, ...), custom_call_target="tpu_custom_call" | custom-call | flops 1800000000 | bytes 1048576 | tf_op jit(solution)/shard_map/pallas_call | solution.py:55
  89.0 2.0 convolution_convert_fusion.5
  90.9 6.7 %shard_map.65 = (bf16[1024,512]{1,0:T(8,128)(2,1)}, f32[4,512]{1,0:T(4,128)S(1)}, f32[1,1024]{1,0:T(1,128)S(1)}) custom-call(s32[5]{0:T(128)S(1)} %stack.23.where, f32[512,1024]{1,0:T(8,128)} %get-tuple-element.27.s_own, f32[512,1024]{1,0:T(8,128)} %get-tuple-element.28.s_other, bf16[512,1024]{1,0:T(8,128)(2,1)} %constant_dynamic-slice_fusion.1.t_own, ...), custom_call_target="tpu_custom_call" | custom-call | flops 1800000000 | bytes 1048576 | tf_op jit(solution)/shard_map/pallas_call | solution.py:55
  97.7 6.7 %shard_map.66 = bf16[4,1024,256]{2,1,0:T(8,128)(2,1)} custom-call(s32[5]{0:T(128)S(1)} %stack.23.where, bf16[1024,512]{1,0:T(8,128)(2,1)} %shard_map.64.first, bf16[1024,512]{1,0:T(8,128)(2,1)} %get-tuple-element.38.last, bf16[2048,2048]{1,0:T(8,128)(2,1)} %weight.3), custom_call_target="tpu_custom_call" | custom-call | flops 2700000000 | bytes 1048576 | tf_op jit(solution)/shard_map/pallas_call | solution.py:55
  105.5 3.0 %collective-permute-start.18 = (bf16[512,512]{1,0:T(8,128)(2,1)S(1)}, bf16[512,512]{1,0:T(8,128)(2,1)S(1)}, u32[]{:S(2)}, u32[]{:S(2)}) collective-permute-start(bf16[512,512]{1,0:T(8,128)(2,1)S(1)} %convolution_convert_fusion.2), channel_id=1, source_target_pairs={{0,128},{64,192},{128,0},{192,64},{1,129},{65,193},{129,1},{193,65... | collective-permute-start | bytes 1572872 | tf_op jit(solution)/shard_map/ppermute | solution.py:26
  109.7 1.6 convolution_convert_fusion
  111.3 2.3 %collective-permute-start.20 = (bf16[512,512]{1,0:T(8,128)(2,1)}, bf16[512,512]{1,0:T(8,128)(2,1)}, u32[]{:S(2)}, u32[]{:S(2)}) collective-permute-start(bf16[512,512]{1,0:T(8,128)(2,1)} %convolution_convert_fusion), channel_id=1, source_target_pairs={{0,192},{64,0},{128,64},{192,128},{1,193},{65,1},{129,65},{193,129... | collective-permute-start | bytes 1572872 | tf_op jit(solution)/shard_map/ppermute | solution.py:26
  113.6 1.6 convolution_convert_fusion.4
  115.2 1.5 convolution_convert_fusion.3
  116.7 3.8 %collective-permute-done.18 = bf16[512,512]{1,0:T(8,128)(2,1)S(1)} collective-permute-done((bf16[512,512]{1,0:T(8,128)(2,1)S(1)}, bf16[512,512]{1,0:T(8,128)(2,1)S(1)}, u32[]{:S(2)}, u32[]{:S(2)}) %collective-permute-start.18) | collective-permute-done | bytes 524320 | tf_op jit(solution)/shard_map/ppermute | solution.py:26
  120.5 1.3 collective-permute-start.11
  121.8 10.8 %collective-permute-done.19 = bf16[512,512]{1,0:T(8,128)(2,1)S(1)} collective-permute-done((bf16[512,512]{1,0:T(8,128)(2,1)S(1)}, bf16[512,512]{1,0:T(8,128)(2,1)S(1)}, u32[]{:S(2)}, u32[]{:S(2)}) %collective-permute-start.19) | collective-permute-done | bytes 524320 | tf_op jit(solution)/shard_map/ppermute | solution.py:26
  134.1 6.0 %all-to-all-start.2 = ((f32[16,1,1024]{2,1,0:T(1,128)}), f32[16,1,1024]{2,1,0:T(1,128)S(1)}, u32[]{:S(2)}, u32[]{:S(2)}) async-start(f32[16,1,1024]{2,1,0:T(1,128)} %broadcast_in_dim.11), calls=%async_computation.2 | async-start | bytes 131072 | tf_op jit(solution)/shard_map/all_to_all | solution.py:35
  140.1 3.3 %fusion.1 = bf16[512,512]{1,0:T(8,128)(2,1)} fusion(bf16[1024,512]{1,0:T(8,128)(2,1)} %get-tuple-element.34, bf16[1024,512]{1,0:T(8,128)(2,1)S(1)} %copy-done.1, bf16[512,512]{1,0:T(8,128)(2,1)} %collective-permute-done.20, bf16[512,512]{1,0:T(8,128)(2,1)} %copy-done.14, bf16[512,512]{1,0:T(8,128)(2,1)} %copy-done.13), kind=kOutput, calls=%fused_computation.3 | convolution fusion | flops 538705920 | bytes 4194304 | tf_op jit(solution)/shard_map/dot_general | solution.py:395
  143.4 2.5 %all-to-all-done.2 = f32[16,1,1024]{2,1,0:T(1,128)S(1)} async-done(((f32[16,1,1024]{2,1,0:T(1,128)}), f32[16,1,1024]{2,1,0:T(1,128)S(1)}, u32[]{:S(2)}, u32[]{:S(2)}) %all-to-all-start.2) | async-done | bytes 65568 | tf_op jit(solution)/shard_map/all_to_all | solution.py:35
  145.9 7.3 %all-to-all-start.4 = ((bf16[8,64,512]{2,1,0:T(8,128)(2,1)}), bf16[8,64,512]{2,1,0:T(8,128)(2,1)S(1)}, u32[]{:S(2)}, u32[]{:S(2)}) async-start(bf16[8,64,512]{2,1,0:T(8,128)(2,1)} %bitcast.16), calls=%async_computation.4 | async-start | bytes 1048576 | tf_op jit(solution)/shard_map/all_to_all | solution.py:400
  153.2 1.5 collective-permute-done.11
  154.8 3.1 %fusion = bf16[512,512]{1,0:T(8,128)(2,1)} fusion(bf16[1024,512]{1,0:T(8,128)(2,1)} %get-tuple-element.34, bf16[1024,512]{1,0:T(8,128)(2,1)S(1)} %copy-done, bf16[512,512]{1,0:T(8,128)(2,1)} %collective-permute-done.12, bf16[512,512]{1,0:T(8,128)(2,1)} %collective-permute-done.11, bf16[512,512]{1,0:T(8,128)(2,1)S(1)} %collective-permute-done.10), kind=kOutput, calls=%fused_computation.2 | convolution fusion | flops 538705920 | bytes 4194304 | tf_op jit(solution)/shard_map/dot_general | solution.py:395
  157.9 7.0 %shard_map.67 = bf16[4,1024,256]{2,1,0:T(8,128)(2,1)} custom-call(s32[5]{0:T(128)S(1)} %stack.23.where, bf16[1024,512]{1,0:T(8,128)(2,1)} %shard_map.64.first, bf16[1024,512]{1,0:T(8,128)(2,1)} %get-tuple-element.38.last, bf16[2048,2048]{1,0:T(8,128)(2,1)} %weight.3, bf16[4,1024,256]{2,1,0:T(8,128)(2,1)} %collective-permute-done.13.refs_0_), custom_call_target="tpu_custom_call" | custom-call | flops 2700000000 | bytes 1048576 | tf_op jit(solution)/shard_map/pallas_call | solution.py:55
  164.9 2.3 %slice_bitcast_fusion.2 = (bf16[1024,256]{1,0:T(8,128)(2,1)}, bf16[1024,256]{1,0:T(8,128)(2,1)S(1)}, bf16[1024,256]{1,0:T(8,128)(2,1)S(1)}) fusion(bf16[4,1024,256]{2,1,0:T(8,128)(2,1)} %shard_map.67), kind=kLoop, calls=%fused_computation.16 | loop fusion | bytes 3145728 | tf_op jit(solution)/shard_map/squeeze | solution.py:413
  167.1 2.9 %collective-permute-start.14 = (bf16[1024,256]{1,0:T(8,128)(2,1)}, bf16[1024,256]{1,0:T(8,128)(2,1)S(1)}, u32[]{:S(2)}, u32[]{:S(2)}) collective-permute-start(bf16[1024,256]{1,0:T(8,128)(2,1)} %get-tuple-element.39), channel_id=1, source_target_pairs={{0,4},{2,6},{4,0},{6,2},{1,5},{3,7},{5,1},{7,3},{8,12},{10,14},{12... | collective-permute-start | bytes 1572872 | tf_op jit(solution)/shard_map/ppermute | solution.py:26
  171.5 7.3 %all-to-all-start.3 = ((bf16[8,64,512]{2,1,0:T(8,128)(2,1)}), bf16[8,64,512]{2,1,0:T(8,128)(2,1)S(1)}, u32[]{:S(2)}, u32[]{:S(2)}) async-start(bf16[8,64,512]{2,1,0:T(8,128)(2,1)} %bitcast.11), calls=%async_computation.3 | async-start | bytes 1048576 | tf_op jit(solution)/shard_map/all_to_all | solution.py:400
  179.1 2.4 %collective-permute-done.14 = bf16[1024,256]{1,0:T(8,128)(2,1)S(1)} collective-permute-done((bf16[1024,256]{1,0:T(8,128)(2,1)}, bf16[1024,256]{1,0:T(8,128)(2,1)S(1)}, u32[]{:S(2)}, u32[]{:S(2)}) %collective-permute-start.14) | collective-permute-done | bytes 524320 | tf_op jit(solution)/shard_map/ppermute | solution.py:26
  181.5 11.6 %collective-permute-done.16 = bf16[1024,256]{1,0:T(8,128)(2,1)S(1)} collective-permute-done((bf16[1024,256]{1,0:T(8,128)(2,1)S(1)}, bf16[1024,256]{1,0:T(8,128)(2,1)S(1)}, u32[]{:S(2)}, u32[]{:S(2)}) %collective-permute-start.16) | collective-permute-done | bytes 524320 | tf_op jit(solution)/shard_map/ppermute | solution.py:26
  194.0 1.4 convert_add_fusion
  195.5 1.5 collective-permute-start.17
  198.4 2.7 %shard_map.68 = f32[64,2048]{1,0:T(8,128)} custom-call(s32[5]{0:T(128)S(1)} %stack.23.where, bf16[8,64,512]{2,1,0:T(8,128)(2,1)} %copy-done.5, bf16[8,64,512]{2,1,0:T(8,128)(2,1)} %copy-done.4), custom_call_target="tpu_custom_call" | custom-call | flops 900000000 | bytes 1048576 | tf_op jit(solution)/shard_map/pallas_call | solution.py:55
  201.0 1.8 collective-permute-done.17
  (76 shorter events, 16.3 us)
Async XLA Ops:
  0.6 7.4 %collective-permute-start.2 = (bf16[512,256]{1,0:T(8,128)(2,1)}, bf16[512,256]{1,0:T(8,128)(2,1)S(1)}, u32[]{:S(2)}, u32[]{:S(2)}) collective-permute-start(bf16[512,256]{1,0:T(8,128)(2,1)} %refs_0_.3), channel_id=1, source_target_pairs={{0,2},{2,4},{4,6},{6,0},{1,3},{3,5},{5,7},{7,1},{8,10},{10,12},{12... | collective-permute-start | bytes 786440 | tf_op jit(solution)/shard_map/ppermute | solution.py:26
  2.7 14.0 %collective-permute-start.1 = (bf16[512,256]{1,0:T(8,128)(2,1)}, bf16[512,256]{1,0:T(8,128)(2,1)S(1)}, u32[]{:S(2)}, u32[]{:S(2)}) collective-permute-start(bf16[512,256]{1,0:T(8,128)(2,1)} %refs_0_.3), channel_id=1, source_target_pairs={{0,4},{2,6},{4,0},{6,2},{1,5},{3,7},{5,1},{7,3},{8,12},{10,14},{12... | collective-permute-start | bytes 786440 | tf_op jit(solution)/shard_map/ppermute | solution.py:26
  5.2 11.6 %collective-permute-start = (bf16[512,256]{1,0:T(8,128)(2,1)}, bf16[512,256]{1,0:T(8,128)(2,1)S(1)}, u32[]{:S(2)}, u32[]{:S(2)}) collective-permute-start(bf16[512,256]{1,0:T(8,128)(2,1)} %refs_0_.3), channel_id=1, source_target_pairs={{0,6},{2,0},{4,2},{6,4},{1,7},{3,1},{5,3},{7,5},{8,14},{10,8},{12,... | collective-permute-start | bytes 786440 | tf_op jit(solution)/shard_map/ppermute | solution.py:26
  6.3 16.1 %collective-permute-start.4 = (bf16[512,256]{1,0:T(8,128)(2,1)}, bf16[512,256]{1,0:T(8,128)(2,1)S(1)}, u32[]{:S(2)}, u32[]{:S(2)}) collective-permute-start(bf16[512,256]{1,0:T(8,128)(2,1)} %refs_0_.3), channel_id=1, source_target_pairs={{0,8},{8,0},{1,9},{9,1},{2,10},{10,2},{3,11},{11,3},{4,12},{12,4},... | collective-permute-start | bytes 786440 | tf_op jit(solution)/shard_map/ppermute | solution.py:30
  8.1 8.7 %copy-start.7 = (bf16[512,256]{1,0:T(8,128)(2,1)}, bf16[512,256]{1,0:T(8,128)(2,1)S(1)}, u32[]{:S(2)}) copy-start(bf16[512,256]{1,0:T(8,128)(2,1)S(1)} %collective-permute-done.2.refs_3_) | copy-start | bytes 786436
  16.7 0.7 copy-start.8
  17.4 0.7 copy-start.9
  20.9 33.1 %collective-permute-start.3 = (bf16[2048,256]{1,0:T(8,128)(2,1)}, bf16[2048,256]{1,0:T(8,128)(2,1)S(1)}, u32[]{:S(2)}, u32[]{:S(2)}) collective-permute-start(bf16[2048,256]{1,0:T(8,128)(2,1)} %shard_map.58.mine.refs_0_), channel_id=1, source_target_pairs={{0,1},{1,0},{2,3},{3,2},{4,5},{5,4},{6,7},{7,6},{8,9},{9,8},{10,11... | collective-permute-start | bytes 3145736 | tf_op jit(solution)/shard_map/ppermute | solution.py:30
  22.5 15.0 %copy-start.6 = (bf16[512,256]{1,0:T(8,128)(2,1)}, bf16[512,256]{1,0:T(8,128)(2,1)S(1)}, u32[]{:S(2)}) copy-start(bf16[512,256]{1,0:T(8,128)(2,1)S(1)} %collective-permute-done.4.refs_0_) | copy-start | bytes 786436
  22.5 9.3 %collective-permute-start.7 = (bf16[512,256]{1,0:T(8,128)(2,1)S(1)}, bf16[512,256]{1,0:T(8,128)(2,1)S(1)}, u32[]{:S(2)}, u32[]{:S(2)}) collective-permute-start(bf16[512,256]{1,0:T(8,128)(2,1)S(1)} %collective-permute-done.4.refs_0_), channel_id=1, source_target_pairs={{0,2},{2,4},{4,6},{6,0},{1,3},{3,5},{5,7},{7,1},{8,10},{10,12},{12... | collective-permute-start | bytes 786440 | tf_op jit(solution)/shard_map/ppermute | solution.py:26
  22.7 14.1 %collective-permute-start.6 = (bf16[512,256]{1,0:T(8,128)(2,1)S(1)}, bf16[512,256]{1,0:T(8,128)(2,1)S(1)}, u32[]{:S(2)}, u32[]{:S(2)}) collective-permute-start(bf16[512,256]{1,0:T(8,128)(2,1)S(1)} %collective-permute-done.4.refs_0_), channel_id=1, source_target_pairs={{0,4},{2,6},{4,0},{6,2},{1,5},{3,7},{5,1},{7,3},{8,12},{10,14},{12... | collective-permute-start | bytes 786440 | tf_op jit(solution)/shard_map/ppermute | solution.py:26
  24.8 12.6 %collective-permute-start.5 = (bf16[512,256]{1,0:T(8,128)(2,1)S(1)}, bf16[512,256]{1,0:T(8,128)(2,1)S(1)}, u32[]{:S(2)}, u32[]{:S(2)}) collective-permute-start(bf16[512,256]{1,0:T(8,128)(2,1)S(1)} %collective-permute-done.4.refs_0_), channel_id=1, source_target_pairs={{0,6},{2,0},{4,2},{6,4},{1,7},{3,1},{5,3},{7,5},{8,14},{10,8},{12,... | collective-permute-start | bytes 786440 | tf_op jit(solution)/shard_map/ppermute | solution.py:26
  31.7 5.7 %copy-start.10 = (bf16[512,256]{1,0:T(8,128)(2,1)}, bf16[512,256]{1,0:T(8,128)(2,1)S(1)}, u32[]{:S(2)}) copy-start(bf16[512,256]{1,0:T(8,128)(2,1)S(1)} %collective-permute-done.7.refs_3_) | copy-start | bytes 786436
  36.8 0.7 copy-start.11
  37.5 0.7 copy-start.12
  41.0 10.6 %copy-start.2 = (bf16[512,2048]{1,0:T(8,128)(2,1)S(1)}, bf16[512,2048]{1,0:T(8,128)(2,1)}, u32[]{:S(2)}) copy-start(bf16[512,2048]{1,0:T(8,128)(2,1)} %teacher.1) | copy-start | bytes 6291460
  41.0 22.2 %collective-permute-start.8 = (bf16[2048,256]{1,0:T(8,128)(2,1)}, bf16[2048,256]{1,0:T(8,128)(2,1)}, u32[]{:S(2)}, u32[]{:S(2)}) collective-permute-start(bf16[2048,256]{1,0:T(8,128)(2,1)} %shard_map.60.refs_2_.mine), channel_id=1, source_target_pairs={{0,1},{1,0},{2,3},{3,2},{4,5},{5,4},{6,7},{7,6},{8,9},{9,8},{10,11... | collective-permute-start | bytes 3145736 | tf_op jit(solution)/shard_map/ppermute | solution.py:30
  46.3 25.1 %all-to-all-start.1 = ((f32[16,2,512]{2,1,0:T(2,128)}), f32[16,2,512]{2,1,0:T(2,128)S(1)}, u32[]{:S(2)}, u32[]{:S(2)}) async-start(f32[16,2,512]{2,1,0:T(2,128)} %broadcast_in_dim.10), calls=%async_computation.1 | async-start | bytes 131072 | tf_op jit(solution)/shard_map/all_to_all | solution.py:35
  52.7 30.7 %collective-permute-start.9 = (bf16[512,1024]{1,0:T(8,128)(2,1)}, bf16[512,1024]{1,0:T(8,128)(2,1)}, u32[]{:S(2)}, u32[]{:S(2)}) collective-permute-start(bf16[512,1024]{1,0:T(8,128)(2,1)} %constant_dynamic-slice_fusion), channel_id=1, source_target_pairs={{0,8},{8,0},{1,9},{9,1},{2,10},{10,2},{3,11},{11,3},{4,12},{12,4},... | collective-permute-start | bytes 3145736 | tf_op jit(solution)/shard_map/ppermute | solution.py:30
  54.0 1.0 copy-start.3
  72.1 11.3 %all-to-all-start = ((f32[16,2,1024]{2,1,0:T(2,128)}), f32[16,2,1024]{2,1,0:T(2,128)S(1)}, u32[]{:S(2)}, u32[]{:S(2)}) async-start(f32[16,2,1024]{2,1,0:T(2,128)} %broadcast_in_dim.9), calls=%async_computation | async-start | bytes 262144 | tf_op jit(solution)/shard_map/all_to_all | solution.py:35
  83.4 5.6 %copy-start.17 = (bf16[1024,512]{1,0:T(8,128)(2,1)S(1)}, bf16[1024,512]{1,0:T(8,128)(2,1)}, u32[]{:S(2)}) copy-start(bf16[1024,512]{1,0:T(8,128)(2,1)} %get-tuple-element.22) | copy-start | bytes 3145732
  97.7 7.1 %copy-start.1 = (bf16[1024,512]{1,0:T(8,128)(2,1)S(1)}, bf16[1024,512]{1,0:T(8,128)(2,1)}, u32[]{:S(2)}) copy-start(bf16[1024,512]{1,0:T(8,128)(2,1)} %get-tuple-element.38.last) | copy-start | bytes 3145732
  97.7 7.1 %copy-start.16 = (bf16[1024,512]{1,0:T(8,128)(2,1)S(1)}, bf16[1024,512]{1,0:T(8,128)(2,1)}, u32[]{:S(2)}) copy-start(bf16[1024,512]{1,0:T(8,128)(2,1)} %get-tuple-element.35) | copy-start | bytes 3145732
  104.4 53.5 %collective-permute-start.13 = (bf16[4,1024,256]{2,1,0:T(8,128)(2,1)}, bf16[4,1024,256]{2,1,0:T(8,128)(2,1)}, u32[]{:S(2)}, u32[]{:S(2)}) collective-permute-start(bf16[4,1024,256]{2,1,0:T(8,128)(2,1)} %shard_map.66), channel_id=1, source_target_pairs={{0,1},{1,0},{2,3},{3,2},{4,5},{5,4},{6,7},{7,6},{8,9},{9,8},{10,11... | collective-permute-start | bytes 6291464 | tf_op jit(solution)/shard_map/ppermute | solution.py:30
  104.7 3.8 %copy-start.15 = (bf16[1024,512]{1,0:T(8,128)(2,1)S(1)}, bf16[1024,512]{1,0:T(8,128)(2,1)}, u32[]{:S(2)}) copy-start(bf16[1024,512]{1,0:T(8,128)(2,1)} %get-tuple-element.36) | copy-start | bytes 3145732
  105.5 15.0 %collective-permute-start.18 = (bf16[512,512]{1,0:T(8,128)(2,1)S(1)}, bf16[512,512]{1,0:T(8,128)(2,1)S(1)}, u32[]{:S(2)}, u32[]{:S(2)}) collective-permute-start(bf16[512,512]{1,0:T(8,128)(2,1)S(1)} %convolution_convert_fusion.2), channel_id=1, source_target_pairs={{0,128},{64,192},{128,0},{192,64},{1,129},{65,193},{129,1},{193,65... | collective-permute-start | bytes 1572872 | tf_op jit(solution)/shard_map/ppermute | solution.py:26
  109.2 4.4 %copy-start = (bf16[1024,512]{1,0:T(8,128)(2,1)S(1)}, bf16[1024,512]{1,0:T(8,128)(2,1)}, u32[]{:S(2)}) copy-start(bf16[1024,512]{1,0:T(8,128)(2,1)} %shard_map.64.first) | copy-start | bytes 3145732
  109.2 23.4 %collective-permute-start.19 = (bf16[512,512]{1,0:T(8,128)(2,1)S(1)}, bf16[512,512]{1,0:T(8,128)(2,1)S(1)}, u32[]{:S(2)}, u32[]{:S(2)}) collective-permute-start(bf16[512,512]{1,0:T(8,128)(2,1)S(1)} %convolution_convert_fusion.1), channel_id=1, source_target_pairs={{0,64},{64,128},{128,192},{192,0},{1,65},{65,129},{129,193},{193,1... | collective-permute-start | bytes 1572872 | tf_op jit(solution)/shard_map/ppermute | solution.py:26
  111.3 28.8 %collective-permute-start.20 = (bf16[512,512]{1,0:T(8,128)(2,1)}, bf16[512,512]{1,0:T(8,128)(2,1)}, u32[]{:S(2)}, u32[]{:S(2)}) collective-permute-start(bf16[512,512]{1,0:T(8,128)(2,1)} %convolution_convert_fusion), channel_id=1, source_target_pairs={{0,192},{64,0},{128,64},{192,128},{1,193},{65,1},{129,65},{193,129... | collective-permute-start | bytes 1572872 | tf_op jit(solution)/shard_map/ppermute | solution.py:26
  115.2 38.1 %collective-permute-start.10 = (bf16[512,512]{1,0:T(8,128)(2,1)}, bf16[512,512]{1,0:T(8,128)(2,1)S(1)}, u32[]{:S(2)}, u32[]{:S(2)}) collective-permute-start(bf16[512,512]{1,0:T(8,128)(2,1)} %convolution_convert_fusion.4), channel_id=1, source_target_pairs={{0,128},{64,192},{128,0},{192,64},{1,129},{65,193},{129,1},{193,65... | collective-permute-start | bytes 1572872 | tf_op jit(solution)/shard_map/ppermute | solution.py:26
  120.5 12.2 %copy-start.13 = (bf16[512,512]{1,0:T(8,128)(2,1)}, bf16[512,512]{1,0:T(8,128)(2,1)S(1)}, u32[]{:S(2)}) copy-start(bf16[512,512]{1,0:T(8,128)(2,1)S(1)} %collective-permute-done.18) | copy-start | bytes 1572868
  120.5 34.3 %collective-permute-start.11 = (bf16[512,512]{1,0:T(8,128)(2,1)}, bf16[512,512]{1,0:T(8,128)(2,1)}, u32[]{:S(2)}, u32[]{:S(2)}) collective-permute-start(bf16[512,512]{1,0:T(8,128)(2,1)} %convolution_convert_fusion.3), channel_id=1, source_target_pairs={{0,64},{64,128},{128,192},{192,0},{1,65},{65,129},{129,193},{193,1... | collective-permute-start | bytes 1572872 | tf_op jit(solution)/shard_map/ppermute | solution.py:26
  132.6 0.8 copy-start.14
  132.6 22.1 %collective-permute-start.12 = (bf16[512,512]{1,0:T(8,128)(2,1)S(1)}, bf16[512,512]{1,0:T(8,128)(2,1)}, u32[]{:S(2)}, u32[]{:S(2)}) collective-permute-start(bf16[512,512]{1,0:T(8,128)(2,1)S(1)} %convolution_convert_fusion.5), channel_id=1, source_target_pairs={{0,192},{64,0},{128,64},{192,128},{1,193},{65,1},{129,65},{193,129... | collective-permute-start | bytes 1572872 | tf_op jit(solution)/shard_map/ppermute | solution.py:26
  134.1 11.8 %all-to-all-start.2 = ((f32[16,1,1024]{2,1,0:T(1,128)}), f32[16,1,1024]{2,1,0:T(1,128)S(1)}, u32[]{:S(2)}, u32[]{:S(2)}) async-start(f32[16,1,1024]{2,1,0:T(1,128)} %broadcast_in_dim.11), calls=%async_computation.2 | async-start | bytes 131072 | tf_op jit(solution)/shard_map/all_to_all | solution.py:35
  145.9 25.5 %all-to-all-start.4 = ((bf16[8,64,512]{2,1,0:T(8,128)(2,1)}), bf16[8,64,512]{2,1,0:T(8,128)(2,1)S(1)}, u32[]{:S(2)}, u32[]{:S(2)}) async-start(bf16[8,64,512]{2,1,0:T(8,128)(2,1)} %bitcast.16), calls=%async_computation.4 | async-start | bytes 1048576 | tf_op jit(solution)/shard_map/all_to_all | solution.py:400
  167.1 14.3 %collective-permute-start.14 = (bf16[1024,256]{1,0:T(8,128)(2,1)}, bf16[1024,256]{1,0:T(8,128)(2,1)S(1)}, u32[]{:S(2)}, u32[]{:S(2)}) collective-permute-start(bf16[1024,256]{1,0:T(8,128)(2,1)} %get-tuple-element.39), channel_id=1, source_target_pairs={{0,4},{2,6},{4,0},{6,2},{1,5},{3,7},{5,1},{7,3},{8,12},{10,14},{12... | collective-permute-start | bytes 1572872 | tf_op jit(solution)/shard_map/ppermute | solution.py:26
  170.0 23.1 %collective-permute-start.16 = (bf16[1024,256]{1,0:T(8,128)(2,1)S(1)}, bf16[1024,256]{1,0:T(8,128)(2,1)S(1)}, u32[]{:S(2)}, u32[]{:S(2)}) collective-permute-start(bf16[1024,256]{1,0:T(8,128)(2,1)S(1)} %get-tuple-element.40), channel_id=1, source_target_pairs={{0,6},{2,0},{4,2},{6,4},{1,7},{3,1},{5,3},{7,5},{8,14},{10,8},{12,... | collective-permute-start | bytes 1572872 | tf_op jit(solution)/shard_map/ppermute | solution.py:26
  170.9 23.1 %collective-permute-start.15 = (bf16[1024,256]{1,0:T(8,128)(2,1)S(1)}, bf16[1024,256]{1,0:T(8,128)(2,1)}, u32[]{:S(2)}, u32[]{:S(2)}) collective-permute-start(bf16[1024,256]{1,0:T(8,128)(2,1)S(1)} %get-tuple-element.41), channel_id=1, source_target_pairs={{0,2},{2,4},{4,6},{6,0},{1,3},{3,5},{5,7},{7,1},{8,10},{10,12},{12... | collective-permute-start | bytes 1572872 | tf_op jit(solution)/shard_map/ppermute | solution.py:26
  171.5 24.0 %copy-start.4 = (bf16[8,64,512]{2,1,0:T(8,128)(2,1)}, bf16[8,64,512]{2,1,0:T(8,128)(2,1)S(1)}, u32[]{:S(2)}) copy-start(bf16[8,64,512]{2,1,0:T(8,128)(2,1)S(1)} %all-to-all-done.4.refs_1_) | copy-start | bytes 1572868
  171.5 26.1 %all-to-all-start.3 = ((bf16[8,64,512]{2,1,0:T(8,128)(2,1)}), bf16[8,64,512]{2,1,0:T(8,128)(2,1)S(1)}, u32[]{:S(2)}, u32[]{:S(2)}) async-start(bf16[8,64,512]{2,1,0:T(8,128)(2,1)} %bitcast.11), calls=%async_computation.3 | async-start | bytes 1048576 | tf_op jit(solution)/shard_map/all_to_all | solution.py:400
  195.5 7.3 %collective-permute-start.17 = (bf16[512,256]{1,0:T(8,128)(2,1)S(1)}, bf16[512,256]{1,0:T(8,128)(2,1)S(1)}, u32[]{:S(2)}, u32[]{:S(2)}) collective-permute-start(bf16[512,256]{1,0:T(8,128)(2,1)S(1)} %slice.69), channel_id=1, source_target_pairs={{0,8},{8,0},{1,9},{9,1},{2,10},{10,2},{3,11},{11,3},{4,12},{12,4},... | collective-permute-start | bytes 786440 | tf_op jit(solution)/shard_map/ppermute | solution.py:30
  197.6 0.8 copy-start.5

commit v2 on v1

v2 whole, which is shorter than its diff:
```python
import functools

import jax
import jax.numpy as jnp
from jax import lax
from jax.experimental import pallas as pl
from jax.experimental.pallas import tpu as pltpu
from jax.sharding import Mesh
from jax.sharding import PartitionSpec as P


DP = ("y", "p", "q")
VOCAB = ("x", "c")
WHOLE_VOCAB = ("q", "x", "c")
SWAP = ((0, 1), (1, 0))
CHUNKS = (512, 512)


grad_scale = 8.0
BF = jnp.bfloat16
F32 = jnp.float32


def sent(array, axis, by):
    size = lax.axis_size(axis)
    return lax.ppermute(array, axis, [(k, (k + by) % size) for k in range(size)])


def swapped(array, axis):
    return lax.ppermute(array, axis, SWAP)


def sent_to_all(array, axis):
    copies = jnp.broadcast_to(array, (lax.axis_size(axis), *array.shape))
    return lax.all_to_all(copies, axis, 0, 0, tiled=True)


def whole(shape):
    return pl.BlockSpec(shape, lambda *_: (0,) * len(shape))


def after(array, *others):
    return lax.optimization_barrier((array, *others))[0]


def call(body, where, operands, in_specs, out_shapes, out_specs, grid=(1,), scratch=(), micros=2, vmem=20):
    operands = [
        pltpu.with_memory_space_constraint(array, pltpu.HBM) if array.size > 2**17 else array
        for array in operands
    ]
    out_shapes = jax.tree.map(
        lambda s: pltpu.HBM(s.shape, s.dtype) if s.size > 2**17 else s, out_shapes
    )
    cost = pl.CostEstimate(flops=int(micros * 4.5e8), bytes_accessed=2**20, transcendentals=0)
    return pl.pallas_call(
        body,
        cost_estimate=cost,
        out_shape=out_shapes,
        grid_spec=pltpu.PrefetchScalarGridSpec(
            num_scalar_prefetch=1,
            grid=grid,
            in_specs=in_specs,
            out_specs=out_specs,
            scratch_shapes=scratch,
        ),
        compiler_params=pltpu.CompilerParams(vmem_limit_bytes=vmem * 2**20),
    )(where, *operands)


def as_row(column):
    return jnp.transpose(jnp.broadcast_to(column, (column.shape[0], 128)))[0:1]


def as_column(row):
    return jnp.transpose(jnp.broadcast_to(row, (128, row.shape[1])))[:, 0:1]


def lane_sums(value):
    lanes = value[:, 0:128]
    for k in range(128, value.shape[1], 128):
        lanes = lanes + value[:, k : k + 128]
    return jnp.sum(lanes, axis=1, keepdims=True)


def totals(stats, value, teacher=None, top=None, row_block=128):
    rows, columns = value.shape
    found = ([], [], [])
    for at in range(0, rows, row_block):
        part = value[at : at + row_block, :].astype(F32)
        lanes = part[:, 0:128]
        for k in range(128, columns, 128):
            lanes = jnp.maximum(lanes, part[:, k : k + 128])
        peak = jnp.max(lanes, axis=1, keepdims=True)
        found[0].append(peak)
        found[1].append(lane_sums(jnp.exp(part - peak)))
        if teacher is not None:
            other = teacher[at : at + row_block, :].astype(F32)
            terms = jnp.exp(other - top[at : at + row_block])
            found[2].append(lane_sums(terms * (other - part)))
    for k, part in enumerate(found):
        if part:
            stats[k : k + 1, :] = as_row(jnp.concatenate(part, axis=0))


def student_body(block, group, where, *refs):
    slices, weights, (teacher, teacher_stats, total, stats) = refs[:8], refs[8:12], refs[12:]
    q, c = where[2], where[4]
    width = slices[0].shape[1]
    step = pl.program_id(0)
    value = None
    for k in range(4):
        for side in (0, 1):
            at = pl.multiple_of((c if side == 0 else 1 - c) * width, width)
            got = jnp.dot(
                slices[2 * k + side][...],
                weights[k][pl.ds(at, width), :],
                preferred_element_type=F32,
            )
            value = got if value is None else value + got
    total[:, pl.ds(pl.multiple_of(step * block, block), block)] = value

    @pl.when(step == pl.num_programs(0) - 1)
    def _():
        if group == 0:
            top = teacher_stats[0:1, :]
        else:
            half = teacher_stats.shape[0] // 2
            every = teacher_stats[pl.ds((1 - q) * half, half), :, :]
            top = jnp.max(every[:, 0], axis=0, keepdims=True)
        totals(stats, total, teacher, as_column(top))


def student_part(where, pairs, weight, teacher, teacher_stats, group, block=256):
    rows, width = pairs[0][0].shape
    columns = weight.shape[1] // 2
    steps = columns // block
    in_specs = [whole((rows, width))] * 8
    for by in range(4):
        in_specs.append(
            pl.BlockSpec(
                (2 * width, block),
                lambda j, at, by=by: (lax.rem(at[3] + by, 4), at[2] * steps + j),
            )
        )
    return call(
        functools.partial(student_body, block, group),
        where,
        [*(array for pair in pairs for array in pair), *[weight] * 4, teacher, teacher_stats],
        in_specs + [whole((rows, columns)), whole(teacher_stats.shape)],
        [jax.ShapeDtypeStruct((rows, columns), F32), jax.ShapeDtypeStruct((3, rows), F32)],
        [whole((rows, columns)), whole((3, rows))],
        (steps,),
        micros=8,
        vmem=28,
    )


def teacher_body(where, teacher, stats):
    totals(stats, teacher)


def arrange_body(where, *refs):
    pairs, outs = refs[:-4], refs[-4:]
    y, x, c = where[0], where[3], where[4]
    width = pairs[0].shape[1]
    rows = outs[0].shape[0] // 2
    for r in range(4):
        d = lax.rem(x + r - y + 4, 4)
        for side in range(4):

            @pl.when(d == side)
            def _(r=r, side=side):
                for group in range(2):
                    mine = pairs[8 * group + 2 * r][...]
                    other = pairs[8 * group + 2 * r + 1][...]
                    to = slice(group * rows, (group + 1) * rows)
                    outs[side][to, 0:width] = jnp.where(c == 0, mine, other)
                    outs[side][to, width : 2 * width] = jnp.where(c == 0, other, mine)


def merged(parts):
    top = jnp.max(parts[0][:, 0], axis=0, keepdims=True)
    for part in parts[1:]:
        top = jnp.maximum(top, jnp.max(part[:, 0], axis=0, keepdims=True))
    total = sum(
        jnp.sum(part[:, 1] * jnp.exp(part[:, 0] - top), axis=0, keepdims=True) for part in parts
    )
    return top, total


def grad_body(first, where, s_own, s_other, t_own, t_other, every_s, every_t, out, *refs):
    if first:
        scales = refs
    else:
        tops, *scales = refs
    q = where[2]
    step = pl.program_id(0)
    steps = pl.num_programs(0)
    block = s_own.shape[0]
    rows = every_t.shape[2]
    half = every_s.shape[0] // 2

    @pl.when(step == 0)
    def _():
        for group in range(2):
            at = slice(group * rows, (group + 1) * rows)
            to = slice((1 - group) * rows, (2 - group) * rows)
            mine = every_s[pl.ds(q * half, half), :, at]
            other = every_s[pl.ds((1 - q) * half, half), :, to]
            s_top, s_total = merged((mine, other))
            source = q if group == 0 else 1 - q
            every = every_t[pl.ds(source * half, half), :, :]
            t_top, t_total = merged((every,))
            if group == 0 and not first:
                cross = jnp.sum(mine[:, 2] * jnp.exp(every[:, 0] - t_top), axis=0, keepdims=True)
                cross = cross + jnp.sum(other[:, 2], axis=0, keepdims=True)
                for k, row in enumerate((s_top, s_total, t_top, t_total, cross)):
                    tops[k : k + 1, :] = row
            wanted = (s_top, grad_scale / s_total, t_top, grad_scale / t_total)
            for row, scale in zip(wanted, scales):
                scale[at, :] = jnp.transpose(jnp.broadcast_to(row, (128, rows)))

    def rows_of(student, teacher):
        at = pl.ds(pl.multiple_of(step * block, block), block)
        s_top, s_scale, t_top, t_scale = (scale[at, :] for scale in scales)
        for k in range(0, out.shape[1], 128):
            s = student[:, k : k + 128]
            t = teacher[:, k : k + 128].astype(F32)
            out[:, k : k + 128] = (
                jnp.exp(s - s_top) * s_scale - jnp.exp(t - t_top) * t_scale
            ).astype(BF)

    @pl.when(step < steps // 2)
    def _():
        rows_of(s_own, t_own)

    @pl.when(step >= steps // 2)
    def _():
        rows_of(s_other, t_other)


def grad_part(where, values, every_s, every_t, count, first, block=256):
    rows, half = values[0].shape
    steps = 2 * rows // block
    place = 0 if first else half // count - 1
    early = pl.BlockSpec((block, count), lambda j, at: (jnp.minimum(j, steps // 2 - 1), place))
    late = pl.BlockSpec((block, count), lambda j, at: (jnp.maximum(j - steps // 2, 0), place))
    shapes = [jax.ShapeDtypeStruct((2 * rows, count), BF)]
    specs = [pl.BlockSpec((block, count), lambda j, at: (j, 0))]
    if not first:
        shapes.append(jax.ShapeDtypeStruct((5, rows), F32))
        specs.append(whole((5, rows)))
    return call(
        functools.partial(grad_body, first),
        where,
        [*values, every_s, every_t],
        [early, late, early, late, whole(every_s.shape), whole(every_t.shape)],
        shapes,
        specs,
        (steps,),
        [pltpu.VMEM((2 * rows, 128), F32)] * 4,
        micros=4,
    )


def hidden_body(with_arrived, where, first, last, *refs):
    weights, refs = refs[:4], refs[4:]
    split = first.shape[1]
    for d in range(4):
        value = lax.dot_general(
            first[...], weights[d][:, :split], (((1,), (1,)), ((), ())), preferred_element_type=F32
        ) + lax.dot_general(
            last[...], weights[d][:, split:], (((1,), (1,)), ((), ())), preferred_element_type=F32
        )
        if with_arrived:
            refs[1 + d][...] = (value + refs[0][d].astype(F32)).astype(BF)
        else:
            refs[0][d] = value.astype(BF)


def hidden_part(where, grads, weight, begin, count, arrived=None, block=256):
    half = weight.shape[1] // 2
    width = 256
    this_core = arrived is not None
    at_row = begin // block

    def weight_block(j, at, d):
        core = at[4] if this_core else 1 - at[4]
        return (2 * lax.rem(at[3] + d, 4) + core, at[2])

    operands = [*grads, *[weight] * 4]
    in_specs = [
        *(pl.BlockSpec((block, g.shape[1]), lambda j, at: (at_row + j, 0)) for g in grads),
        *(
            pl.BlockSpec((width, half), functools.partial(weight_block, d=d))
            for d in range(4)
        ),
    ]
    if this_core:
        operands.append(arrived)
        in_specs.append(pl.BlockSpec((4, block, width), lambda j, at: (0, at_row + j, 0)))
        shapes = [jax.ShapeDtypeStruct((count, width), BF)] * 4
        specs = [pl.BlockSpec((block, width), lambda j, at: (j, 0))] * 4
    else:
        shapes = jax.ShapeDtypeStruct((4, count, width), BF)
        specs = pl.BlockSpec((4, block, width), lambda j, at: (0, j, 0))
    return call(
        functools.partial(hidden_body, this_core),
        where,
        operands,
        in_specs,
        shapes,
        specs,
        (count // block,),
        micros=6,
    )


def final_body(where, *refs):
    out = refs[-1]
    half = out.shape[1] // 2
    begin = 0
    for piece in refs[:-1]:
        chunk = piece.shape[2]
        for side in (0, 1):
            at = side * half + begin
            out[:, at : at + chunk] = sum(piece[2 * p + side].astype(F32) for p in range(4))
        begin += chunk


def per_device(hidden_states, teacher_logits, head_weight):
    rows, width = hidden_states.shape
    _, columns = head_weight.shape
    half = columns // 2
    where = jnp.stack([lax.axis_index(name) for name in (*DP, *VOCAB)]).astype(jnp.int32)
    q = lax.axis_index("q")

    other_hidden = swapped(hidden_states, "q")
    (teacher_stats,) = call(
        teacher_body,
        where,
        [teacher_logits],
        [whole(teacher_logits.shape)],
        [jax.ShapeDtypeStruct((2, rows), F32)],
        [whole((2, rows))],
        micros=5,
    )
    every_teacher = sent_to_all(teacher_stats, WHOLE_VOCAB)
    kept_teacher = lax.dynamic_slice_in_dim(teacher_logits, q * half, half, 1)
    sent_teacher = lax.dynamic_slice_in_dim(teacher_logits, (1 - q) * half, half, 1)
    arrived_teacher = swapped(sent_teacher, "q")
    gathered = []
    for piece in (hidden_states, other_hidden):
        slices = [piece, *(sent(piece, "x", by) for by in (-1, 2, 1))]
        pairs = []
        for part in slices:
            pairs.append((part, swapped(part, "c")))
        gathered.append(pairs)

    student_own, stats_own = student_part(
        where, gathered[0], head_weight, kept_teacher, teacher_stats, 0
    )
    student_other, stats_other = student_part(
        where, gathered[1], head_weight, arrived_teacher, every_teacher, 1
    )
    every_student = sent_to_all(jnp.concatenate([stats_own, stats_other], axis=1), WHOLE_VOCAB)
    flat = [array for pairs in gathered for pair in pairs for array in pair]
    blocks = call(
        arrange_body,
        where,
        flat,
        [whole(array.shape) for array in flat],
        [jax.ShapeDtypeStruct((2 * rows, 2 * width), BF)] * 4,
        [whole((2 * rows, 2 * width))] * 4,
        micros=5,
    )
    values = (student_own, student_other, kept_teacher, arrived_teacher)
    (grad_first,) = grad_part(where, values, every_student, every_teacher, CHUNKS[0], True)

    pieces = []
    begin = -CHUNKS[0]
    grads = grad_first
    gate = None
    owned = []
    for k, chunk in enumerate(CHUNKS):
        if k:
            grads = after(grad_last, gate)[:, begin : begin + chunk]
        begin += chunk
        parts = []
        for d in (2, 1, 3):
            part = lax.dot_general(
                blocks[d], grads, (((0,), (0,)), ((), ())), preferred_element_type=F32
            ).astype(BF)
            parts.append(sent(part, "y", d))
        if k == 0:
            later = tuple(after(value, part) for value in values)
            grad_last, tops = grad_part(
                where, later, every_student, every_teacher, half - CHUNKS[0], False
            )
            leaving = hidden_part(where, (grad_first, grad_last), head_weight, 0, 2 * rows)
            across_core = swapped(leaving, "c")
            gate = leaving
        owned.append((grads, parts))
    reduced = {}
    for k, (chunk, (grads, parts)) in enumerate(zip(CHUNKS, owned)):
        own = lax.dot_general(
            blocks[0], grads, (((0,), (0,)), ((), ())), preferred_element_type=F32
        )
        total = own + sum(part.astype(F32) for part in parts)
        total = total.astype(BF).reshape(8, -1, chunk)
        pieces.append(lax.all_to_all(total, ("p", "q"), 0, 0, tiled=True))
        if k == 0:
            gate = total
            for group in (1, 0):
                later = (grad_first, after(grad_last, gate))
                value = hidden_part(
                    where, later, head_weight, group * rows, rows, across_core
                )
                gate = value[0]
                moved = [sent(value[d], "x", d) for d in (2, 1, 3)]
                reduced[group] = value[0].astype(F32) + sum(part.astype(F32) for part in moved)
    head_grad = call(
        final_body,
        where,
        pieces,
        [whole(piece.shape) for piece in pieces],
        jax.ShapeDtypeStruct((pieces[0].shape[1], columns), F32),
        whole((pieces[0].shape[1], columns)),
    )
    partner = swapped(reduced[1].astype(BF), "q")
    hidden_grad = (reduced[0] + partner.astype(F32)).astype(BF)

    student_max, student_total, teacher_max, teacher_total, cross_term = tops
    divergence = (
        cross_term / teacher_total
        - teacher_max
        - jnp.log(teacher_total)
        + student_max
        + jnp.log(student_total)
    )
    return divergence, hidden_grad, head_grad


def solution(mesh):
    split = Mesh(mesh.devices.reshape(4, 4, 2, 4, 2), (*DP, *VOCAB))
    placed = (P(DP, VOCAB), P(DP, VOCAB), P(None, VOCAB))

    return jax.shard_map(
        per_device,
        mesh=split,
        in_specs=placed,
        out_specs=(P(DP), P(DP, VOCAB), P(DP, VOCAB)),
        check_vma=False,
    )
```

time: 205 us -> 211 us (1.029)
  waiting for transfers between devices: 55.3 us -> 81.8 us
  Pallas kernels: 59.2 us -> 54.1 us
  local copies, waits for them, and re-layouts: 11.4 us -> 6.79 us
  starting transfers between devices: 59.3 us -> 54.7 us
  matrix products: 14.5 us -> 10.1 us
    ppermute x6 -> x12, waiting for transfers between devices: 1.8 us -> 17.8 us  [swapped(): return lax.ppermute(array, axis, SWAP)]
    ppermute x15 -> x18, waiting for transfers between devices: 50.9 us -> 61.9 us  [sent(): lax.ppermute(array, axis, [(k, (k + by) % size) for k in range(size)])]
    all_to_all x3 -> x2, starting transfers between devices: 16.2 us -> 10.1 us  [sent_to_all(): return lax.all_to_all(copies, axis, 0, 0, tiled=True)]
    ppermute x6 -> x12, starting transfers between devices: 7.66 us -> 13.5 us  [swapped(): return lax.ppermute(array, axis, SWAP)]
    pallas_call x11 -> x10, Pallas kernels: 59.2 us -> 54.1 us  [call(): pl.pallas_call(body, cost_estimate=cost, out_shape=out_shapes, grid_spec=...]
    ppermute x15 -> x18, starting transfers between devices: 20.9 us -> 17.4 us  [sent(): lax.ppermute(array, axis, [(k, (k + by) % size) for k in range(size)])]
    dot_general x2, matrix products: 6.4 us -> 3.11 us  [per_device(): lax.dot_general(blocks[0], grads, (((0,), (0,)), ((), ())), preferred_ele...]
    unnamed x36 -> x24, local copies, waits for them, and re-layouts: 4.81 us -> 2.19 us
  transfers between devices with their start and end apart: 26 -> 34, of which waited for: 12 -> 13; matrix products, arithmetic and copies ran while one was open for 11% -> 6% of each run, Pallas kernels for 20% -> 19%
where the time goes in v2:
time: 211 us; the launch traced here: 210 us
  waiting for transfers between devices  81.8 us (39%)
  starting transfers between devices  54.7 us (26%)
  Pallas kernels  54.1 us (26%)
  matrix products  10.1 us (5%)
  local copies, waits for them, and re-layouts  6.79 us (3%)
    ppermute x18, waiting for transfers between devices, sent(): lax.ppermute(array, axis, [(k, (k + by) % size) for k in range(size)])  61.9 us
    pallas_call x10, Pallas kernels, call(): pl.pallas_call(body, cost_estimate=cost, out_shape=out_shapes, grid_spec=...  54.1 us
    ppermute x12, waiting for transfers between devices, swapped(): return lax.ppermute(array, axis, SWAP)  17.8 us
    ppermute x18, starting transfers between devices, sent(): lax.ppermute(array, axis, [(k, (k + by) % size) for k in range(size)])  17.4 us
    all_to_all x2, starting transfers between devices, per_device(): pieces.append(lax.all_to_all(total, ('p', 'q'), 0, 0, tiled=True))  13.6 us
    ppermute x12, starting transfers between devices, swapped(): return lax.ppermute(array, axis, SWAP)  13.5 us
    all_to_all x2, starting transfers between devices, sent_to_all(): return lax.all_to_all(copies, axis, 0, 0, tiled=True)  10.1 us
    dot_general x6, matrix products, per_device(): lax.dot_general(blocks[d], grads, (((0,), (0,)), ((), ())), preferred_ele...  6.94 us
  transfers between devices with their start and end apart: 34, of which 13 were waited for; matrix products, arithmetic and copies ran while one was open for 6% of the time, Pallas kernels for 19%

profile of v2, /device:TPU:1, one launch (start us, length us, event | category | flops | bytes accessed | tf_op | source)
XLA Modules:
  0.0 209.9 jit_solution(16675641438572899987)
XLA Ops:
  0.6 3.3 %collective-permute-start = (bf16[512,256]{1,0:T(8,128)(2,1)}, bf16[512,256]{1,0:T(8,128)(2,1)S(1)}, u32[]{:S(2)}, u32[]{:S(2)}) collective-permute-start(bf16[512,256]{1,0:T(8,128)(2,1)} %refs_0_.6), channel_id=1, source_target_pairs={{0,1},{1,0},{2,3},{3,2},{4,5},{5,4},{6,7},{7,6},{8,9},{9,8},{10,11... | collective-permute-start | bytes 786440 | tf_op jit(solution)/shard_map/ppermute | solution.py:30
  5.2 3.1 %constant_dynamic-slice_fusion = (bf16[512,1024]{1,0:T(8,128)(2,1)}, bf16[512,1024]{1,0:T(8,128)(2,1)}) fusion(bf16[512,2048]{1,0:T(8,128)(2,1)} %teacher.1, s32[]{:T(128)S(6)} %select_n.7, s32[]{:T(128)S(6)} %select_n.6), kind=kLoop, calls=%fused_computation.14 | loop fusion | bytes 4194312 | tf_op jit(solution)/shard_map/dynamic_slice | solution.py:350
  8.3 1.6 collective-permute-start.15
  10.6 1.3 collective-permute-done.1.refs_2_
  11.9 1.5 collective-permute-start.2
  13.9 2.1 collective-permute-start.4
  16.0 3.7 %collective-permute-done.5.refs_6_ = bf16[512,256]{1,0:T(8,128)(2,1)S(1)} collective-permute-done((bf16[512,256]{1,0:T(8,128)(2,1)S(1)}, bf16[512,256]{1,0:T(8,128)(2,1)S(1)}, u32[]{:S(2)}, u32[]{:S(2)}) %collective-permute-start.5) | collective-permute-done | bytes 262176 | tf_op jit(solution)/shard_map/ppermute | solution.py:26
  19.7 1.1 collective-permute-start.6
  20.7 17.8 %collective-permute-done.7.refs_8_.refs_0_ = bf16[512,256]{1,0:T(8,128)(2,1)S(1)} collective-permute-done((bf16[512,256]{1,0:T(8,128)(2,1)S(1)}, bf16[512,256]{1,0:T(8,128)(2,1)S(1)}, u32[]{:S(2)}, u32[]{:S(2)}) %collective-permute-start.7) | collective-permute-done | bytes 262176 | tf_op jit(solution)/shard_map/ppermute | solution.py:30
  38.5 2.2 %collective-permute-start.9 = (bf16[512,256]{1,0:T(8,128)(2,1)S(1)}, bf16[512,256]{1,0:T(8,128)(2,1)S(1)}, u32[]{:S(2)}, u32[]{:S(2)}) collective-permute-start(bf16[512,256]{1,0:T(8,128)(2,1)S(1)} %collective-permute-done.7.refs_8_.refs_0_), channel_id=1, source_target_pairs={{0,6},{2,0},{4,2},{6,4},{1,7},{3,1},{5,3},{7,5},{8,14},{10,8},{12,... | collective-permute-start | bytes 786440 | tf_op jit(solution)/shard_map/ppermute | solution.py:26
  41.0 0.9 collective-permute-start.13
  41.9 3.4 %shard_map.58.refs_13_ = f32[2,512]{1,0:T(2,128)S(1)} custom-call(s32[5]{0:T(128)S(1)} %stack.23.where, bf16[512,2048]{1,0:T(8,128)(2,1)} %teacher.1), custom_call_target="tpu_custom_call" | custom-call | flops 2249999872 | bytes 1048576 | tf_op jit(solution)/shard_map/pallas_call | solution.py:55
  46.0 6.7 %all-to-all-start = ((f32[16,2,512]{2,1,0:T(2,128)}), f32[16,2,512]{2,1,0:T(2,128)S(1)}, u32[]{:S(2)}, u32[]{:S(2)}) async-start(f32[16,2,512]{2,1,0:T(2,128)} %broadcast_in_dim.6), calls=%async_computation | async-start | bytes 131072 | tf_op jit(solution)/shard_map/all_to_all | solution.py:35
  53.4 2.6 %collective-permute-done.13.refs_14_.refs_6_ = bf16[512,256]{1,0:T(8,128)(2,1)S(1)} collective-permute-done((bf16[512,256]{1,0:T(8,128)(2,1)S(1)}, bf16[512,256]{1,0:T(8,128)(2,1)S(1)}, u32[]{:S(2)}, u32[]{:S(2)}) %collective-permute-start.13) | collective-permute-done | bytes 262176 | tf_op jit(solution)/shard_map/ppermute | solution.py:26
  56.6 9.0 %shard_map.59 = (f32[512,1024]{1,0:T(8,128)}, f32[3,512]{1,0:T(4,128)S(1)}) custom-call(s32[5]{0:T(128)S(1)} %stack.23.where, bf16[512,256]{1,0:T(8,128)(2,1)S(1)} %copy-done, bf16[512,256]{1,0:T(8,128)(2,1)S(1)} %collective-permute-done.refs_1_, bf16[512,256]{1,0:T(8,128)(2,1)S(1)} %collective-permute-done.1.refs_2_, ...), custom_call_target="tpu_custom_call" | custom-call | flops 3600000000 | bytes 1048576 | tf_op jit(solution)/shard_map/pallas_call | solution.py:55
  65.6 9.2 %shard_map.61 = (f32[512,1024]{1,0:T(8,128)}, f32[3,512]{1,0:T(4,128)S(1)}) custom-call(s32[5]{0:T(128)S(1)} %stack.23.where, bf16[512,256]{1,0:T(8,128)(2,1)S(1)} %collective-permute-done.7.refs_8_.refs_0_, bf16[512,256]{1,0:T(8,128)(2,1)S(1)} %collective-permute-done.8.refs_9_.refs_1_, bf16[512,256]{1,0:T(8,128)(2,1)S(1)} %collective-permute-done.9.refs_10_.refs_2_, ...), custom_call_target="tpu_custom_call" | custom-call | flops 3600000000 | bytes 1048576 | tf_op jit(solution)/shard_map/pallas_call | solution.py:55
  75.6 3.4 %all-to-all-start.1 = ((f32[16,3,1024]{2,1,0:T(4,128)}), f32[16,3,1024]{2,1,0:T(4,128)S(1)}, u32[]{:S(2)}, u32[]{:S(2)}) async-start(f32[16,3,1024]{2,1,0:T(4,128)} %broadcast_in_dim.7), calls=%async_computation.1 | async-start | bytes 524288 | tf_op jit(solution)/shard_map/all_to_all | solution.py:35
  79.0 0.9 copy-done.2
  80.0 4.1 %shard_map.60 = (bf16[1024,512]{1,0:T(8,128)(2,1)}, bf16[1024,512]{1,0:T(8,128)(2,1)}, bf16[1024,512]{1,0:T(8,128)(2,1)}, bf16[1024,512]{1,0:T(8,128)(2,1)}) custom-call(s32[5]{0:T(128)S(1)} %stack.23.where, bf16[512,256]{1,0:T(8,128)(2,1)S(1)} %copy-done, bf16[512,256]{1,0:T(8,128)(2,1)S(1)} %collective-permute-done.refs_1_, ...), custom_call_target="tpu_custom_call" | custom-call | flops 2249999872 | bytes 1048576 | tf_op jit(solution)/shard_map/pallas_call | solution.py:55
  84.0 2.1 %all-to-all-done.1.every_s = f32[16,3,1024]{2,1,0:T(4,128)S(1)} async-done(((f32[16,3,1024]{2,1,0:T(4,128)}), f32[16,3,1024]{2,1,0:T(4,128)S(1)}, u32[]{:S(2)}, u32[]{:S(2)}) %all-to-all-start.1) | async-done | bytes 196640 | tf_op jit(solution)/shard_map/all_to_all | solution.py:35
  86.2 5.5 %shard_map.62.first = bf16[1024,512]{1,0:T(8,128)(2,1)} custom-call(s32[5]{0:T(128)S(1)} %stack.23.where, f32[512,1024]{1,0:T(8,128)} %get-tuple-element.33.s_own, f32[512,1024]{1,0:T(8,128)} %get-tuple-element.34.s_other, bf16[512,1024]{1,0:T(8,128)(2,1)} %get-tuple-element.35.refs_12_.t_own, bf16[512,1024]{1,0:T(8,128)(2,1)} %collective-permute-done.15.refs_12_.t_other, ...), custom_call_target="tpu_custom_call" | custom-call | flops 1800000000 | bytes 1048576 | tf_op jit(solution)/shard_map/pallas_call | solution.py:55
  91.7 2.0 convolution_convert_fusion.5
  93.7 2.4 %collective-permute-start.18 = (bf16[512,512]{1,0:T(8,128)(2,1)S(1)}, bf16[512,512]{1,0:T(8,128)(2,1)S(1)}, u32[]{:S(2)}, u32[]{:S(2)}) collective-permute-start(bf16[512,512]{1,0:T(8,128)(2,1)S(1)} %convolution_convert_fusion.5), channel_id=1, source_target_pairs={{0,192},{64,0},{128,64},{192,128},{1,193},{65,1},{129,65},{193,129... | collective-permute-start | bytes 1572872 | tf_op jit(solution)/shard_map/ppermute | solution.py:26
  96.1 5.5 %shard_map.63 = (bf16[1024,512]{1,0:T(8,128)(2,1)}, f32[5,512]{1,0:T(8,128)S(1)}) custom-call(s32[5]{0:T(128)S(1)} %stack.23.where, f32[512,1024]{1,0:T(8,128)} %get-tuple-element.33.s_own, f32[512,1024]{1,0:T(8,128)} %get-tuple-element.34.s_other, bf16[512,1024]{1,0:T(8,128)(2,1)} %get-tuple-element.35.refs_12_.t_own, ...), custom_call_target="tpu_custom_call" | custom-call | flops 1800000000 | bytes 1048576 | tf_op jit(solution)/shard_map/pallas_call | solution.py:55
  101.6 6.7 %shard_map.64 = bf16[4,1024,256]{2,1,0:T(8,128)(2,1)} custom-call(s32[5]{0:T(128)S(1)} %stack.23.where, bf16[1024,512]{1,0:T(8,128)(2,1)} %shard_map.62.first, bf16[1024,512]{1,0:T(8,128)(2,1)} %get-tuple-element.52.last, bf16[2048,2048]{1,0:T(8,128)(2,1)} %refs_3_.5, bf16[2048,2048]{1,0:T(8,128)(2,1)} %refs_3_.5, bf16[2048,2048]{1,0:T(8,128)(2,1)} %refs_3_.5, ...), custom_call_target="tpu_custom_call" | custom-call | flops 2700000000 | bytes 1048576 | tf_op jit(solution)/shard_map/pallas_call | solution.py:55
  108.3 1.2 collective-permute-start.19
  111.4 1.6 collective-permute-start.16
  114.5 21.7 %collective-permute-done.17 = bf16[512,512]{1,0:T(8,128)(2,1)S(1)} collective-permute-done((bf16[512,512]{1,0:T(8,128)(2,1)S(1)}, bf16[512,512]{1,0:T(8,128)(2,1)S(1)}, u32[]{:S(2)}, u32[]{:S(2)}) %collective-permute-start.17) | collective-permute-done | bytes 524320 | tf_op jit(solution)/shard_map/ppermute | solution.py:26
  136.2 1.6 fusion
  137.8 7.3 %all-to-all-start.2 = ((bf16[8,64,512]{2,1,0:T(8,128)(2,1)}), bf16[8,64,512]{2,1,0:T(8,128)(2,1)S(1)}, u32[]{:S(2)}, u32[]{:S(2)}) async-start(bf16[8,64,512]{2,1,0:T(8,128)(2,1)} %bitcast.6), calls=%async_computation.2 | async-start | bytes 1048576 | tf_op jit(solution)/shard_map/all_to_all | solution.py:411
  145.1 2.1 convolution_convert_fusion.2
  147.2 1.5 collective-permute-start.28
  149.2 10.3 %collective-permute-done.29 = bf16[512,512]{1,0:T(8,128)(2,1)S(1)} collective-permute-done((bf16[512,512]{1,0:T(8,128)(2,1)S(1)}, bf16[512,512]{1,0:T(8,128)(2,1)S(1)}, u32[]{:S(2)}, u32[]{:S(2)}) %collective-permute-start.29) | collective-permute-done | bytes 524320 | tf_op jit(solution)/shard_map/ppermute | solution.py:26
  159.5 2.0 collective-permute-done.28
  161.6 9.8 %collective-permute-done.27 = bf16[512,512]{1,0:T(8,128)(2,1)S(1)} collective-permute-done((bf16[512,512]{1,0:T(8,128)(2,1)S(1)}, bf16[512,512]{1,0:T(8,128)(2,1)S(1)}, u32[]{:S(2)}, u32[]{:S(2)}) %collective-permute-start.27) | collective-permute-done | bytes 524320 | tf_op jit(solution)/shard_map/ppermute | solution.py:26
  171.4 1.6 fusion.1
  173.0 6.3 %all-to-all-start.3 = ((bf16[8,64,512]{2,1,0:T(8,128)(2,1)}), bf16[8,64,512]{2,1,0:T(8,128)(2,1)S(1)}, u32[]{:S(2)}, u32[]{:S(2)}) async-start(bf16[8,64,512]{2,1,0:T(8,128)(2,1)} %bitcast.7), calls=%async_computation.3 | async-start | bytes 1048576 | tf_op jit(solution)/shard_map/all_to_all | solution.py:411
  179.3 4.0 %shard_map.65 = (bf16[512,256]{1,0:T(8,128)(2,1)S(1)}, bf16[512,256]{1,0:T(8,128)(2,1)S(1)}, bf16[512,256]{1,0:T(8,128)(2,1)S(1)}, bf16[512,256]{1,0:T(8,128)(2,1)S(1)}) custom-call(s32[5]{0:T(128)S(1)} %stack.23.where, bf16[1024,512]{1,0:T(8,128)(2,1)} %shard_map.62.first, bf16[1024,512]{1,0:T(8,128)(2,1)} %get-tuple-element.52.last, ...), custom_call_target="tpu_custom_call" | custom-call | flops 2700000000 | bytes 1048576 | tf_op jit(solution)/shard_map/pallas_call | solution.py:55
  183.9 1.1 collective-permute-start.24
  185.1 4.0 %shard_map.66 = (bf16[512,256]{1,0:T(8,128)(2,1)S(1)}, bf16[512,256]{1,0:T(8,128)(2,1)S(1)}, bf16[512,256]{1,0:T(8,128)(2,1)S(1)}, bf16[512,256]{1,0:T(8,128)(2,1)S(1)}) custom-call(s32[5]{0:T(128)S(1)} %stack.23.where, bf16[1024,512]{1,0:T(8,128)(2,1)} %shard_map.62.first, bf16[1024,512]{1,0:T(8,128)(2,1)} %get-tuple-element.52.last, ...), custom_call_target="tpu_custom_call" | custom-call | flops 2700000000 | bytes 1048576 | tf_op jit(solution)/shard_map/pallas_call | solution.py:55
  189.2 2.3 %collective-permute-start.22 = (bf16[512,256]{1,0:T(8,128)(2,1)S(1)}, bf16[512,256]{1,0:T(8,128)(2,1)S(1)}, u32[]{:S(2)}, u32[]{:S(2)}) collective-permute-start(bf16[512,256]{1,0:T(8,128)(2,1)S(1)} %get-tuple-element.48), channel_id=1, source_target_pairs={{0,6},{2,0},{4,2},{6,4},{1,7},{3,1},{5,3},{7,5},{8,14},{10,8},{12,... | collective-permute-start | bytes 786440 | tf_op jit(solution)/shard_map/ppermute | solution.py:26
  191.4 2.0 collective-permute-start.20
  194.1 1.5 collective-permute-start.26
  196.2 0.8 copy-done.6
  197.0 2.7 %shard_map.67 = f32[64,2048]{1,0:T(8,128)} custom-call(s32[5]{0:T(128)S(1)} %stack.23.where, bf16[8,64,512]{2,1,0:T(8,128)(2,1)} %copy-done.5, bf16[8,64,512]{2,1,0:T(8,128)(2,1)} %copy-done.6), custom_call_target="tpu_custom_call" | custom-call | flops 900000000 | bytes 1048576 | tf_op jit(solution)/shard_map/pallas_call | solution.py:55
  199.7 2.0 collective-permute-done.22
  201.6 7.4 %collective-permute-done.21 = bf16[512,256]{1,0:T(8,128)(2,1)S(1)} collective-permute-done((bf16[512,256]{1,0:T(8,128)(2,1)S(1)}, bf16[512,256]{1,0:T(8,128)(2,1)S(1)}, u32[]{:S(2)}, u32[]{:S(2)}) %collective-permute-start.21) | collective-permute-done | bytes 262176 | tf_op jit(solution)/shard_map/ppermute | solution.py:26
  209.0 0.9 add_convert_fusion
  (70 shorter events, 11.5 us)
Async XLA Ops:
  0.6 9.9 %collective-permute-start = (bf16[512,256]{1,0:T(8,128)(2,1)}, bf16[512,256]{1,0:T(8,128)(2,1)S(1)}, u32[]{:S(2)}, u32[]{:S(2)}) collective-permute-start(bf16[512,256]{1,0:T(8,128)(2,1)} %refs_0_.6), channel_id=1, source_target_pairs={{0,1},{1,0},{2,3},{3,2},{4,5},{5,4},{6,7},{7,6},{8,9},{9,8},{10,11... | collective-permute-start | bytes 786440 | tf_op jit(solution)/shard_map/ppermute | solution.py:30
  3.9 8.0 %collective-permute-start.1 = (bf16[512,256]{1,0:T(8,128)(2,1)}, bf16[512,256]{1,0:T(8,128)(2,1)S(1)}, u32[]{:S(2)}, u32[]{:S(2)}) collective-permute-start(bf16[512,256]{1,0:T(8,128)(2,1)} %refs_0_.6), channel_id=1, source_target_pairs={{0,6},{2,0},{4,2},{6,4},{1,7},{3,1},{5,3},{7,5},{8,14},{10,8},{12,... | collective-permute-start | bytes 786440 | tf_op jit(solution)/shard_map/ppermute | solution.py:26
  4.7 9.2 %collective-permute-start.3 = (bf16[512,256]{1,0:T(8,128)(2,1)}, bf16[512,256]{1,0:T(8,128)(2,1)S(1)}, u32[]{:S(2)}, u32[]{:S(2)}) collective-permute-start(bf16[512,256]{1,0:T(8,128)(2,1)} %refs_0_.6), channel_id=1, source_target_pairs={{0,4},{2,6},{4,0},{6,2},{1,5},{3,7},{5,1},{7,3},{8,12},{10,14},{12... | collective-permute-start | bytes 786440 | tf_op jit(solution)/shard_map/ppermute | solution.py:26
  5.2 4.7 %copy-start = (bf16[512,256]{1,0:T(8,128)(2,1)S(1)}, bf16[512,256]{1,0:T(8,128)(2,1)}, u32[]{:S(2)}) copy-start(bf16[512,256]{1,0:T(8,128)(2,1)} %refs_0_.6) | copy-start | bytes 786436
  8.3 57.3 %collective-permute-start.15 = (bf16[512,1024]{1,0:T(8,128)(2,1)}, bf16[512,1024]{1,0:T(8,128)(2,1)}, u32[]{:S(2)}, u32[]{:S(2)}) collective-permute-start(bf16[512,1024]{1,0:T(8,128)(2,1)} %get-tuple-element.53), channel_id=1, source_target_pairs={{0,8},{8,0},{1,9},{9,1},{2,10},{10,2},{3,11},{11,3},{4,12},{12,4},... | collective-permute-start | bytes 3145736 | tf_op jit(solution)/shard_map/ppermute | solution.py:30
  9.9 9.7 %collective-permute-start.5 = (bf16[512,256]{1,0:T(8,128)(2,1)S(1)}, bf16[512,256]{1,0:T(8,128)(2,1)S(1)}, u32[]{:S(2)}, u32[]{:S(2)}) collective-permute-start(bf16[512,256]{1,0:T(8,128)(2,1)S(1)} %copy-done), channel_id=1, source_target_pairs={{0,2},{2,4},{4,6},{6,0},{1,3},{3,5},{5,7},{7,1},{8,10},{10,12},{12... | collective-permute-start | bytes 786440 | tf_op jit(solution)/shard_map/ppermute | solution.py:26
  10.6 28.0 %collective-permute-start.7 = (bf16[512,256]{1,0:T(8,128)(2,1)S(1)}, bf16[512,256]{1,0:T(8,128)(2,1)S(1)}, u32[]{:S(2)}, u32[]{:S(2)}) collective-permute-start(bf16[512,256]{1,0:T(8,128)(2,1)S(1)} %copy-done), channel_id=1, source_target_pairs={{0,8},{8,0},{1,9},{9,1},{2,10},{10,2},{3,11},{11,3},{4,12},{12,4},... | collective-permute-start | bytes 786440 | tf_op jit(solution)/shard_map/ppermute | solution.py:30
  11.9 28.9 %collective-permute-start.2 = (bf16[512,256]{1,0:T(8,128)(2,1)S(1)}, bf16[512,256]{1,0:T(8,128)(2,1)S(1)}, u32[]{:S(2)}, u32[]{:S(2)}) collective-permute-start(bf16[512,256]{1,0:T(8,128)(2,1)S(1)} %collective-permute-done.1.refs_2_), channel_id=1, source_target_pairs={{0,1},{1,0},{2,3},{3,2},{4,5},{5,4},{6,7},{7,6},{8,9},{9,8},{10,11... | collective-permute-start | bytes 786440 | tf_op jit(solution)/shard_map/ppermute | solution.py:30
  13.9 27.1 %collective-permute-start.4 = (bf16[512,256]{1,0:T(8,128)(2,1)S(1)}, bf16[512,256]{1,0:T(8,128)(2,1)S(1)}, u32[]{:S(2)}, u32[]{:S(2)}) collective-permute-start(bf16[512,256]{1,0:T(8,128)(2,1)S(1)} %collective-permute-done.3.refs_4_), channel_id=1, source_target_pairs={{0,1},{1,0},{2,3},{3,2},{4,5},{5,4},{6,7},{7,6},{8,9},{9,8},{10,11... | collective-permute-start | bytes 786440 | tf_op jit(solution)/shard_map/ppermute | solution.py:30
  19.7 33.0 %collective-permute-start.6 = (bf16[512,256]{1,0:T(8,128)(2,1)S(1)}, bf16[512,256]{1,0:T(8,128)(2,1)S(1)}, u32[]{:S(2)}, u32[]{:S(2)}) collective-permute-start(bf16[512,256]{1,0:T(8,128)(2,1)S(1)} %collective-permute-done.5.refs_6_), channel_id=1, source_target_pairs={{0,1},{1,0},{2,3},{3,2},{4,5},{5,4},{6,7},{7,6},{8,9},{9,8},{10,11... | collective-permute-start | bytes 786440 | tf_op jit(solution)/shard_map/ppermute | solution.py:30
  38.5 14.3 %collective-permute-start.9 = (bf16[512,256]{1,0:T(8,128)(2,1)S(1)}, bf16[512,256]{1,0:T(8,128)(2,1)S(1)}, u32[]{:S(2)}, u32[]{:S(2)}) collective-permute-start(bf16[512,256]{1,0:T(8,128)(2,1)S(1)} %collective-permute-done.7.refs_8_.refs_0_), channel_id=1, source_target_pairs={{0,6},{2,0},{4,2},{6,4},{1,7},{3,1},{5,3},{7,5},{8,14},{10,8},{12,... | collective-permute-start | bytes 786440 | tf_op jit(solution)/shard_map/ppermute | solution.py:26
  40.8 12.5 %collective-permute-start.11 = (bf16[512,256]{1,0:T(8,128)(2,1)S(1)}, bf16[512,256]{1,0:T(8,128)(2,1)S(1)}, u32[]{:S(2)}, u32[]{:S(2)}) collective-permute-start(bf16[512,256]{1,0:T(8,128)(2,1)S(1)} %collective-permute-done.7.refs_8_.refs_0_), channel_id=1, source_target_pairs={{0,4},{2,6},{4,0},{6,2},{1,5},{3,7},{5,1},{7,3},{8,12},{10,14},{12... | collective-permute-start | bytes 786440 | tf_op jit(solution)/shard_map/ppermute | solution.py:26
  41.0 15.0 %collective-permute-start.13 = (bf16[512,256]{1,0:T(8,128)(2,1)S(1)}, bf16[512,256]{1,0:T(8,128)(2,1)S(1)}, u32[]{:S(2)}, u32[]{:S(2)}) collective-permute-start(bf16[512,256]{1,0:T(8,128)(2,1)S(1)} %collective-permute-done.7.refs_8_.refs_0_), channel_id=1, source_target_pairs={{0,2},{2,4},{4,6},{6,0},{1,3},{3,5},{5,7},{7,1},{8,10},{10,12},{12... | collective-permute-start | bytes 786440 | tf_op jit(solution)/shard_map/ppermute | solution.py:26
  46.0 19.5 %all-to-all-start = ((f32[16,2,512]{2,1,0:T(2,128)}), f32[16,2,512]{2,1,0:T(2,128)S(1)}, u32[]{:S(2)}, u32[]{:S(2)}) async-start(f32[16,2,512]{2,1,0:T(2,128)} %broadcast_in_dim.6), calls=%async_computation | async-start | bytes 131072 | tf_op jit(solution)/shard_map/all_to_all | solution.py:35
  52.7 12.8 %collective-permute-start.8 = (bf16[512,256]{1,0:T(8,128)(2,1)S(1)}, bf16[512,256]{1,0:T(8,128)(2,1)S(1)}, u32[]{:S(2)}, u32[]{:S(2)}) collective-permute-start(bf16[512,256]{1,0:T(8,128)(2,1)S(1)} %collective-permute-done.7.refs_8_.refs_0_), channel_id=1, source_target_pairs={{0,1},{1,0},{2,3},{3,2},{4,5},{5,4},{6,7},{7,6},{8,9},{9,8},{10,11... | collective-permute-start | bytes 786440 | tf_op jit(solution)/shard_map/ppermute | solution.py:30
  52.9 12.7 %collective-permute-start.10 = (bf16[512,256]{1,0:T(8,128)(2,1)S(1)}, bf16[512,256]{1,0:T(8,128)(2,1)}, u32[]{:S(2)}, u32[]{:S(2)}) collective-permute-start(bf16[512,256]{1,0:T(8,128)(2,1)S(1)} %collective-permute-done.9.refs_10_.refs_2_), channel_id=1, source_target_pairs={{0,1},{1,0},{2,3},{3,2},{4,5},{5,4},{6,7},{7,6},{8,9},{9,8},{10,11... | collective-permute-start | bytes 786440 | tf_op jit(solution)/shard_map/ppermute | solution.py:30
  53.3 12.3 %collective-permute-start.12 = (bf16[512,256]{1,0:T(8,128)(2,1)S(1)}, bf16[512,256]{1,0:T(8,128)(2,1)}, u32[]{:S(2)}, u32[]{:S(2)}) collective-permute-start(bf16[512,256]{1,0:T(8,128)(2,1)S(1)} %collective-permute-done.11.refs_12_.refs_4_), channel_id=1, source_target_pairs={{0,1},{1,0},{2,3},{3,2},{4,5},{5,4},{6,7},{7,6},{8,9},{9,8},{10,11... | collective-permute-start | bytes 786440 | tf_op jit(solution)/shard_map/ppermute | solution.py:30
  56.0 9.6 %collective-permute-start.14 = (bf16[512,256]{1,0:T(8,128)(2,1)S(1)}, bf16[512,256]{1,0:T(8,128)(2,1)}, u32[]{:S(2)}, u32[]{:S(2)}) collective-permute-start(bf16[512,256]{1,0:T(8,128)(2,1)S(1)} %collective-permute-done.13.refs_14_.refs_6_), channel_id=1, source_target_pairs={{0,1},{1,0},{2,3},{3,2},{4,5},{5,4},{6,7},{7,6},{8,9},{9,8},{10,11... | collective-permute-start | bytes 786440 | tf_op jit(solution)/shard_map/ppermute | solution.py:30
  65.5 9.3 %copy-start.1 = (bf16[512,256]{1,0:T(8,128)(2,1)}, bf16[512,256]{1,0:T(8,128)(2,1)S(1)}, u32[]{:S(2)}) copy-start(bf16[512,256]{1,0:T(8,128)(2,1)S(1)} %collective-permute-done.8.refs_9_.refs_1_) | copy-start | bytes 786436
  75.6 10.6 %all-to-all-start.1 = ((f32[16,3,1024]{2,1,0:T(4,128)}), f32[16,3,1024]{2,1,0:T(4,128)S(1)}, u32[]{:S(2)}, u32[]{:S(2)}) async-start(f32[16,3,1024]{2,1,0:T(4,128)} %broadcast_in_dim.7), calls=%async_computation.1 | async-start | bytes 524288 | tf_op jit(solution)/shard_map/all_to_all | solution.py:35
  79.0 1.0 copy-start.2
  86.2 5.5 %copy-start.11 = (bf16[1024,512]{1,0:T(8,128)(2,1)S(1)}, bf16[1024,512]{1,0:T(8,128)(2,1)}, u32[]{:S(2)}) copy-start(bf16[1024,512]{1,0:T(8,128)(2,1)} %get-tuple-element.29) | copy-start | bytes 3145732
  93.7 20.8 %collective-permute-start.18 = (bf16[512,512]{1,0:T(8,128)(2,1)S(1)}, bf16[512,512]{1,0:T(8,128)(2,1)S(1)}, u32[]{:S(2)}, u32[]{:S(2)}) collective-permute-start(bf16[512,512]{1,0:T(8,128)(2,1)S(1)} %convolution_convert_fusion.5), channel_id=1, source_target_pairs={{0,192},{64,0},{128,64},{192,128},{1,193},{65,1},{129,65},{193,129... | collective-permute-start | bytes 1572872 | tf_op jit(solution)/shard_map/ppermute | solution.py:26
  101.6 7.9 %copy-start.3 = (bf16[1024,512]{1,0:T(8,128)(2,1)S(1)}, bf16[1024,512]{1,0:T(8,128)(2,1)}, u32[]{:S(2)}) copy-start(bf16[1024,512]{1,0:T(8,128)(2,1)} %shard_map.62.first) | copy-start | bytes 3145732
  101.6 7.9 %copy-start.10 = (bf16[1024,512]{1,0:T(8,128)(2,1)S(1)}, bf16[1024,512]{1,0:T(8,128)(2,1)}, u32[]{:S(2)}) copy-start(bf16[1024,512]{1,0:T(8,128)(2,1)} %get-tuple-element.41) | copy-start | bytes 3145732
  108.3 71.0 %collective-permute-start.19 = (bf16[4,1024,256]{2,1,0:T(8,128)(2,1)}, bf16[4,1024,256]{2,1,0:T(8,128)(2,1)}, u32[]{:S(2)}, u32[]{:S(2)}) collective-permute-start(bf16[4,1024,256]{2,1,0:T(8,128)(2,1)} %shard_map.64), channel_id=1, source_target_pairs={{0,1},{1,0},{2,3},{3,2},{4,5},{5,4},{6,7},{7,6},{8,9},{9,8},{10,11... | collective-permute-start | bytes 6291464 | tf_op jit(solution)/shard_map/ppermute | solution.py:30
  109.5 1.2 copy-start.9
  110.2 26.0 %collective-permute-start.17 = (bf16[512,512]{1,0:T(8,128)(2,1)S(1)}, bf16[512,512]{1,0:T(8,128)(2,1)S(1)}, u32[]{:S(2)}, u32[]{:S(2)}) collective-permute-start(bf16[512,512]{1,0:T(8,128)(2,1)S(1)} %convolution_convert_fusion.3), channel_id=1, source_target_pairs={{0,64},{64,128},{128,192},{192,0},{1,65},{65,129},{129,193},{193,1... | collective-permute-start | bytes 1572872 | tf_op jit(solution)/shard_map/ppermute | solution.py:26
  110.7 2.3 %copy-start.4 = (bf16[1024,512]{1,0:T(8,128)(2,1)S(1)}, bf16[1024,512]{1,0:T(8,128)(2,1)}, u32[]{:S(2)}) copy-start(bf16[1024,512]{1,0:T(8,128)(2,1)} %get-tuple-element.52.last) | copy-start | bytes 3145732
  111.4 24.8 %collective-permute-start.16 = (bf16[512,512]{1,0:T(8,128)(2,1)S(1)}, bf16[512,512]{1,0:T(8,128)(2,1)S(1)}, u32[]{:S(2)}, u32[]{:S(2)}) collective-permute-start(bf16[512,512]{1,0:T(8,128)(2,1)S(1)} %convolution_convert_fusion.4), channel_id=1, source_target_pairs={{0,128},{64,192},{128,0},{192,64},{1,129},{65,193},{129,1},{193,65... | collective-permute-start | bytes 1572872 | tf_op jit(solution)/shard_map/ppermute | solution.py:26
  113.7 22.5 %copy-start.7 = (bf16[1024,512]{1,0:T(8,128)(2,1)S(1)}, bf16[1024,512]{1,0:T(8,128)(2,1)}, u32[]{:S(2)}) copy-start(bf16[1024,512]{1,0:T(8,128)(2,1)} %get-tuple-element.39) | copy-start | bytes 3145732
  137.8 35.2 %all-to-all-start.2 = ((bf16[8,64,512]{2,1,0:T(8,128)(2,1)}), bf16[8,64,512]{2,1,0:T(8,128)(2,1)S(1)}, u32[]{:S(2)}, u32[]{:S(2)}) async-start(bf16[8,64,512]{2,1,0:T(8,128)(2,1)} %bitcast.6), calls=%async_computation.2 | async-start | bytes 1048576 | tf_op jit(solution)/shard_map/all_to_all | solution.py:411
  145.1 26.3 %copy-start.8 = (bf16[1024,512]{1,0:T(8,128)(2,1)S(1)}, bf16[1024,512]{1,0:T(8,128)(2,1)}, u32[]{:S(2)}) copy-start(bf16[1024,512]{1,0:T(8,128)(2,1)} %get-tuple-element.39) | copy-start | bytes 3145732
  147.1 12.4 %collective-permute-start.29 = (bf16[512,512]{1,0:T(8,128)(2,1)S(1)}, bf16[512,512]{1,0:T(8,128)(2,1)S(1)}, u32[]{:S(2)}, u32[]{:S(2)}) collective-permute-start(bf16[512,512]{1,0:T(8,128)(2,1)S(1)} %convolution_convert_fusion), channel_id=1, source_target_pairs={{0,192},{64,0},{128,64},{192,128},{1,193},{65,1},{129,65},{193,129... | collective-permute-start | bytes 1572872 | tf_op jit(solution)/shard_map/ppermute | solution.py:26
  147.2 14.3 %collective-permute-start.28 = (bf16[512,512]{1,0:T(8,128)(2,1)S(1)}, bf16[512,512]{1,0:T(8,128)(2,1)S(1)}, u32[]{:S(2)}, u32[]{:S(2)}) collective-permute-start(bf16[512,512]{1,0:T(8,128)(2,1)S(1)} %convolution_convert_fusion.1), channel_id=1, source_target_pairs={{0,64},{64,128},{128,192},{192,0},{1,65},{65,129},{129,193},{193,1... | collective-permute-start | bytes 1572872 | tf_op jit(solution)/shard_map/ppermute | solution.py:26
  148.7 22.7 %collective-permute-start.27 = (bf16[512,512]{1,0:T(8,128)(2,1)S(1)}, bf16[512,512]{1,0:T(8,128)(2,1)S(1)}, u32[]{:S(2)}, u32[]{:S(2)}) collective-permute-start(bf16[512,512]{1,0:T(8,128)(2,1)S(1)} %convolution_convert_fusion.2), channel_id=1, source_target_pairs={{0,128},{64,192},{128,0},{192,64},{1,129},{65,193},{129,1},{193,65... | collective-permute-start | bytes 1572872 | tf_op jit(solution)/shard_map/ppermute | solution.py:26
  173.0 10.4 %copy-start.5 = (bf16[8,64,512]{2,1,0:T(8,128)(2,1)}, bf16[8,64,512]{2,1,0:T(8,128)(2,1)S(1)}, u32[]{:S(2)}) copy-start(bf16[8,64,512]{2,1,0:T(8,128)(2,1)S(1)} %all-to-all-done.2.refs_0_) | copy-start | bytes 1572868
  173.0 23.3 %all-to-all-start.3 = ((bf16[8,64,512]{2,1,0:T(8,128)(2,1)}), bf16[8,64,512]{2,1,0:T(8,128)(2,1)S(1)}, u32[]{:S(2)}, u32[]{:S(2)}) async-start(bf16[8,64,512]{2,1,0:T(8,128)(2,1)} %bitcast.7), calls=%async_computation.3 | async-start | bytes 1048576 | tf_op jit(solution)/shard_map/all_to_all | solution.py:411
  183.4 8.1 %collective-permute-start.25 = (bf16[512,256]{1,0:T(8,128)(2,1)S(1)}, bf16[512,256]{1,0:T(8,128)(2,1)S(1)}, u32[]{:S(2)}, u32[]{:S(2)}) collective-permute-start(bf16[512,256]{1,0:T(8,128)(2,1)S(1)} %get-tuple-element.51), channel_id=1, source_target_pairs={{0,6},{2,0},{4,2},{6,4},{1,7},{3,1},{5,3},{7,5},{8,14},{10,8},{12,... | collective-permute-start | bytes 786440 | tf_op jit(solution)/shard_map/ppermute | solution.py:26
  183.9 10.1 %collective-permute-start.24 = (bf16[512,256]{1,0:T(8,128)(2,1)S(1)}, bf16[512,256]{1,0:T(8,128)(2,1)S(1)}, u32[]{:S(2)}, u32[]{:S(2)}) collective-permute-start(bf16[512,256]{1,0:T(8,128)(2,1)S(1)} %get-tuple-element.50), channel_id=1, source_target_pairs={{0,2},{2,4},{4,6},{6,0},{1,3},{3,5},{5,7},{7,1},{8,10},{10,12},{12... | collective-permute-start | bytes 786440 | tf_op jit(solution)/shard_map/ppermute | solution.py:26
  184.9 9.0 %collective-permute-start.23 = (bf16[512,256]{1,0:T(8,128)(2,1)S(1)}, bf16[512,256]{1,0:T(8,128)(2,1)S(1)}, u32[]{:S(2)}, u32[]{:S(2)}) collective-permute-start(bf16[512,256]{1,0:T(8,128)(2,1)S(1)} %get-tuple-element.49), channel_id=1, source_target_pairs={{0,4},{2,6},{4,0},{6,2},{1,5},{3,7},{5,1},{7,3},{8,12},{10,14},{12... | collective-permute-start | bytes 786440 | tf_op jit(solution)/shard_map/ppermute | solution.py:26
  189.2 12.5 %collective-permute-start.22 = (bf16[512,256]{1,0:T(8,128)(2,1)S(1)}, bf16[512,256]{1,0:T(8,128)(2,1)S(1)}, u32[]{:S(2)}, u32[]{:S(2)}) collective-permute-start(bf16[512,256]{1,0:T(8,128)(2,1)S(1)} %get-tuple-element.48), channel_id=1, source_target_pairs={{0,6},{2,0},{4,2},{6,4},{1,7},{3,1},{5,3},{7,5},{8,14},{10,8},{12,... | collective-permute-start | bytes 786440 | tf_op jit(solution)/shard_map/ppermute | solution.py:26
  191.4 17.6 %collective-permute-start.21 = (bf16[512,256]{1,0:T(8,128)(2,1)S(1)}, bf16[512,256]{1,0:T(8,128)(2,1)S(1)}, u32[]{:S(2)}, u32[]{:S(2)}) collective-permute-start(bf16[512,256]{1,0:T(8,128)(2,1)S(1)} %get-tuple-element.47), channel_id=1, source_target_pairs={{0,2},{2,4},{4,6},{6,0},{1,3},{3,5},{5,7},{7,1},{8,10},{10,12},{12... | collective-permute-start | bytes 786440 | tf_op jit(solution)/shard_map/ppermute | solution.py:26
  191.4 17.6 %collective-permute-start.20 = (bf16[512,256]{1,0:T(8,128)(2,1)S(1)}, bf16[512,256]{1,0:T(8,128)(2,1)S(1)}, u32[]{:S(2)}, u32[]{:S(2)}) collective-permute-start(bf16[512,256]{1,0:T(8,128)(2,1)S(1)} %get-tuple-element.46), channel_id=1, source_target_pairs={{0,4},{2,6},{4,0},{6,2},{1,5},{3,7},{5,1},{7,3},{8,12},{10,14},{12... | collective-permute-start | bytes 786440 | tf_op jit(solution)/shard_map/ppermute | solution.py:26
  194.1 14.9 %collective-permute-start.26 = (bf16[512,256]{1,0:T(8,128)(2,1)S(1)}, bf16[512,256]{1,0:T(8,128)(2,1)S(1)}, u32[]{:S(2)}, u32[]{:S(2)}) collective-permute-start(bf16[512,256]{1,0:T(8,128)(2,1)S(1)} %add_convert_fusion.1), channel_id=1, source_target_pairs={{0,8},{8,0},{1,9},{9,1},{2,10},{10,2},{3,11},{11,3},{4,12},{12,4},... | collective-permute-start | bytes 786440 | tf_op jit(solution)/shard_map/ppermute | solution.py:30
  196.2 0.8 copy-start.6

commit v3 on v2

--- a/solution.py
+++ b/solution.py
@@ -43,10 +43,12 @@
     return lax.optimization_barrier((array, *others))[0]
 
 
-def call(body, where, operands, in_specs, out_shapes, out_specs, grid=(1,), scratch=(), micros=2, vmem=20):
+def call(body, where, operands, in_specs, out_shapes, out_specs, grid=(1,), scratch=(), micros=2, vmem=20, loose=()):
     operands = [
-        pltpu.with_memory_space_constraint(array, pltpu.HBM) if array.size > 2**17 else array
-        for array in operands
+        pltpu.with_memory_space_constraint(array, pltpu.HBM)
+        if array.size > 2**17 and k not in loose
+        else array
+        for k, array in enumerate(operands)
     ]
     out_shapes = jax.tree.map(
         lambda s: pltpu.HBM(s.shape, s.dtype) if s.size > 2**17 else s, out_shapes
@@ -71,10 +73,6 @@
     return jnp.transpose(jnp.broadcast_to(column, (column.shape[0], 128)))[0:1]
 
 
-def as_column(row):
-    return jnp.transpose(jnp.broadcast_to(row, (128, row.shape[1])))[:, 0:1]
-
-
 def lane_sums(value):
     lanes = value[:, 0:128]
     for k in range(128, value.shape[1], 128):
@@ -82,9 +80,9 @@
     return jnp.sum(lanes, axis=1, keepdims=True)
 
 
-def totals(stats, value, teacher=None, top=None, row_block=128):
+def totals(stats, value, row_block=128):
     rows, columns = value.shape
-    found = ([], [], [])
+    found = ([], [])
     for at in range(0, rows, row_block):
         part = value[at : at + row_block, :].astype(F32)
         lanes = part[:, 0:128]
@@ -93,44 +91,64 @@
         peak = jnp.max(lanes, axis=1, keepdims=True)
         found[0].append(peak)
         found[1].append(lane_sums(jnp.exp(part - peak)))
-        if teacher is not None:
-            other = teacher[at : at + row_block, :].astype(F32)
-            terms = jnp.exp(other - top[at : at + row_block])
-            found[2].append(lane_sums(terms * (other - part)))
     for k, part in enumerate(found):
-        if part:
-            stats[k : k + 1, :] = as_row(jnp.concatenate(part, axis=0))
-
-
-def student_body(block, group, where, *refs):
-    slices, weights, (teacher, teacher_stats, total, stats) = refs[:8], refs[8:12], refs[12:]
-    q, c = where[2], where[4]
-    width = slices[0].shape[1]
+        stats[k : k + 1, :] = as_row(jnp.concatenate(part, axis=0))
+
+
+LOWEST = -3.0e38
+
+
+def student_body(where, *refs):
+    slices, weights, refs = refs[:8], refs[8:12], refs[12:]
+    teacher, teacher_stats, total, stats, peaks, masses, crosses, tops = refs
+    c = where[4]
+    rows, width = slices[0].shape
     step = pl.program_id(0)
-    value = None
-    for k in range(4):
-        for side in (0, 1):
-            at = pl.multiple_of((c if side == 0 else 1 - c) * width, width)
-            got = jnp.dot(
-                slices[2 * k + side][...],
-                weights[k][pl.ds(at, width), :],
-                preferred_element_type=F32,
-            )
-            value = got if value is None else value + got
-    total[:, pl.ds(pl.multiple_of(step * block, block), block)] = value
+
+    @pl.when(step == 0)
+    def _():
+        tops[...] = jnp.transpose(jnp.broadcast_to(teacher_stats[0:1, :], (128, rows)))
+        peaks[...] = jnp.full(peaks.shape, LOWEST, F32)
+        masses[...] = jnp.zeros(masses.shape, F32)
+        crosses[...] = jnp.zeros(crosses.shape, F32)
+
+    for begin in range(0, total.shape[1], 256):
+        value = None
+        for k in range(4):
+            for side in (0, 1):
+                at = pl.multiple_of((c if side == 0 else 1 - c) * width, width)
+                got = jnp.dot(
+                    slices[2 * k + side][...],
+                    weights[k][pl.ds(at, width), begin : begin + 256],
+                    preferred_element_type=F32,
+                )
+                value = got if value is None else value + got
+        total[:, begin : begin + 256] = value
+        for row in range(0, rows, 64):
+            at = slice(row, row + 64)
+            parts = [value[at, k : k + 128] for k in (0, 128)]
+            old = peaks[at, :]
+            new = jnp.maximum(jnp.maximum(old, parts[0]), parts[1])
+            mass = masses[at, :] * jnp.exp(old - new)
+            cross = crosses[at, :]
+            for k, part in enumerate(parts):
+                mass = mass + jnp.exp(part - new)
+                t = teacher[at, begin + 128 * k : begin + 128 * k + 128].astype(F32)
+                cross = cross + jnp.exp(t - tops[at, :]) * (t - part)
+            peaks[at, :] = new
+            masses[at, :] = mass
+            crosses[at, :] = cross
 
     @pl.when(step == pl.num_programs(0) - 1)
     def _():
-        if group == 0:
-            top = teacher_stats[0:1, :]
-        else:
-            half = teacher_stats.shape[0] // 2
-            every = teacher_stats[pl.ds((1 - q) * half, half), :, :]
-            top = jnp.max(every[:, 0], axis=0, keepdims=True)
-        totals(stats, total, teacher, as_column(top))
-
-
-def student_part(where, pairs, weight, teacher, teacher_stats, group, block=256):
+        peak = jnp.max(peaks[...], axis=1, keepdims=True)
+        mass = jnp.sum(masses[...] * jnp.exp(peaks[...] - peak), axis=1, keepdims=True)
+        cross = jnp.sum(crosses[...], axis=1, keepdims=True)
+        for k, column in enumerate((peak, mass, cross)):
+            stats[k : k + 1, :] = as_row(column)
+
+
+def student_part(where, pairs, weight, teacher, teacher_stats, group, block=512):
     rows, width = pairs[0][0].shape
     columns = weight.shape[1] // 2
     steps = columns // block
@@ -142,20 +160,31 @@
                 lambda j, at, by=by: (lax.rem(at[3] + by, 4), at[2] * steps + j),
             )
         )
+    tile = pl.BlockSpec((rows, block), lambda j, at: (0, j))
+    kept = pl.BlockSpec((rows, block), lambda j, at: (0, at[2] * steps + j))
     return call(
-        functools.partial(student_body, block, group),
+        student_body,
         where,
         [*(array for pair in pairs for array in pair), *[weight] * 4, teacher, teacher_stats],
-        in_specs + [whole((rows, columns)), whole(teacher_stats.shape)],
+        in_specs + [kept if group == 0 else tile, whole(teacher_stats.shape)],
         [jax.ShapeDtypeStruct((rows, columns), F32), jax.ShapeDtypeStruct((3, rows), F32)],
-        [whole((rows, columns)), whole((3, rows))],
+        [tile, whole((3, rows))],
         (steps,),
+        [pltpu.VMEM((rows, 128), F32)] * 4,
         micros=8,
         vmem=28,
-    )
-
-
-def teacher_body(where, teacher, stats):
+        loose=(12,) if group else (),
+    )
+
+
+def teacher_body(where, teacher, stats, leaving):
+    half = leaving.shape[1]
+    for side in (0, 1):
+
+        @pl.when(where[2] == side)
+        def _(side=side):
+            leaving[...] = teacher[:, (1 - side) * half : (2 - side) * half]
+
     totals(stats, teacher)
 
 
@@ -178,17 +207,18 @@
                     outs[side][to, width : 2 * width] = jnp.where(c == 0, other, mine)
 
 
-def merged(parts):
-    top = jnp.max(parts[0][:, 0], axis=0, keepdims=True)
-    for part in parts[1:]:
-        top = jnp.maximum(top, jnp.max(part[:, 0], axis=0, keepdims=True))
+def merged(peaks, sums):
+    top = jnp.max(peaks[0], axis=0, keepdims=True)
+    for peak in peaks[1:]:
+        top = jnp.maximum(top, jnp.max(peak, axis=0, keepdims=True))
     total = sum(
-        jnp.sum(part[:, 1] * jnp.exp(part[:, 0] - top), axis=0, keepdims=True) for part in parts
+        jnp.sum(part * jnp.exp(peak - top), axis=0, keepdims=True)
+        for peak, part in zip(peaks, sums)
     )
     return top, total
 
 
-def grad_body(first, where, s_own, s_other, t_own, t_other, every_s, every_t, out, *refs):
+def grad_body(first, where, s_own, s_other, t_own, t_other, every, out, *refs):
     if first:
         scales = refs
     else:
@@ -197,23 +227,24 @@
     step = pl.program_id(0)
     steps = pl.num_programs(0)
     block = s_own.shape[0]
-    rows = every_t.shape[2]
-    half = every_s.shape[0] // 2
+    rows = every.shape[2] // 2
+    half = every.shape[0] // 2
 
     @pl.when(step == 0)
     def _():
         for group in range(2):
             at = slice(group * rows, (group + 1) * rows)
             to = slice((1 - group) * rows, (2 - group) * rows)
-            mine = every_s[pl.ds(q * half, half), :, at]
-            other = every_s[pl.ds((1 - q) * half, half), :, to]
-            s_top, s_total = merged((mine, other))
+            mine = every[pl.ds(q * half, half), :, at]
+            other = every[pl.ds((1 - q) * half, half), :, to]
+            s_top, s_total = merged((mine[:, 0], other[:, 0]), (mine[:, 1], other[:, 1]))
             source = q if group == 0 else 1 - q
-            every = every_t[pl.ds(source * half, half), :, :]
-            t_top, t_total = merged((every,))
+            teacher = every[pl.ds(source * half, half), :, :][:, 3]
+            t_peaks = teacher[:, :rows]
+            t_top, t_total = merged((t_peaks,), (teacher[:, rows:],))
             if group == 0 and not first:
-                cross = jnp.sum(mine[:, 2] * jnp.exp(every[:, 0] - t_top), axis=0, keepdims=True)
-                cross = cross + jnp.sum(other[:, 2], axis=0, keepdims=True)
+                cross = (mine[:, 2] + other[:, 2]) * jnp.exp(t_peaks - t_top)
+                cross = jnp.sum(cross, axis=0, keepdims=True)
                 for k, row in enumerate((s_top, s_total, t_top, t_total, cross)):
                     tops[k : k + 1, :] = row
             wanted = (s_top, grad_scale / s_total, t_top, grad_scale / t_total)
@@ -239,11 +270,15 @@
         rows_of(s_other, t_other)
 
 
-def grad_part(where, values, every_s, every_t, count, first, block=256):
+def grad_part(where, values, every, count, first, block=256):
     rows, half = values[0].shape
     steps = 2 * rows // block
     place = 0 if first else half // count - 1
     early = pl.BlockSpec((block, count), lambda j, at: (jnp.minimum(j, steps // 2 - 1), place))
+    kept = pl.BlockSpec(
+        (block, count),
+        lambda j, at: (jnp.minimum(j, steps // 2 - 1), at[2] * (half // count) + place),
+    )
     late = pl.BlockSpec((block, count), lambda j, at: (jnp.maximum(j - steps // 2, 0), place))
     shapes = [jax.ShapeDtypeStruct((2 * rows, count), BF)]
     specs = [pl.BlockSpec((block, count), lambda j, at: (j, 0))]
@@ -253,13 +288,14 @@
     return call(
         functools.partial(grad_body, first),
         where,
-        [*values, every_s, every_t],
-        [early, late, early, late, whole(every_s.shape), whole(every_t.shape)],
+        [*values, every],
+        [early, late, kept, late, whole(every.shape)],
         shapes,
         specs,
         (steps,),
         [pltpu.VMEM((2 * rows, 128), F32)] * 4,
         micros=4,
+        loose=(3,),
     )
 
 
@@ -316,16 +352,33 @@
     )
 
 
-def final_body(where, *refs):
+def final_body(where, piece, *refs):
     out = refs[-1]
-    half = out.shape[1] // 2
-    begin = 0
-    for piece in refs[:-1]:
-        chunk = piece.shape[2]
-        for side in (0, 1):
-            at = side * half + begin
-            out[:, at : at + chunk] = sum(piece[2 * p + side].astype(F32) for p in range(4))
-        begin += chunk
+    side = pl.program_id(0)
+    for s in (0, 1):
+
+        @pl.when(side == s)
+        def _(s=s):
+            out[...] = sum(piece[2 * p + s].astype(F32) for p in range(4))
+
+
+def final_part(where, piece, columns, place, before=None):
+    _, rows, chunk = piece.shape
+    n = columns // 2 // chunk
+    shape = jax.ShapeDtypeStruct((rows, columns), F32)
+    return pl.pallas_call(
+        final_body,
+        out_shape=shape,
+        grid_spec=pltpu.PrefetchScalarGridSpec(
+            num_scalar_prefetch=1,
+            grid=(2,),
+            in_specs=[whole(piece.shape)]
+            + ([] if before is None else [pl.BlockSpec(memory_space=pl.ANY)]),
+            out_specs=pl.BlockSpec((rows, chunk), lambda j, at: (0, j * n + place)),
+        ),
+        input_output_aliases={} if before is None else {2: 0},
+        cost_estimate=pl.CostEstimate(flops=2**29, bytes_accessed=2**20, transcendentals=0),
+    )(where, pltpu.with_memory_space_constraint(piece, pltpu.HBM), *([before] if place else []))
 
 
 def per_device(hidden_states, teacher_logits, head_weight):
@@ -333,21 +386,18 @@
     _, columns = head_weight.shape
     half = columns // 2
     where = jnp.stack([lax.axis_index(name) for name in (*DP, *VOCAB)]).astype(jnp.int32)
-    q = lax.axis_index("q")
 
     other_hidden = swapped(hidden_states, "q")
-    (teacher_stats,) = call(
+    teacher_stats, sent_teacher = call(
         teacher_body,
         where,
         [teacher_logits],
         [whole(teacher_logits.shape)],
-        [jax.ShapeDtypeStruct((2, rows), F32)],
-        [whole((2, rows))],
+        [jax.ShapeDtypeStruct((2, rows), F32), jax.ShapeDtypeStruct((rows, half), BF)],
+        [whole((2, rows)), whole((rows, half))],
         micros=5,
     )
-    every_teacher = sent_to_all(teacher_stats, WHOLE_VOCAB)
-    kept_teacher = lax.dynamic_slice_in_dim(teacher_logits, q * half, half, 1)
-    sent_teacher = lax.dynamic_slice_in_dim(teacher_logits, (1 - q) * half, half, 1)
+    partner_stats = swapped(teacher_stats, "q")
     arrived_teacher = swapped(sent_teacher, "q")
     gathered = []
     for piece in (hidden_states, other_hidden):
@@ -358,12 +408,16 @@
         gathered.append(pairs)
 
     student_own, stats_own = student_part(
-        where, gathered[0], head_weight, kept_teacher, teacher_stats, 0
+        where, gathered[0], head_weight, teacher_logits, teacher_stats, 0
     )
     student_other, stats_other = student_part(
-        where, gathered[1], head_weight, arrived_teacher, every_teacher, 1
-    )
-    every_student = sent_to_all(jnp.concatenate([stats_own, stats_other], axis=1), WHOLE_VOCAB)
+        where, gathered[1], head_weight, arrived_teacher, partner_stats, 1
+    )
+    local = jnp.concatenate(
+        [jnp.concatenate([stats_own, stats_other], axis=1), teacher_stats.reshape(1, 2 * rows)],
+        axis=0,
+    )
+    every = sent_to_all(local, WHOLE_VOCAB)
     flat = [array for pairs in gathered for pair in pairs for array in pair]
     blocks = call(
         arrange_body,
@@ -374,8 +428,8 @@
         [whole((2 * rows, 2 * width))] * 4,
         micros=5,
     )
-    values = (student_own, student_other, kept_teacher, arrived_teacher)
-    (grad_first,) = grad_part(where, values, every_student, every_teacher, CHUNKS[0], True)
+    values = (student_own, student_other, teacher_logits, arrived_teacher)
+    (grad_first,) = grad_part(where, values, every, CHUNKS[0], True)
 
     pieces = []
     begin = -CHUNKS[0]
@@ -395,7 +449,7 @@
         if k == 0:
             later = tuple(after(value, part) for value in values)
             grad_last, tops = grad_part(
-                where, later, every_student, every_teacher, half - CHUNKS[0], False
+                where, later, every, half - CHUNKS[0], False
             )
             leaving = hidden_part(where, (grad_first, grad_last), head_weight, 0, 2 * rows)
             across_core = swapped(leaving, "c")
@@ -418,17 +472,14 @@
                 )
                 gate = value[0]
                 moved = [sent(value[d], "x", d) for d in (2, 1, 3)]
-                reduced[group] = value[0].astype(F32) + sum(part.astype(F32) for part in moved)
-    head_grad = call(
-        final_body,
-        where,
-        pieces,
-        [whole(piece.shape) for piece in pieces],
-        jax.ShapeDtypeStruct((pieces[0].shape[1], columns), F32),
-        whole((pieces[0].shape[1], columns)),
-    )
-    partner = swapped(reduced[1].astype(BF), "q")
-    hidden_grad = (reduced[0] + partner.astype(F32)).astype(BF)
+                reduced[group] = [value[0], *moved]
+    head_grad = None
+    for k, piece in enumerate(pieces):
+        head_grad = final_part(where, piece, columns, k, head_grad)
+    leaving = sum(part.astype(F32) for part in reduced[1]).astype(BF)
+    partner = swapped(leaving, "q")
+    staying = sum(part.astype(F32) for part in reduced[0])
+    hidden_grad = (staying + after(partner, head_grad).astype(F32)).astype(BF)
 
     student_max, student_total, teacher_max, teacher_total, cross_term = tops
     divergence = (

time: 211 us -> 221 us (1.047)
  starting transfers between devices: 54.7 us -> 60.1 us
  waiting for transfers between devices: 81.8 us -> 86.3 us
  Pallas kernels: 54.1 us -> 51 us
  local copies, waits for them, and re-layouts: 6.79 us -> 9.32 us
    ppermute x12 -> x13, waiting for transfers between devices: 17.8 us -> 27.6 us  [swapped(): return lax.ppermute(array, axis, SWAP)]
    pallas_call x10 -> x9, Pallas kernels: 54.1 us -> 46 us  [call(): pl.pallas_call(body, cost_estimate=cost, out_shape=out_shapes, grid_spec=...]
    ppermute x18, starting transfers between devices: 17.4 us -> 23.9 us  [sent(): lax.ppermute(array, axis, [(k, (k + by) % size) for k in range(size)])]
    unnamed x24 -> x57, local copies, waits for them, and re-layouts: 2.19 us -> 8.48 us
    all_to_all x2 -> x1, starting transfers between devices: 10.1 us -> 5 us  [sent_to_all(): return lax.all_to_all(copies, axis, 0, 0, tiled=True)]
    pallas_call x0 -> x2, Pallas kernels: none -> 4.95 us  [final_part(): pl.pallas_call(final_body, out_shape=shape, grid_spec=pltpu.PrefetchScala...]
    ppermute x12 -> x13, starting transfers between devices: 13.5 us -> 16.8 us  [swapped(): return lax.ppermute(array, axis, SWAP)]
    ppermute x18, waiting for transfers between devices: 61.9 us -> 58.8 us  [sent(): lax.ppermute(array, axis, [(k, (k + by) % size) for k in range(size)])]
  transfers between devices with their start and end apart: 34 -> 34, of which waited for: 13 -> 9; matrix products, arithmetic and copies ran while one was open for 6% -> 4% of each run, Pallas kernels for 19% -> 18%
where the time goes in v3:
time: 221 us; the launch traced here: 219 us
  waiting for transfers between devices  86.3 us (39%)
  starting transfers between devices  60.1 us (27%)
  Pallas kernels  51 us (23%)
  matrix products  10.2 us (5%)
  local copies, waits for them, and re-layouts  9.32 us (4%)
    ppermute x18, waiting for transfers between devices, sent(): lax.ppermute(array, axis, [(k, (k + by) % size) for k in range(size)])  58.8 us
    pallas_call x9, Pallas kernels, call(): pl.pallas_call(body, cost_estimate=cost, out_shape=out_shapes, grid_spec=...  46 us
    ppermute x13, waiting for transfers between devices, swapped(): return lax.ppermute(array, axis, SWAP)  27.6 us
    ppermute x18, starting transfers between devices, sent(): lax.ppermute(array, axis, [(k, (k + by) % size) for k in range(size)])  23.9 us
    ppermute x13, starting transfers between devices, swapped(): return lax.ppermute(array, axis, SWAP)  16.8 us
    all_to_all x2, starting transfers between devices, per_device(): pieces.append(lax.all_to_all(total, ('p', 'q'), 0, 0, tiled=True))  14.4 us
    unnamed x57, local copies, waits for them, and re-layouts  8.48 us
    dot_general x6, matrix products, per_device(): lax.dot_general(blocks[d], grads, (((0,), (0,)), ((), ())), preferred_ele...  7.08 us
  transfers between devices with their start and end apart: 34, of which 9 were waited for; matrix products, arithmetic and copies ran while one was open for 4% of the time, Pallas kernels for 18%

profile of v3, /device:TPU:1, one launch (start us, length us, event | category | flops | bytes accessed | tf_op | source)
XLA Modules:
  0.0 219.3 jit_solution(4174163326271975622)
XLA Ops:
  0.6 2.1 collective-permute-start.5
  2.7 2.5 %collective-permute-start.3 = (bf16[512,256]{1,0:T(8,128)(2,1)}, bf16[512,256]{1,0:T(8,128)(2,1)S(1)}, u32[]{:S(2)}, u32[]{:S(2)}) collective-permute-start(bf16[512,256]{1,0:T(8,128)(2,1)} %refs_0_.6), channel_id=1, source_target_pairs={{0,4},{2,6},{4,0},{6,2},{1,5},{3,7},{5,1},{7,3},{8,12},{10,14},{12... | collective-permute-start | bytes 786440 | tf_op jit(solution)/shard_map/ppermute | solution.py:26
  5.2 1.2 collective-permute-start.1
  6.4 3.4 %shard_map.58 = (f32[2,512]{1,0:T(2,128)S(1)}, bf16[512,1024]{1,0:T(8,128)(2,1)}) custom-call(s32[5]{0:T(128)S(1)} %stack.23.where, bf16[512,2048]{1,0:T(8,128)(2,1)} %t_own.2), custom_call_target="tpu_custom_call" | custom-call | flops 2249999872 | bytes 1048576 | tf_op jit(solution)/shard_map/pallas_call | solution.py:57
  9.9 1.7 collective-permute-start.15
  11.7 22.1 %collective-permute-done.16.refs_13_ = f32[2,512]{1,0:T(2,128)S(1)} collective-permute-done((f32[2,512]{1,0:T(2,128)S(1)}, f32[2,512]{1,0:T(2,128)S(1)}, u32[]{:S(2)}, u32[]{:S(2)}) %collective-permute-start.16) | collective-permute-done | bytes 4128 | tf_op jit(solution)/shard_map/ppermute | solution.py:30
  33.8 2.2 %collective-permute-start = (bf16[512,256]{1,0:T(8,128)(2,1)S(1)}, bf16[512,256]{1,0:T(8,128)(2,1)S(1)}, u32[]{:S(2)}, u32[]{:S(2)}) collective-permute-start(bf16[512,256]{1,0:T(8,128)(2,1)S(1)} %copy-done), channel_id=1, source_target_pairs={{0,1},{1,0},{2,3},{3,2},{4,5},{5,4},{6,7},{7,6},{8,9},{9,8},{10,11... | collective-permute-start | bytes 786440 | tf_op jit(solution)/shard_map/ppermute | solution.py:30
  36.0 1.5 collective-permute-start.7
  38.4 5.4 %collective-permute-done.7.refs_8_.refs_0_ = bf16[512,256]{1,0:T(8,128)(2,1)S(1)} collective-permute-done((bf16[512,256]{1,0:T(8,128)(2,1)S(1)}, bf16[512,256]{1,0:T(8,128)(2,1)S(1)}, u32[]{:S(2)}, u32[]{:S(2)}) %collective-permute-start.7) | collective-permute-done | bytes 262176 | tf_op jit(solution)/shard_map/ppermute | solution.py:30
  45.0 1.6 collective-permute-start.9
  46.6 1.6 collective-permute-start.8
  48.2 5.2 %collective-permute-done.13.refs_14_.refs_6_ = bf16[512,256]{1,0:T(8,128)(2,1)S(1)} collective-permute-done((bf16[512,256]{1,0:T(8,128)(2,1)S(1)}, bf16[512,256]{1,0:T(8,128)(2,1)S(1)}, u32[]{:S(2)}, u32[]{:S(2)}) %collective-permute-start.13) | collective-permute-done | bytes 262176 | tf_op jit(solution)/shard_map/ppermute | solution.py:26
  53.3 6.0 %collective-permute-start.14 = (bf16[512,256]{1,0:T(8,128)(2,1)S(1)}, bf16[512,256]{1,0:T(8,128)(2,1)S(1)}, u32[]{:S(2)}, u32[]{:S(2)}) collective-permute-start(bf16[512,256]{1,0:T(8,128)(2,1)S(1)} %collective-permute-done.13.refs_14_.refs_6_), channel_id=1, source_target_pairs={{0,1},{1,0},{2,3},{3,2},{4,5},{5,4},{6,7},{7,6},{8,9},{9,8},{10,11... | collective-permute-start | bytes 786440 | tf_op jit(solution)/shard_map/ppermute | solution.py:30
  60.0 7.2 %shard_map.59 = (f32[512,1024]{1,0:T(8,128)}, f32[3,512]{1,0:T(4,128)S(1)}) custom-call(s32[5]{0:T(128)S(1)} %stack.23.where, bf16[512,256]{1,0:T(8,128)(2,1)S(1)} %copy-done, bf16[512,256]{1,0:T(8,128)(2,1)S(1)} %collective-permute-done.refs_1_, bf16[512,256]{1,0:T(8,128)(2,1)S(1)} %collective-permute-done.1.refs_2_, ...), custom_call_target="tpu_custom_call" | custom-call | flops 3600000000 | bytes 1048576 | tf_op jit(solution)/shard_map/pallas_call | solution.py:57
  67.2 7.0 %shard_map.61 = (f32[512,1024]{1,0:T(8,128)}, f32[3,512]{1,0:T(4,128)S(1)}) custom-call(s32[5]{0:T(128)S(1)} %stack.23.where, bf16[512,256]{1,0:T(8,128)(2,1)S(1)} %collective-permute-done.7.refs_8_.refs_0_, bf16[512,256]{1,0:T(8,128)(2,1)S(1)} %collective-permute-done.8.refs_9_.refs_1_, bf16[512,256]{1,0:T(8,128)(2,1)S(1)} %collective-permute-done.9.refs_10_.refs_2_, ...), custom_call_target="tpu_custom_call" | custom-call | flops 3600000000 | bytes 1048576 | tf_op jit(solution)/shard_map/pallas_call | solution.py:57
  75.0 5.0 %all-to-all-start = ((f32[16,4,1024]{2,1,0:T(4,128)}), f32[16,4,1024]{2,1,0:T(4,128)S(1)}, u32[]{:S(2)}, u32[]{:S(2)}) async-start(f32[16,4,1024]{2,1,0:T(4,128)} %broadcast_in_dim.3), calls=%async_computation | async-start | bytes 524288 | tf_op jit(solution)/shard_map/all_to_all | solution.py:35
  81.0 0.9 copy-done.4
  81.9 0.9 copy-done.6
  82.9 0.9 copy-done.8
  83.8 0.9 copy-done.10
  84.8 0.9 copy-done.12
  86.7 0.9 copy-done.16
  87.6 2.9 %shard_map.60 = (bf16[1024,512]{1,0:T(8,128)(2,1)}, bf16[1024,512]{1,0:T(8,128)(2,1)}, bf16[1024,512]{1,0:T(8,128)(2,1)}, bf16[1024,512]{1,0:T(8,128)(2,1)}) custom-call(s32[5]{0:T(128)S(1)} %stack.23.where, bf16[512,256]{1,0:T(8,128)(2,1)S(1)} %copy-done, bf16[512,256]{1,0:T(8,128)(2,1)S(1)} %collective-permute-done.refs_1_, ...), custom_call_target="tpu_custom_call" | custom-call | flops 2249999872 | bytes 1048576 | tf_op jit(solution)/shard_map/pallas_call | solution.py:57
  90.6 5.4 %shard_map.62.first = bf16[1024,512]{1,0:T(8,128)(2,1)} custom-call(s32[5]{0:T(128)S(1)} %stack.23.where, f32[512,1024]{1,0:T(8,128)} %get-tuple-element.38.s_own, f32[512,1024]{1,0:T(8,128)} %get-tuple-element.39.s_other, bf16[512,2048]{1,0:T(8,128)(2,1)} %t_own.2, bf16[512,1024]{1,0:T(8,128)(2,1)S(1)} %collective-permute-done.15.refs_12_.t_other, ...), custom_call_target="tpu_custom_call" | custom-call | flops 1800000000 | bytes 1048576 | tf_op jit(solution)/shard_map/pallas_call | solution.py:57
  96.0 2.1 convolution_convert_fusion.5
  98.1 2.8 %collective-permute-start.19 = (bf16[512,512]{1,0:T(8,128)(2,1)S(1)}, bf16[512,512]{1,0:T(8,128)(2,1)S(1)}, u32[]{:S(2)}, u32[]{:S(2)}) collective-permute-start(bf16[512,512]{1,0:T(8,128)(2,1)S(1)} %convolution_convert_fusion.5), channel_id=1, source_target_pairs={{0,192},{64,0},{128,64},{192,128},{1,193},{65,1},{129,65},{193,129... | collective-permute-start | bytes 1572872 | tf_op jit(solution)/shard_map/ppermute | solution.py:26
  101.6 5.4 %shard_map.63 = (bf16[1024,512]{1,0:T(8,128)(2,1)}, f32[5,512]{1,0:T(8,128)S(1)}) custom-call(s32[5]{0:T(128)S(1)} %stack.23.where, f32[512,1024]{1,0:T(8,128)} %get-tuple-element.38.s_own, f32[512,1024]{1,0:T(8,128)} %get-tuple-element.39.s_other, bf16[512,2048]{1,0:T(8,128)(2,1)} %t_own.2, bf16[512,1024]{1,0:T(8,128)(2,1)S(1)} %collective-permute-done.15.refs_12_.t_other, ...), custom_call_target="tpu_custom_call" | custom-call | flops 1800000000 | bytes 1048576 | tf_op jit(solution)/shard_map/pallas_call | solution.py:57
  107.0 6.7 %shard_map.64 = bf16[4,1024,256]{2,1,0:T(8,128)(2,1)} custom-call(s32[5]{0:T(128)S(1)} %stack.23.where, bf16[1024,512]{1,0:T(8,128)(2,1)} %shard_map.62.first, bf16[1024,512]{1,0:T(8,128)(2,1)} %get-tuple-element.49.last, bf16[2048,2048]{1,0:T(8,128)(2,1)} %refs_3_.5, bf16[2048,2048]{1,0:T(8,128)(2,1)} %refs_3_.5, bf16[2048,2048]{1,0:T(8,128)(2,1)} %refs_3_.5, ...), custom_call_target="tpu_custom_call" | custom-call | flops 2700000000 | bytes 1048576 | tf_op jit(solution)/shard_map/pallas_call | solution.py:57
  117.4 12.4 %collective-permute-done.17 = bf16[512,512]{1,0:T(8,128)(2,1)S(1)} collective-permute-done((bf16[512,512]{1,0:T(8,128)(2,1)S(1)}, bf16[512,512]{1,0:T(8,128)(2,1)S(1)}, u32[]{:S(2)}, u32[]{:S(2)}) %collective-permute-start.17) | collective-permute-done | bytes 524320 | tf_op jit(solution)/shard_map/ppermute | solution.py:26
  129.8 11.7 %collective-permute-done.18 = bf16[512,512]{1,0:T(8,128)(2,1)S(1)} collective-permute-done((bf16[512,512]{1,0:T(8,128)(2,1)S(1)}, bf16[512,512]{1,0:T(8,128)(2,1)S(1)}, u32[]{:S(2)}, u32[]{:S(2)}) %collective-permute-start.18) | collective-permute-done | bytes 524320 | tf_op jit(solution)/shard_map/ppermute | solution.py:26
  141.5 1.6 fusion
  143.0 7.8 %all-to-all-start.2 = ((bf16[8,64,512]{2,1,0:T(8,128)(2,1)}), bf16[8,64,512]{2,1,0:T(8,128)(2,1)S(1)}, u32[]{:S(2)}, u32[]{:S(2)}) async-start(bf16[8,64,512]{2,1,0:T(8,128)(2,1)} %bitcast.6), calls=%async_computation.2 | async-start | bytes 1048576 | tf_op jit(solution)/shard_map/all_to_all | solution.py:465
  150.8 2.0 convolution_convert_fusion.2
  153.4 2.6 %collective-permute-start.30 = (bf16[512,512]{1,0:T(8,128)(2,1)S(1)}, bf16[512,512]{1,0:T(8,128)(2,1)S(1)}, u32[]{:S(2)}, u32[]{:S(2)}) collective-permute-start(bf16[512,512]{1,0:T(8,128)(2,1)S(1)} %convolution_convert_fusion), channel_id=1, source_target_pairs={{0,192},{64,0},{128,64},{192,128},{1,193},{65,1},{129,65},{193,129... | collective-permute-start | bytes 1572872 | tf_op jit(solution)/shard_map/ppermute | solution.py:26
  156.0 11.2 %collective-permute-done.28 = bf16[512,512]{1,0:T(8,128)(2,1)S(1)} collective-permute-done((bf16[512,512]{1,0:T(8,128)(2,1)S(1)}, bf16[512,512]{1,0:T(8,128)(2,1)S(1)}, u32[]{:S(2)}, u32[]{:S(2)}) %collective-permute-start.28) | collective-permute-done | bytes 524320 | tf_op jit(solution)/shard_map/ppermute | solution.py:26
  167.2 12.3 %collective-permute-done.29 = bf16[512,512]{1,0:T(8,128)(2,1)S(1)} collective-permute-done((bf16[512,512]{1,0:T(8,128)(2,1)S(1)}, bf16[512,512]{1,0:T(8,128)(2,1)S(1)}, u32[]{:S(2)}, u32[]{:S(2)}) %collective-permute-start.29) | collective-permute-done | bytes 524320 | tf_op jit(solution)/shard_map/ppermute | solution.py:26
  179.5 1.5 fusion.1
  181.1 6.7 %all-to-all-start.1 = ((bf16[8,64,512]{2,1,0:T(8,128)(2,1)}), bf16[8,64,512]{2,1,0:T(8,128)(2,1)S(1)}, u32[]{:S(2)}, u32[]{:S(2)}) async-start(bf16[8,64,512]{2,1,0:T(8,128)(2,1)} %bitcast.7), calls=%async_computation.1 | async-start | bytes 1048576 | tf_op jit(solution)/shard_map/all_to_all | solution.py:465
  187.7 4.0 %shard_map.65 = (bf16[512,256]{1,0:T(8,128)(2,1)S(1)}, bf16[512,256]{1,0:T(8,128)(2,1)S(1)}, bf16[512,256]{1,0:T(8,128)(2,1)S(1)}, bf16[512,256]{1,0:T(8,128)(2,1)S(1)}) custom-call(s32[5]{0:T(128)S(1)} %stack.23.where, bf16[1024,512]{1,0:T(8,128)(2,1)} %shard_map.62.first, bf16[1024,512]{1,0:T(8,128)(2,1)} %get-tuple-element.49.last, ...), custom_call_target="tpu_custom_call" | custom-call | flops 2700000000 | bytes 1048576 | tf_op jit(solution)/shard_map/pallas_call | solution.py:57
  191.8 2.8 %collective-permute-start.24 = (bf16[512,256]{1,0:T(8,128)(2,1)S(1)}, bf16[512,256]{1,0:T(8,128)(2,1)S(1)}, u32[]{:S(2)}, u32[]{:S(2)}) collective-permute-start(bf16[512,256]{1,0:T(8,128)(2,1)S(1)} %get-tuple-element.54), channel_id=1, source_target_pairs={{0,4},{2,6},{4,0},{6,2},{1,5},{3,7},{5,1},{7,3},{8,12},{10,14},{12... | collective-permute-start | bytes 786440 | tf_op jit(solution)/shard_map/ppermute | solution.py:26
  194.9 2.4 %collective-permute-start.26 = (bf16[512,256]{1,0:T(8,128)(2,1)S(1)}, bf16[512,256]{1,0:T(8,128)(2,1)S(1)}, u32[]{:S(2)}, u32[]{:S(2)}) collective-permute-start(bf16[512,256]{1,0:T(8,128)(2,1)S(1)} %get-tuple-element.56), channel_id=1, source_target_pairs={{0,6},{2,0},{4,2},{6,4},{1,7},{3,1},{5,3},{7,5},{8,14},{10,8},{12,... | collective-permute-start | bytes 786440 | tf_op jit(solution)/shard_map/ppermute | solution.py:26
  197.3 4.0 %shard_map.66 = (bf16[512,256]{1,0:T(8,128)(2,1)S(1)}, bf16[512,256]{1,0:T(8,128)(2,1)S(1)}, bf16[512,256]{1,0:T(8,128)(2,1)S(1)}, bf16[512,256]{1,0:T(8,128)(2,1)S(1)}) custom-call(s32[5]{0:T(128)S(1)} %stack.23.where, bf16[1024,512]{1,0:T(8,128)(2,1)} %shard_map.62.first, bf16[1024,512]{1,0:T(8,128)(2,1)} %get-tuple-element.49.last, ...), custom_call_target="tpu_custom_call" | custom-call | flops 2700000000 | bytes 1048576 | tf_op jit(solution)/shard_map/pallas_call | solution.py:57
  202.0 2.2 collective-permute-start.23
  204.2 4.2 %collective-permute-done.25 = bf16[512,256]{1,0:T(8,128)(2,1)S(1)} collective-permute-done((bf16[512,256]{1,0:T(8,128)(2,1)S(1)}, bf16[512,256]{1,0:T(8,128)(2,1)S(1)}, u32[]{:S(2)}, u32[]{:S(2)}) %collective-permute-start.25) | collective-permute-done | bytes 262176 | tf_op jit(solution)/shard_map/ppermute | solution.py:26
  208.5 1.8 collective-permute-start.27
  210.9 2.5 %shard_map.67.refs_0_ = f32[64,2048]{1,0:T(8,128)} custom-call(s32[5]{0:T(128)} %copy-done.17, bf16[8,64,512]{2,1,0:T(8,128)(2,1)} %copy-done.21), custom_call_target="tpu_custom_call" | custom-call | flops 536870912 | bytes 1048576 | tf_op jit(solution)/shard_map/pallas_call | solution.py:369
  214.2 2.5 %shard_map.68 = f32[64,2048]{1,0:T(8,128)} custom-call(s32[5]{0:T(128)} %copy-done.17, bf16[8,64,512]{2,1,0:T(8,128)(2,1)} %copy-done.22, f32[64,2048]{1,0:T(8,128)} %shard_map.67.refs_0_), custom_call_target="tpu_custom_call", output_to_operand_aliasing={{}: (2, {})} | custom-call | flops 536870912 | bytes 1048576 | tf_op jit(solution)/shard_map/pallas_call | solution.py:369
  216.7 1.8 collective-permute-done.22
  (102 shorter events, 14.1 us)
Async XLA Ops:
  0.6 35.4 %collective-permute-start.5 = (bf16[512,256]{1,0:T(8,128)(2,1)}, bf16[512,256]{1,0:T(8,128)(2,1)S(1)}, u32[]{:S(2)}, u32[]{:S(2)}) collective-permute-start(bf16[512,256]{1,0:T(8,128)(2,1)} %refs_0_.6), channel_id=1, source_target_pairs={{0,2},{2,4},{4,6},{6,0},{1,3},{3,5},{5,7},{7,1},{8,10},{10,12},{12... | collective-permute-start | bytes 786440 | tf_op jit(solution)/shard_map/ppermute | solution.py:26
  2.7 34.7 %collective-permute-start.3 = (bf16[512,256]{1,0:T(8,128)(2,1)}, bf16[512,256]{1,0:T(8,128)(2,1)S(1)}, u32[]{:S(2)}, u32[]{:S(2)}) collective-permute-start(bf16[512,256]{1,0:T(8,128)(2,1)} %refs_0_.6), channel_id=1, source_target_pairs={{0,4},{2,6},{4,0},{6,2},{1,5},{3,7},{5,1},{7,3},{8,12},{10,14},{12... | collective-permute-start | bytes 786440 | tf_op jit(solution)/shard_map/ppermute | solution.py:26
  5.2 32.7 %collective-permute-start.1 = (bf16[512,256]{1,0:T(8,128)(2,1)}, bf16[512,256]{1,0:T(8,128)(2,1)S(1)}, u32[]{:S(2)}, u32[]{:S(2)}) collective-permute-start(bf16[512,256]{1,0:T(8,128)(2,1)} %refs_0_.6), channel_id=1, source_target_pairs={{0,6},{2,0},{4,2},{6,4},{1,7},{3,1},{5,3},{7,5},{8,14},{10,8},{12,... | collective-permute-start | bytes 786440 | tf_op jit(solution)/shard_map/ppermute | solution.py:26
  6.4 190.8 %copy-start.17 = (s32[5]{0:T(128)}, s32[5]{0:T(128)S(1)}, u32[]{:S(2)}) copy-start(s32[5]{0:T(128)S(1)} %stack.23.where) | copy-start | bytes 64
  6.4 27.4 %copy-start = (bf16[512,256]{1,0:T(8,128)(2,1)S(1)}, bf16[512,256]{1,0:T(8,128)(2,1)}, u32[]{:S(2)}) copy-start(bf16[512,256]{1,0:T(8,128)(2,1)} %refs_0_.6) | copy-start | bytes 786436
  9.9 57.3 %collective-permute-start.15 = (bf16[512,1024]{1,0:T(8,128)(2,1)}, bf16[512,1024]{1,0:T(8,128)(2,1)S(1)}, u32[]{:S(2)}, u32[]{:S(2)}) collective-permute-start(bf16[512,1024]{1,0:T(8,128)(2,1)} %get-tuple-element.34), channel_id=1, source_target_pairs={{0,8},{8,0},{1,9},{9,1},{2,10},{10,2},{3,11},{11,3},{4,12},{12,4},... | collective-permute-start | bytes 3145736 | tf_op jit(solution)/shard_map/ppermute | solution.py:30
  11.6 22.2 %collective-permute-start.16 = (f32[2,512]{1,0:T(2,128)S(1)}, f32[2,512]{1,0:T(2,128)S(1)}, u32[]{:S(2)}, u32[]{:S(2)}) collective-permute-start(f32[2,512]{1,0:T(2,128)S(1)} %get-tuple-element.31.refs_13_), channel_id=1, source_target_pairs={{0,8},{8,0},{1,9},{9,1},{2,10},{10,2},{3,11},{11,3},{4,12},{12,4},... | collective-permute-start | bytes 12296 | tf_op jit(solution)/shard_map/ppermute | solution.py:30
  33.8 4.2 %collective-permute-start = (bf16[512,256]{1,0:T(8,128)(2,1)S(1)}, bf16[512,256]{1,0:T(8,128)(2,1)S(1)}, u32[]{:S(2)}, u32[]{:S(2)}) collective-permute-start(bf16[512,256]{1,0:T(8,128)(2,1)S(1)} %copy-done), channel_id=1, source_target_pairs={{0,1},{1,0},{2,3},{3,2},{4,5},{5,4},{6,7},{7,6},{8,9},{9,8},{10,11... | collective-permute-start | bytes 786440 | tf_op jit(solution)/shard_map/ppermute | solution.py:30
  36.0 7.8 %collective-permute-start.7 = (bf16[512,256]{1,0:T(8,128)(2,1)S(1)}, bf16[512,256]{1,0:T(8,128)(2,1)S(1)}, u32[]{:S(2)}, u32[]{:S(2)}) collective-permute-start(bf16[512,256]{1,0:T(8,128)(2,1)S(1)} %copy-done), channel_id=1, source_target_pairs={{0,8},{8,0},{1,9},{9,1},{2,10},{10,2},{3,11},{11,3},{4,12},{12,4},... | collective-permute-start | bytes 786440 | tf_op jit(solution)/shard_map/ppermute | solution.py:30
  37.5 6.6 %collective-permute-start.6 = (bf16[512,256]{1,0:T(8,128)(2,1)S(1)}, bf16[512,256]{1,0:T(8,128)(2,1)S(1)}, u32[]{:S(2)}, u32[]{:S(2)}) collective-permute-start(bf16[512,256]{1,0:T(8,128)(2,1)S(1)} %collective-permute-done.5.refs_6_), channel_id=1, source_target_pairs={{0,1},{1,0},{2,3},{3,2},{4,5},{5,4},{6,7},{7,6},{8,9},{9,8},{10,11... | collective-permute-start | bytes 786440 | tf_op jit(solution)/shard_map/ppermute | solution.py:30
  37.8 7.1 %collective-permute-start.4 = (bf16[512,256]{1,0:T(8,128)(2,1)S(1)}, bf16[512,256]{1,0:T(8,128)(2,1)S(1)}, u32[]{:S(2)}, u32[]{:S(2)}) collective-permute-start(bf16[512,256]{1,0:T(8,128)(2,1)S(1)} %collective-permute-done.3.refs_4_), channel_id=1, source_target_pairs={{0,1},{1,0},{2,3},{3,2},{4,5},{5,4},{6,7},{7,6},{8,9},{9,8},{10,11... | collective-permute-start | bytes 786440 | tf_op jit(solution)/shard_map/ppermute | solution.py:30
  38.0 8.6 %collective-permute-start.2 = (bf16[512,256]{1,0:T(8,128)(2,1)S(1)}, bf16[512,256]{1,0:T(8,128)(2,1)S(1)}, u32[]{:S(2)}, u32[]{:S(2)}) collective-permute-start(bf16[512,256]{1,0:T(8,128)(2,1)S(1)} %collective-permute-done.1.refs_2_), channel_id=1, source_target_pairs={{0,1},{1,0},{2,3},{3,2},{4,5},{5,4},{6,7},{7,6},{8,9},{9,8},{10,11... | collective-permute-start | bytes 786440 | tf_op jit(solution)/shard_map/ppermute | solution.py:30
  43.8 9.5 %collective-permute-start.13 = (bf16[512,256]{1,0:T(8,128)(2,1)S(1)}, bf16[512,256]{1,0:T(8,128)(2,1)S(1)}, u32[]{:S(2)}, u32[]{:S(2)}) collective-permute-start(bf16[512,256]{1,0:T(8,128)(2,1)S(1)} %collective-permute-done.7.refs_8_.refs_0_), channel_id=1, source_target_pairs={{0,2},{2,4},{4,6},{6,0},{1,3},{3,5},{5,7},{7,1},{8,10},{10,12},{12... | collective-permute-start | bytes 786440 | tf_op jit(solution)/shard_map/ppermute | solution.py:26
  44.1 15.2 %collective-permute-start.11 = (bf16[512,256]{1,0:T(8,128)(2,1)S(1)}, bf16[512,256]{1,0:T(8,128)(2,1)S(1)}, u32[]{:S(2)}, u32[]{:S(2)}) collective-permute-start(bf16[512,256]{1,0:T(8,128)(2,1)S(1)} %collective-permute-done.7.refs_8_.refs_0_), channel_id=1, source_target_pairs={{0,4},{2,6},{4,0},{6,2},{1,5},{3,7},{5,1},{7,3},{8,12},{10,14},{12... | collective-permute-start | bytes 786440 | tf_op jit(solution)/shard_map/ppermute | solution.py:26
  45.0 14.5 %collective-permute-start.9 = (bf16[512,256]{1,0:T(8,128)(2,1)S(1)}, bf16[512,256]{1,0:T(8,128)(2,1)S(1)}, u32[]{:S(2)}, u32[]{:S(2)}) collective-permute-start(bf16[512,256]{1,0:T(8,128)(2,1)S(1)} %collective-permute-done.7.refs_8_.refs_0_), channel_id=1, source_target_pairs={{0,6},{2,0},{4,2},{6,4},{1,7},{3,1},{5,3},{7,5},{8,14},{10,8},{12,... | collective-permute-start | bytes 786440 | tf_op jit(solution)/shard_map/ppermute | solution.py:26
  46.6 20.6 %copy-start.1 = (bf16[512,256]{1,0:T(8,128)(2,1)}, bf16[512,256]{1,0:T(8,128)(2,1)S(1)}, u32[]{:S(2)}) copy-start(bf16[512,256]{1,0:T(8,128)(2,1)S(1)} %collective-permute-done.2.refs_3_) | copy-start | bytes 786436
  46.6 20.6 %collective-permute-start.8 = (bf16[512,256]{1,0:T(8,128)(2,1)S(1)}, bf16[512,256]{1,0:T(8,128)(2,1)S(1)}, u32[]{:S(2)}, u32[]{:S(2)}) collective-permute-start(bf16[512,256]{1,0:T(8,128)(2,1)S(1)} %collective-permute-done.7.refs_8_.refs_0_), channel_id=1, source_target_pairs={{0,1},{1,0},{2,3},{3,2},{4,5},{5,4},{6,7},{7,6},{8,9},{9,8},{10,11... | collective-permute-start | bytes 786440 | tf_op jit(solution)/shard_map/ppermute | solution.py:30
  53.3 13.9 %copy-start.3 = (bf16[512,256]{1,0:T(8,128)(2,1)}, bf16[512,256]{1,0:T(8,128)(2,1)S(1)}, u32[]{:S(2)}) copy-start(bf16[512,256]{1,0:T(8,128)(2,1)S(1)} %collective-permute-done.13.refs_14_.refs_6_) | copy-start | bytes 786436
  53.3 13.8 %collective-permute-start.14 = (bf16[512,256]{1,0:T(8,128)(2,1)S(1)}, bf16[512,256]{1,0:T(8,128)(2,1)S(1)}, u32[]{:S(2)}, u32[]{:S(2)}) collective-permute-start(bf16[512,256]{1,0:T(8,128)(2,1)S(1)} %collective-permute-done.13.refs_14_.refs_6_), channel_id=1, source_target_pairs={{0,1},{1,0},{2,3},{3,2},{4,5},{5,4},{6,7},{7,6},{8,9},{9,8},{10,11... | collective-permute-start | bytes 786440 | tf_op jit(solution)/shard_map/ppermute | solution.py:30
  59.3 7.9 %copy-start.5 = (bf16[512,256]{1,0:T(8,128)(2,1)}, bf16[512,256]{1,0:T(8,128)(2,1)S(1)}, u32[]{:S(2)}) copy-start(bf16[512,256]{1,0:T(8,128)(2,1)S(1)} %collective-permute-done.11.refs_12_.refs_4_) | copy-start | bytes 786436
  59.3 7.8 %collective-permute-start.12 = (bf16[512,256]{1,0:T(8,128)(2,1)S(1)}, bf16[512,256]{1,0:T(8,128)(2,1)S(1)}, u32[]{:S(2)}, u32[]{:S(2)}) collective-permute-start(bf16[512,256]{1,0:T(8,128)(2,1)S(1)} %collective-permute-done.11.refs_12_.refs_4_), channel_id=1, source_target_pairs={{0,1},{1,0},{2,3},{3,2},{4,5},{5,4},{6,7},{7,6},{8,9},{9,8},{10,11... | collective-permute-start | bytes 786440 | tf_op jit(solution)/shard_map/ppermute | solution.py:30
  59.4 7.8 %copy-start.7 = (bf16[512,256]{1,0:T(8,128)(2,1)}, bf16[512,256]{1,0:T(8,128)(2,1)S(1)}, u32[]{:S(2)}) copy-start(bf16[512,256]{1,0:T(8,128)(2,1)S(1)} %collective-permute-done.9.refs_10_.refs_2_) | copy-start | bytes 786436
  59.4 7.7 %collective-permute-start.10 = (bf16[512,256]{1,0:T(8,128)(2,1)S(1)}, bf16[512,256]{1,0:T(8,128)(2,1)S(1)}, u32[]{:S(2)}, u32[]{:S(2)}) collective-permute-start(bf16[512,256]{1,0:T(8,128)(2,1)S(1)} %collective-permute-done.9.refs_10_.refs_2_), channel_id=1, source_target_pairs={{0,1},{1,0},{2,3},{3,2},{4,5},{5,4},{6,7},{7,6},{8,9},{9,8},{10,11... | collective-permute-start | bytes 786440 | tf_op jit(solution)/shard_map/ppermute | solution.py:30
  67.1 7.1 %copy-start.9 = (bf16[512,256]{1,0:T(8,128)(2,1)}, bf16[512,256]{1,0:T(8,128)(2,1)S(1)}, u32[]{:S(2)}) copy-start(bf16[512,256]{1,0:T(8,128)(2,1)S(1)} %collective-permute-done.8.refs_9_.refs_1_) | copy-start | bytes 786436
  67.2 7.1 %copy-start.11 = (bf16[512,256]{1,0:T(8,128)(2,1)}, bf16[512,256]{1,0:T(8,128)(2,1)S(1)}, u32[]{:S(2)}) copy-start(bf16[512,256]{1,0:T(8,128)(2,1)S(1)} %collective-permute-done.14.refs_15_.refs_7_) | copy-start | bytes 786436
  67.2 7.1 %copy-start.13 = (bf16[512,256]{1,0:T(8,128)(2,1)}, bf16[512,256]{1,0:T(8,128)(2,1)S(1)}, u32[]{:S(2)}) copy-start(bf16[512,256]{1,0:T(8,128)(2,1)S(1)} %collective-permute-done.12.refs_13_.refs_5_) | copy-start | bytes 786436
  67.2 7.1 %copy-start.15 = (bf16[512,256]{1,0:T(8,128)(2,1)}, bf16[512,256]{1,0:T(8,128)(2,1)S(1)}, u32[]{:S(2)}) copy-start(bf16[512,256]{1,0:T(8,128)(2,1)S(1)} %collective-permute-done.10.refs_11_.refs_3_) | copy-start | bytes 786436
  75.0 15.6 %all-to-all-start = ((f32[16,4,1024]{2,1,0:T(4,128)}), f32[16,4,1024]{2,1,0:T(4,128)S(1)}, u32[]{:S(2)}, u32[]{:S(2)}) async-start(f32[16,4,1024]{2,1,0:T(4,128)} %broadcast_in_dim.3), calls=%async_computation | async-start | bytes 524288 | tf_op jit(solution)/shard_map/all_to_all | solution.py:35
  98.1 43.4 %collective-permute-start.19 = (bf16[512,512]{1,0:T(8,128)(2,1)S(1)}, bf16[512,512]{1,0:T(8,128)(2,1)S(1)}, u32[]{:S(2)}, u32[]{:S(2)}) collective-permute-start(bf16[512,512]{1,0:T(8,128)(2,1)S(1)} %convolution_convert_fusion.5), channel_id=1, source_target_pairs={{0,192},{64,0},{128,64},{192,128},{1,193},{65,1},{129,65},{193,129... | collective-permute-start | bytes 1572872 | tf_op jit(solution)/shard_map/ppermute | solution.py:26
  107.0 7.0 %copy-start.25 = (bf16[1024,512]{1,0:T(8,128)(2,1)S(1)}, bf16[1024,512]{1,0:T(8,128)(2,1)}, u32[]{:S(2)}) copy-start(bf16[1024,512]{1,0:T(8,128)(2,1)} %get-tuple-element.45) | copy-start | bytes 3145732
  113.7 74.1 %collective-permute-start.20 = (bf16[4,1024,256]{2,1,0:T(8,128)(2,1)}, bf16[4,1024,256]{2,1,0:T(8,128)(2,1)}, u32[]{:S(2)}, u32[]{:S(2)}) collective-permute-start(bf16[4,1024,256]{2,1,0:T(8,128)(2,1)} %shard_map.64), channel_id=1, source_target_pairs={{0,1},{1,0},{2,3},{3,2},{4,5},{5,4},{6,7},{7,6},{8,9},{9,8},{10,11... | collective-permute-start | bytes 6291464 | tf_op jit(solution)/shard_map/ppermute | solution.py:30
  114.8 15.0 %collective-permute-start.17 = (bf16[512,512]{1,0:T(8,128)(2,1)S(1)}, bf16[512,512]{1,0:T(8,128)(2,1)S(1)}, u32[]{:S(2)}, u32[]{:S(2)}) collective-permute-start(bf16[512,512]{1,0:T(8,128)(2,1)S(1)} %convolution_convert_fusion.4), channel_id=1, source_target_pairs={{0,128},{64,192},{128,0},{192,64},{1,129},{65,193},{129,1},{193,65... | collective-permute-start | bytes 1572872 | tf_op jit(solution)/shard_map/ppermute | solution.py:26
  115.3 26.2 %collective-permute-start.18 = (bf16[512,512]{1,0:T(8,128)(2,1)S(1)}, bf16[512,512]{1,0:T(8,128)(2,1)S(1)}, u32[]{:S(2)}, u32[]{:S(2)}) collective-permute-start(bf16[512,512]{1,0:T(8,128)(2,1)S(1)} %convolution_convert_fusion.3), channel_id=1, source_target_pairs={{0,64},{64,128},{128,192},{192,0},{1,65},{65,129},{129,193},{193,1... | collective-permute-start | bytes 1572872 | tf_op jit(solution)/shard_map/ppermute | solution.py:26
  116.7 24.8 %copy-start.23 = (bf16[1024,512]{1,0:T(8,128)(2,1)S(1)}, bf16[1024,512]{1,0:T(8,128)(2,1)}, u32[]{:S(2)}) copy-start(bf16[1024,512]{1,0:T(8,128)(2,1)} %get-tuple-element.44) | copy-start | bytes 3145732
  143.0 38.0 %all-to-all-start.2 = ((bf16[8,64,512]{2,1,0:T(8,128)(2,1)}), bf16[8,64,512]{2,1,0:T(8,128)(2,1)S(1)}, u32[]{:S(2)}, u32[]{:S(2)}) async-start(bf16[8,64,512]{2,1,0:T(8,128)(2,1)} %bitcast.6), calls=%async_computation.2 | async-start | bytes 1048576 | tf_op jit(solution)/shard_map/all_to_all | solution.py:465
  150.8 28.7 %copy-start.24 = (bf16[1024,512]{1,0:T(8,128)(2,1)S(1)}, bf16[1024,512]{1,0:T(8,128)(2,1)}, u32[]{:S(2)}) copy-start(bf16[1024,512]{1,0:T(8,128)(2,1)} %get-tuple-element.44) | copy-start | bytes 3145732
  152.9 14.4 %collective-permute-start.28 = (bf16[512,512]{1,0:T(8,128)(2,1)S(1)}, bf16[512,512]{1,0:T(8,128)(2,1)S(1)}, u32[]{:S(2)}, u32[]{:S(2)}) collective-permute-start(bf16[512,512]{1,0:T(8,128)(2,1)S(1)} %convolution_convert_fusion.2), channel_id=1, source_target_pairs={{0,128},{64,192},{128,0},{192,64},{1,129},{65,193},{129,1},{193,65... | collective-permute-start | bytes 1572872 | tf_op jit(solution)/shard_map/ppermute | solution.py:26
  153.3 26.2 %collective-permute-start.29 = (bf16[512,512]{1,0:T(8,128)(2,1)S(1)}, bf16[512,512]{1,0:T(8,128)(2,1)S(1)}, u32[]{:S(2)}, u32[]{:S(2)}) collective-permute-start(bf16[512,512]{1,0:T(8,128)(2,1)S(1)} %convolution_convert_fusion.1), channel_id=1, source_target_pairs={{0,64},{64,128},{128,192},{192,0},{1,65},{65,129},{129,193},{193,1... | collective-permute-start | bytes 1572872 | tf_op jit(solution)/shard_map/ppermute | solution.py:26
  153.4 26.1 %collective-permute-start.30 = (bf16[512,512]{1,0:T(8,128)(2,1)S(1)}, bf16[512,512]{1,0:T(8,128)(2,1)S(1)}, u32[]{:S(2)}, u32[]{:S(2)}) collective-permute-start(bf16[512,512]{1,0:T(8,128)(2,1)S(1)} %convolution_convert_fusion), channel_id=1, source_target_pairs={{0,192},{64,0},{128,64},{192,128},{1,193},{65,1},{129,65},{193,129... | collective-permute-start | bytes 1572872 | tf_op jit(solution)/shard_map/ppermute | solution.py:26
  181.1 10.7 %copy-start.21 = (bf16[8,64,512]{2,1,0:T(8,128)(2,1)}, bf16[8,64,512]{2,1,0:T(8,128)(2,1)S(1)}, u32[]{:S(2)}) copy-start(bf16[8,64,512]{2,1,0:T(8,128)(2,1)S(1)} %all-to-all-done.2.piece) | copy-start | bytes 1572868
  181.1 32.3 %all-to-all-start.1 = ((bf16[8,64,512]{2,1,0:T(8,128)(2,1)}), bf16[8,64,512]{2,1,0:T(8,128)(2,1)S(1)}, u32[]{:S(2)}, u32[]{:S(2)}) async-start(bf16[8,64,512]{2,1,0:T(8,128)(2,1)} %bitcast.7), calls=%async_computation.1 | async-start | bytes 1048576 | tf_op jit(solution)/shard_map/all_to_all | solution.py:465
  191.8 10.2 %collective-permute-start.24 = (bf16[512,256]{1,0:T(8,128)(2,1)S(1)}, bf16[512,256]{1,0:T(8,128)(2,1)S(1)}, u32[]{:S(2)}, u32[]{:S(2)}) collective-permute-start(bf16[512,256]{1,0:T(8,128)(2,1)S(1)} %get-tuple-element.54), channel_id=1, source_target_pairs={{0,4},{2,6},{4,0},{6,2},{1,5},{3,7},{5,1},{7,3},{8,12},{10,14},{12... | collective-permute-start | bytes 786440 | tf_op jit(solution)/shard_map/ppermute | solution.py:26
  194.6 13.7 %collective-permute-start.25 = (bf16[512,256]{1,0:T(8,128)(2,1)S(1)}, bf16[512,256]{1,0:T(8,128)(2,1)S(1)}, u32[]{:S(2)}, u32[]{:S(2)}) collective-permute-start(bf16[512,256]{1,0:T(8,128)(2,1)S(1)} %get-tuple-element.55), channel_id=1, source_target_pairs={{0,2},{2,4},{4,6},{6,0},{1,3},{3,5},{5,7},{7,1},{8,10},{10,12},{12... | collective-permute-start | bytes 786440 | tf_op jit(solution)/shard_map/ppermute | solution.py:26
  194.9 13.5 %collective-permute-start.26 = (bf16[512,256]{1,0:T(8,128)(2,1)S(1)}, bf16[512,256]{1,0:T(8,128)(2,1)S(1)}, u32[]{:S(2)}, u32[]{:S(2)}) collective-permute-start(bf16[512,256]{1,0:T(8,128)(2,1)S(1)} %get-tuple-element.56), channel_id=1, source_target_pairs={{0,6},{2,0},{4,2},{6,4},{1,7},{3,1},{5,3},{7,5},{8,14},{10,8},{12,... | collective-permute-start | bytes 786440 | tf_op jit(solution)/shard_map/ppermute | solution.py:26
  201.3 15.4 %collective-permute-start.21 = (bf16[512,256]{1,0:T(8,128)(2,1)S(1)}, bf16[512,256]{1,0:T(8,128)(2,1)S(1)}, u32[]{:S(2)}, u32[]{:S(2)}) collective-permute-start(bf16[512,256]{1,0:T(8,128)(2,1)S(1)} %get-tuple-element.51), channel_id=1, source_target_pairs={{0,4},{2,6},{4,0},{6,2},{1,5},{3,7},{5,1},{7,3},{8,12},{10,14},{12... | collective-permute-start | bytes 786440 | tf_op jit(solution)/shard_map/ppermute | solution.py:26
  201.4 17.1 %collective-permute-start.22 = (bf16[512,256]{1,0:T(8,128)(2,1)S(1)}, bf16[512,256]{1,0:T(8,128)(2,1)S(1)}, u32[]{:S(2)}, u32[]{:S(2)}) collective-permute-start(bf16[512,256]{1,0:T(8,128)(2,1)S(1)} %get-tuple-element.52), channel_id=1, source_target_pairs={{0,2},{2,4},{4,6},{6,0},{1,3},{3,5},{5,7},{7,1},{8,10},{10,12},{12... | collective-permute-start | bytes 786440 | tf_op jit(solution)/shard_map/ppermute | solution.py:26
  202.0 16.5 %collective-permute-start.23 = (bf16[512,256]{1,0:T(8,128)(2,1)S(1)}, bf16[512,256]{1,0:T(8,128)(2,1)S(1)}, u32[]{:S(2)}, u32[]{:S(2)}) collective-permute-start(bf16[512,256]{1,0:T(8,128)(2,1)S(1)} %get-tuple-element.53), channel_id=1, source_target_pairs={{0,6},{2,0},{4,2},{6,4},{1,7},{3,1},{5,3},{7,5},{8,14},{10,8},{12,... | collective-permute-start | bytes 786440 | tf_op jit(solution)/shard_map/ppermute | solution.py:26
  208.5 8.2 %collective-permute-start.27 = (bf16[512,256]{1,0:T(8,128)(2,1)S(1)}, bf16[512,256]{1,0:T(8,128)(2,1)S(1)}, u32[]{:S(2)}, u32[]{:S(2)}) collective-permute-start(bf16[512,256]{1,0:T(8,128)(2,1)S(1)} %add_convert_fusion.1), channel_id=1, source_target_pairs={{0,8},{8,0},{1,9},{9,1},{2,10},{10,2},{3,11},{11,3},{4,12},{12,4},... | collective-permute-start | bytes 786440 | tf_op jit(solution)/shard_map/ppermute | solution.py:30
  (14 other events, 32.6 us)

commit v4 on v3

--- a/solution.py
+++ b/solution.py
@@ -73,6 +73,10 @@
     return jnp.transpose(jnp.broadcast_to(column, (column.shape[0], 128)))[0:1]
 
 
+def as_column(row):
+    return jnp.transpose(jnp.broadcast_to(row, (128, row.shape[1])))[:, 0:1]
+
+
 def lane_sums(value):
     lanes = value[:, 0:128]
     for k in range(128, value.shape[1], 128):
@@ -98,19 +102,23 @@
 LOWEST = -3.0e38
 
 
-def student_body(where, *refs):
+def student_body(group, where, *refs):
     slices, weights, refs = refs[:8], refs[8:12], refs[12:]
-    teacher, teacher_stats, total, stats, peaks, masses, crosses, tops = refs
+    if group == 0:
+        teacher, teacher_stats, total, stats, peaks, masses, crosses, tops = refs
+    else:
+        total, stats, peaks, masses = refs
     c = where[4]
     rows, width = slices[0].shape
     step = pl.program_id(0)
 
     @pl.when(step == 0)
     def _():
-        tops[...] = jnp.transpose(jnp.broadcast_to(teacher_stats[0:1, :], (128, rows)))
+        if group == 0:
+            tops[...] = jnp.transpose(jnp.broadcast_to(teacher_stats[0:1, :], (128, rows)))
+            crosses[...] = jnp.zeros(crosses.shape, F32)
         peaks[...] = jnp.full(peaks.shape, LOWEST, F32)
         masses[...] = jnp.zeros(masses.shape, F32)
-        crosses[...] = jnp.zeros(crosses.shape, F32)
 
     for begin in range(0, total.shape[1], 256):
         value = None
@@ -130,25 +138,30 @@
             old = peaks[at, :]
             new = jnp.maximum(jnp.maximum(old, parts[0]), parts[1])
             mass = masses[at, :] * jnp.exp(old - new)
-            cross = crosses[at, :]
+            cross = crosses[at, :] if group == 0 else None
             for k, part in enumerate(parts):
                 mass = mass + jnp.exp(part - new)
+                if group:
+                    continue
                 t = teacher[at, begin + 128 * k : begin + 128 * k + 128].astype(F32)
                 cross = cross + jnp.exp(t - tops[at, :]) * (t - part)
             peaks[at, :] = new
             masses[at, :] = mass
-            crosses[at, :] = cross
+            if group == 0:
+                crosses[at, :] = cross
 
     @pl.when(step == pl.num_programs(0) - 1)
     def _():
         peak = jnp.max(peaks[...], axis=1, keepdims=True)
         mass = jnp.sum(masses[...] * jnp.exp(peaks[...] - peak), axis=1, keepdims=True)
-        cross = jnp.sum(crosses[...], axis=1, keepdims=True)
-        for k, column in enumerate((peak, mass, cross)):
+        found = [peak, mass]
+        if group == 0:
+            found.append(jnp.sum(crosses[...], axis=1, keepdims=True))
+        for k, column in enumerate(found):
             stats[k : k + 1, :] = as_row(column)
 
 
-def student_part(where, pairs, weight, teacher, teacher_stats, group, block=512):
+def student_part(where, pairs, weight, group, teacher=None, teacher_stats=None, block=512):
     rows, width = pairs[0][0].shape
     columns = weight.shape[1] // 2
     steps = columns // block
@@ -163,18 +176,28 @@
     tile = pl.BlockSpec((rows, block), lambda j, at: (0, j))
     kept = pl.BlockSpec((rows, block), lambda j, at: (0, at[2] * steps + j))
     return call(
-        student_body,
+        functools.partial(student_body, group),
         where,
-        [*(array for pair in pairs for array in pair), *[weight] * 4, teacher, teacher_stats],
-        in_specs + [kept if group == 0 else tile, whole(teacher_stats.shape)],
-        [jax.ShapeDtypeStruct((rows, columns), F32), jax.ShapeDtypeStruct((3, rows), F32)],
-        [tile, whole((3, rows))],
+        [*(array for pair in pairs for array in pair), *[weight] * 4]
+        + ([teacher, teacher_stats] if group == 0 else []),
+        in_specs + ([kept, whole(teacher_stats.shape)] if group == 0 else []),
+        [jax.ShapeDtypeStruct((rows, columns), F32), jax.ShapeDtypeStruct((3 - group, rows), F32)],
+        [tile, whole((3 - group, rows))],
         (steps,),
-        [pltpu.VMEM((rows, 128), F32)] * 4,
+        [pltpu.VMEM((rows, 128), F32)] * (4 - 2 * group),
         micros=8,
         vmem=28,
-        loose=(12,) if group else (),
-    )
+    )
+
+
+def cross_body(where, student, teacher, teacher_stats, cross):
+    top = as_column(teacher_stats[0:1, :])
+    lanes = None
+    for k in range(0, student.shape[1], 128):
+        t = teacher[:, k : k + 128].astype(F32)
+        part = jnp.exp(t - top) * (t - student[:, k : k + 128])
+        lanes = part if lanes is None else lanes + part
+    cross[...] = as_row(jnp.sum(lanes, axis=1, keepdims=True))
 
 
 def teacher_body(where, teacher, stats, leaving):
@@ -408,11 +431,21 @@
         gathered.append(pairs)
 
     student_own, stats_own = student_part(
-        where, gathered[0], head_weight, teacher_logits, teacher_stats, 0
-    )
-    student_other, stats_other = student_part(
-        where, gathered[1], head_weight, arrived_teacher, partner_stats, 1
-    )
+        where, gathered[0], head_weight, 0, teacher_logits, teacher_stats
+    )
+    student_other, stats_other = student_part(where, gathered[1], head_weight, 1)
+    tile = pl.BlockSpec((128, half), lambda j, at: (j, 0))
+    cross_other = call(
+        cross_body,
+        where,
+        [student_other, arrived_teacher, partner_stats],
+        [tile, tile, pl.BlockSpec((2, 128), lambda j, at: (0, j))],
+        jax.ShapeDtypeStruct((1, rows), F32),
+        pl.BlockSpec((1, 128), lambda j, at: (0, j)),
+        (rows // 128,),
+        loose=(1,),
+    )
+    stats_other = jnp.concatenate([stats_other, cross_other], axis=0)
     local = jnp.concatenate(
         [jnp.concatenate([stats_own, stats_other], axis=1), teacher_stats.reshape(1, 2 * rows)],
         axis=0,

time: 221 us -> 204 us (0.923)
  waiting for transfers between devices: 86.3 us -> 69.2 us
  Pallas kernels: 51 us -> 54 us
  starting transfers between devices: 60.1 us -> 57.4 us
    ppermute x13, waiting for transfers between devices: 27.6 us -> 0.03 us  [swapped(): return lax.ppermute(array, axis, SWAP)]
    ppermute x18, waiting for transfers between devices: 58.8 us -> 69.1 us  [sent(): lax.ppermute(array, axis, [(k, (k + by) % size) for k in range(size)])]
    pallas_call x9 -> x10, Pallas kernels: 46 us -> 49.1 us  [call(): pl.pallas_call(body, cost_estimate=cost, out_shape=out_shapes, grid_spec=...]
    ppermute x13, starting transfers between devices: 16.8 us -> 14 us  [swapped(): return lax.ppermute(array, axis, SWAP)]
  transfers between devices with their start and end apart: 34 -> 34, of which waited for: 9 -> 8; matrix products, arithmetic and copies ran while one was open for 4% -> 4% of each run, Pallas kernels for 18% -> 22%
where the time goes in v4:
time: 204 us; the launch traced here: 203 us
  waiting for transfers between devices  69.2 us (34%)
  starting transfers between devices  57.4 us (28%)
  Pallas kernels  54 us (26%)
  matrix products  10.2 us (5%)
  local copies, waits for them, and re-layouts  9.32 us (5%)
    ppermute x18, waiting for transfers between devices, sent(): lax.ppermute(array, axis, [(k, (k + by) % size) for k in range(size)])  69.1 us
    pallas_call x10, Pallas kernels, call(): pl.pallas_call(body, cost_estimate=cost, out_shape=out_shapes, grid_spec=...  49.1 us
    ppermute x18, starting transfers between devices, sent(): lax.ppermute(array, axis, [(k, (k + by) % size) for k in range(size)])  23.9 us
    all_to_all x2, starting transfers between devices, per_device(): pieces.append(lax.all_to_all(total, ('p', 'q'), 0, 0, tiled=True))  14.4 us
    ppermute x13, starting transfers between devices, swapped(): return lax.ppermute(array, axis, SWAP)  14 us
    unnamed x57, local copies, waits for them, and re-layouts  8.48 us
    dot_general x6, matrix products, per_device(): lax.dot_general(blocks[d], grads, (((0,), (0,)), ((), ())), preferred_ele...  7.08 us
    all_to_all x1, starting transfers between devices, sent_to_all(): return lax.all_to_all(copies, axis, 0, 0, tiled=True)  5.16 us
  transfers between devices with their start and end apart: 34, of which 8 were waited for; matrix products, arithmetic and copies ran while one was open for 4% of the time, Pallas kernels for 22%

profile of v4, /device:TPU:1, one launch (start us, length us, event | category | flops | bytes accessed | tf_op | source)
XLA Modules:
  0.0 202.7 jit_solution(3880691069579335407)
XLA Ops:
  0.6 2.1 %collective-permute-start.5 = (bf16[512,256]{1,0:T(8,128)(2,1)}, bf16[512,256]{1,0:T(8,128)(2,1)S(1)}, u32[]{:S(2)}, u32[]{:S(2)}) collective-permute-start(bf16[512,256]{1,0:T(8,128)(2,1)} %refs_0_.6), channel_id=1, source_target_pairs={{0,2},{2,4},{4,6},{6,0},{1,3},{3,5},{5,7},{7,1},{8,10},{10,12},{12... | collective-permute-start | bytes 786440 | tf_op jit(solution)/shard_map/ppermute | solution.py:26
  2.7 2.5 %collective-permute-start.3 = (bf16[512,256]{1,0:T(8,128)(2,1)}, bf16[512,256]{1,0:T(8,128)(2,1)S(1)}, u32[]{:S(2)}, u32[]{:S(2)}) collective-permute-start(bf16[512,256]{1,0:T(8,128)(2,1)} %refs_0_.6), channel_id=1, source_target_pairs={{0,4},{2,6},{4,0},{6,2},{1,5},{3,7},{5,1},{7,3},{8,12},{10,14},{12... | collective-permute-start | bytes 786440 | tf_op jit(solution)/shard_map/ppermute | solution.py:26
  5.2 1.2 collective-permute-start.1
  6.3 1.5 collective-permute-start
  7.9 1.6 collective-permute-start.7
  9.6 2.3 %collective-permute-start.6 = (bf16[512,256]{1,0:T(8,128)(2,1)S(1)}, bf16[512,256]{1,0:T(8,128)(2,1)S(1)}, u32[]{:S(2)}, u32[]{:S(2)}) collective-permute-start(bf16[512,256]{1,0:T(8,128)(2,1)S(1)} %collective-permute-done.5.refs_6_), channel_id=1, source_target_pairs={{0,1},{1,0},{2,3},{3,2},{4,5},{5,4},{6,7},{7,6},{8,9},{9,8},{10,11... | collective-permute-start | bytes 786440 | tf_op jit(solution)/shard_map/ppermute | solution.py:30
  11.9 4.9 %collective-permute-done.3.refs_4_ = bf16[512,256]{1,0:T(8,128)(2,1)S(1)} collective-permute-done((bf16[512,256]{1,0:T(8,128)(2,1)}, bf16[512,256]{1,0:T(8,128)(2,1)S(1)}, u32[]{:S(2)}, u32[]{:S(2)}) %collective-permute-start.3) | collective-permute-done | bytes 262176 | tf_op jit(solution)/shard_map/ppermute | solution.py:26
  16.7 1.5 collective-permute-start.4
  18.3 3.4 %shard_map.58 = (f32[2,512]{1,0:T(2,128)S(1)}, bf16[512,1024]{1,0:T(8,128)(2,1)}) custom-call(s32[5]{0:T(128)S(1)} %stack.23.where, bf16[512,2048]{1,0:T(8,128)(2,1)} %t_own.2), custom_call_target="tpu_custom_call" | custom-call | flops 2249999872 | bytes 1048576 | tf_op jit(solution)/shard_map/pallas_call | solution.py:57
  21.7 1.7 collective-permute-start.15
  24.4 2.1 %collective-permute-start.9 = (bf16[512,256]{1,0:T(8,128)(2,1)S(1)}, bf16[512,256]{1,0:T(8,128)(2,1)S(1)}, u32[]{:S(2)}, u32[]{:S(2)}) collective-permute-start(bf16[512,256]{1,0:T(8,128)(2,1)S(1)} %collective-permute-done.7.refs_8_.refs_0_), channel_id=1, source_target_pairs={{0,6},{2,0},{4,2},{6,4},{1,7},{3,1},{5,3},{7,5},{8,14},{10,8},{12,... | collective-permute-start | bytes 786440 | tf_op jit(solution)/shard_map/ppermute | solution.py:26
  26.5 1.0 collective-permute-start.8
  27.5 10.7 %collective-permute-done.13.refs_14_.refs_6_ = bf16[512,256]{1,0:T(8,128)(2,1)S(1)} collective-permute-done((bf16[512,256]{1,0:T(8,128)(2,1)S(1)}, bf16[512,256]{1,0:T(8,128)(2,1)S(1)}, u32[]{:S(2)}, u32[]{:S(2)}) %collective-permute-start.13) | collective-permute-done | bytes 262176 | tf_op jit(solution)/shard_map/ppermute | solution.py:26
  38.2 1.1 collective-permute-start.14
  39.9 7.2 %shard_map.59 = (f32[512,1024]{1,0:T(8,128)}, f32[3,512]{1,0:T(4,128)S(1)}) custom-call(s32[5]{0:T(128)S(1)} %stack.23.where, bf16[512,256]{1,0:T(8,128)(2,1)S(1)} %copy-done, bf16[512,256]{1,0:T(8,128)(2,1)S(1)} %collective-permute-done.refs_1_, bf16[512,256]{1,0:T(8,128)(2,1)S(1)} %collective-permute-done.1.refs_2_, ...), custom_call_target="tpu_custom_call" | custom-call | flops 3600000000 | bytes 1048576 | tf_op jit(solution)/shard_map/pallas_call | solution.py:57
  47.3 6.3 %shard_map.61 = (f32[512,1024]{1,0:T(8,128)}, f32[2,512]{1,0:T(2,128)S(1)}) custom-call(s32[5]{0:T(128)S(1)} %stack.23.where, bf16[512,256]{1,0:T(8,128)(2,1)S(1)} %collective-permute-done.7.refs_8_.refs_0_, bf16[512,256]{1,0:T(8,128)(2,1)S(1)} %collective-permute-done.8.refs_9_.refs_1_, bf16[512,256]{1,0:T(8,128)(2,1)S(1)} %collective-permute-done.9.refs_10_.refs_2_, ...), custom_call_target="tpu_custom_call" | custom-call | flops 3600000000 | bytes 1048576 | tf_op jit(solution)/shard_map/pallas_call | solution.py:57
  53.7 3.7 %shard_map.62 = f32[1,512]{1,0:T(1,128)S(1)} custom-call(s32[5]{0:T(128)S(1)} %stack.23.where, f32[512,1024]{1,0:T(8,128)} %get-tuple-element.39.student.s_other, bf16[512,1024]{1,0:T(8,128)(2,1)S(1)} %collective-permute-done.15.teacher.t_other, f32[2,512]{1,0:T(2,128)S(1)} %collective-permute-done.16.teacher_stats), custom_call_target="tpu_custom_call" | custom-call | flops 900000000 | bytes 1048576 | tf_op jit(solution)/shard_map/pallas_call | solution.py:57
  58.2 5.2 %all-to-all-start = ((f32[16,4,1024]{2,1,0:T(4,128)}), f32[16,4,1024]{2,1,0:T(4,128)S(1)}, u32[]{:S(2)}, u32[]{:S(2)}) async-start(f32[16,4,1024]{2,1,0:T(4,128)} %broadcast_in_dim.3), calls=%async_computation | async-start | bytes 524288 | tf_op jit(solution)/shard_map/all_to_all | solution.py:35
  64.3 0.9 copy-done.4
  66.2 0.9 copy-done.8
  67.2 0.9 copy-done.10
  69.1 0.9 copy-done.14
  71.0 2.9 %shard_map.60 = (bf16[1024,512]{1,0:T(8,128)(2,1)}, bf16[1024,512]{1,0:T(8,128)(2,1)}, bf16[1024,512]{1,0:T(8,128)(2,1)}, bf16[1024,512]{1,0:T(8,128)(2,1)}) custom-call(s32[5]{0:T(128)S(1)} %stack.23.where, bf16[512,256]{1,0:T(8,128)(2,1)S(1)} %copy-done, bf16[512,256]{1,0:T(8,128)(2,1)S(1)} %collective-permute-done.refs_1_, ...), custom_call_target="tpu_custom_call" | custom-call | flops 2249999872 | bytes 1048576 | tf_op jit(solution)/shard_map/pallas_call | solution.py:57
  73.9 5.4 %shard_map.63.first = bf16[1024,512]{1,0:T(8,128)(2,1)} custom-call(s32[5]{0:T(128)S(1)} %stack.23.where, f32[512,1024]{1,0:T(8,128)} %get-tuple-element.38.s_own, f32[512,1024]{1,0:T(8,128)} %get-tuple-element.39.student.s_other, bf16[512,2048]{1,0:T(8,128)(2,1)} %t_own.2, bf16[512,1024]{1,0:T(8,128)(2,1)S(1)} %collective-permute-done.15.teacher.t_other, ...), custom_call_target="tpu_custom_call" | custom-call | flops 1800000000 | bytes 1048576 | tf_op jit(solution)/shard_map/pallas_call | solution.py:57
  79.3 2.1 %convolution_convert_fusion.5 = bf16[512,512]{1,0:T(8,128)(2,1)S(1)} fusion(bf16[1024,512]{1,0:T(8,128)(2,1)S(1)} %copy-done.27, bf16[1024,512]{1,0:T(8,128)(2,1)} %shard_map.63.first), kind=kOutput, calls=%fused_computation.9 | convolution fusion | flops 537133056 | bytes 2621440 | tf_op jit(solution)/shard_map/dot_general | solution.py:478
  81.4 2.8 %collective-permute-start.19 = (bf16[512,512]{1,0:T(8,128)(2,1)S(1)}, bf16[512,512]{1,0:T(8,128)(2,1)S(1)}, u32[]{:S(2)}, u32[]{:S(2)}) collective-permute-start(bf16[512,512]{1,0:T(8,128)(2,1)S(1)} %convolution_convert_fusion.5), channel_id=1, source_target_pairs={{0,192},{64,0},{128,64},{192,128},{1,193},{65,1},{129,65},{193,129... | collective-permute-start | bytes 1572872 | tf_op jit(solution)/shard_map/ppermute | solution.py:26
  85.0 5.4 %shard_map.64 = (bf16[1024,512]{1,0:T(8,128)(2,1)}, f32[5,512]{1,0:T(8,128)S(1)}) custom-call(s32[5]{0:T(128)S(1)} %stack.23.where, f32[512,1024]{1,0:T(8,128)} %get-tuple-element.38.s_own, f32[512,1024]{1,0:T(8,128)} %get-tuple-element.39.student.s_other, bf16[512,2048]{1,0:T(8,128)(2,1)} %t_own.2, ...), custom_call_target="tpu_custom_call" | custom-call | flops 1800000000 | bytes 1048576 | tf_op jit(solution)/shard_map/pallas_call | solution.py:57
  90.4 6.7 %shard_map.65 = bf16[4,1024,256]{2,1,0:T(8,128)(2,1)} custom-call(s32[5]{0:T(128)S(1)} %stack.23.where, bf16[1024,512]{1,0:T(8,128)(2,1)} %shard_map.63.first, bf16[1024,512]{1,0:T(8,128)(2,1)} %get-tuple-element.49.last, bf16[2048,2048]{1,0:T(8,128)(2,1)} %refs_3_.5, bf16[2048,2048]{1,0:T(8,128)(2,1)} %refs_3_.5, bf16[2048,2048]{1,0:T(8,128)(2,1)} %refs_3_.5, ...), custom_call_target="tpu_custom_call" | custom-call | flops 2700000000 | bytes 1048576 | tf_op jit(solution)/shard_map/pallas_call | solution.py:57
  100.8 12.3 %collective-permute-done.17 = bf16[512,512]{1,0:T(8,128)(2,1)S(1)} collective-permute-done((bf16[512,512]{1,0:T(8,128)(2,1)S(1)}, bf16[512,512]{1,0:T(8,128)(2,1)S(1)}, u32[]{:S(2)}, u32[]{:S(2)}) %collective-permute-start.17) | collective-permute-done | bytes 524320 | tf_op jit(solution)/shard_map/ppermute | solution.py:26
  113.1 11.7 %collective-permute-done.18 = bf16[512,512]{1,0:T(8,128)(2,1)S(1)} collective-permute-done((bf16[512,512]{1,0:T(8,128)(2,1)S(1)}, bf16[512,512]{1,0:T(8,128)(2,1)S(1)}, u32[]{:S(2)}, u32[]{:S(2)}) %collective-permute-start.18) | collective-permute-done | bytes 524320 | tf_op jit(solution)/shard_map/ppermute | solution.py:26
  124.8 1.5 fusion
  126.4 7.8 %all-to-all-start.2 = ((bf16[8,64,512]{2,1,0:T(8,128)(2,1)}), bf16[8,64,512]{2,1,0:T(8,128)(2,1)S(1)}, u32[]{:S(2)}, u32[]{:S(2)}) async-start(bf16[8,64,512]{2,1,0:T(8,128)(2,1)} %bitcast.6), calls=%async_computation.2 | async-start | bytes 1048576 | tf_op jit(solution)/shard_map/all_to_all | solution.py:498
  134.2 2.1 %convolution_convert_fusion.2 = bf16[512,512]{1,0:T(8,128)(2,1)S(1)} fusion(bf16[1024,512]{1,0:T(8,128)(2,1)} %get-tuple-element.45, bf16[1024,512]{1,0:T(8,128)(2,1)S(1)} %copy-done.20), kind=kOutput, calls=%fused_computation.6 | convolution fusion | flops 537133056 | bytes 2621440 | tf_op jit(solution)/shard_map/dot_general | solution.py:478
  136.8 2.6 %collective-permute-start.30 = (bf16[512,512]{1,0:T(8,128)(2,1)S(1)}, bf16[512,512]{1,0:T(8,128)(2,1)S(1)}, u32[]{:S(2)}, u32[]{:S(2)}) collective-permute-start(bf16[512,512]{1,0:T(8,128)(2,1)S(1)} %convolution_convert_fusion), channel_id=1, source_target_pairs={{0,192},{64,0},{128,64},{192,128},{1,193},{65,1},{129,65},{193,129... | collective-permute-start | bytes 1572872 | tf_op jit(solution)/shard_map/ppermute | solution.py:26
  139.3 11.2 %collective-permute-done.28 = bf16[512,512]{1,0:T(8,128)(2,1)S(1)} collective-permute-done((bf16[512,512]{1,0:T(8,128)(2,1)S(1)}, bf16[512,512]{1,0:T(8,128)(2,1)S(1)}, u32[]{:S(2)}, u32[]{:S(2)}) %collective-permute-start.28) | collective-permute-done | bytes 524320 | tf_op jit(solution)/shard_map/ppermute | solution.py:26
  150.6 12.3 %collective-permute-done.29 = bf16[512,512]{1,0:T(8,128)(2,1)S(1)} collective-permute-done((bf16[512,512]{1,0:T(8,128)(2,1)S(1)}, bf16[512,512]{1,0:T(8,128)(2,1)S(1)}, u32[]{:S(2)}, u32[]{:S(2)}) %collective-permute-start.29) | collective-permute-done | bytes 524320 | tf_op jit(solution)/shard_map/ppermute | solution.py:26
  162.9 1.5 fusion.1
  164.4 6.6 %all-to-all-start.1 = ((bf16[8,64,512]{2,1,0:T(8,128)(2,1)}), bf16[8,64,512]{2,1,0:T(8,128)(2,1)S(1)}, u32[]{:S(2)}, u32[]{:S(2)}) async-start(bf16[8,64,512]{2,1,0:T(8,128)(2,1)} %bitcast.7), calls=%async_computation.1 | async-start | bytes 1048576 | tf_op jit(solution)/shard_map/all_to_all | solution.py:498
  171.1 4.0 %shard_map.66 = (bf16[512,256]{1,0:T(8,128)(2,1)S(1)}, bf16[512,256]{1,0:T(8,128)(2,1)S(1)}, bf16[512,256]{1,0:T(8,128)(2,1)S(1)}, bf16[512,256]{1,0:T(8,128)(2,1)S(1)}) custom-call(s32[5]{0:T(128)S(1)} %stack.23.where, bf16[1024,512]{1,0:T(8,128)(2,1)} %shard_map.63.first, bf16[1024,512]{1,0:T(8,128)(2,1)} %get-tuple-element.49.last, ...), custom_call_target="tpu_custom_call" | custom-call | flops 2700000000 | bytes 1048576 | tf_op jit(solution)/shard_map/pallas_call | solution.py:57
  175.1 2.8 %collective-permute-start.24 = (bf16[512,256]{1,0:T(8,128)(2,1)S(1)}, bf16[512,256]{1,0:T(8,128)(2,1)S(1)}, u32[]{:S(2)}, u32[]{:S(2)}) collective-permute-start(bf16[512,256]{1,0:T(8,128)(2,1)S(1)} %get-tuple-element.54), channel_id=1, source_target_pairs={{0,4},{2,6},{4,0},{6,2},{1,5},{3,7},{5,1},{7,3},{8,12},{10,14},{12... | collective-permute-start | bytes 786440 | tf_op jit(solution)/shard_map/ppermute | solution.py:26
  178.2 2.4 %collective-permute-start.26 = (bf16[512,256]{1,0:T(8,128)(2,1)S(1)}, bf16[512,256]{1,0:T(8,128)(2,1)S(1)}, u32[]{:S(2)}, u32[]{:S(2)}) collective-permute-start(bf16[512,256]{1,0:T(8,128)(2,1)S(1)} %get-tuple-element.56), channel_id=1, source_target_pairs={{0,6},{2,0},{4,2},{6,4},{1,7},{3,1},{5,3},{7,5},{8,14},{10,8},{12,... | collective-permute-start | bytes 786440 | tf_op jit(solution)/shard_map/ppermute | solution.py:26
  180.6 4.0 %shard_map.67 = (bf16[512,256]{1,0:T(8,128)(2,1)S(1)}, bf16[512,256]{1,0:T(8,128)(2,1)S(1)}, bf16[512,256]{1,0:T(8,128)(2,1)S(1)}, bf16[512,256]{1,0:T(8,128)(2,1)S(1)}) custom-call(s32[5]{0:T(128)S(1)} %stack.23.where, bf16[1024,512]{1,0:T(8,128)(2,1)} %shard_map.63.first, bf16[1024,512]{1,0:T(8,128)(2,1)} %get-tuple-element.49.last, ...), custom_call_target="tpu_custom_call" | custom-call | flops 2700000000 | bytes 1048576 | tf_op jit(solution)/shard_map/pallas_call | solution.py:57
  185.3 2.2 %collective-permute-start.23 = (bf16[512,256]{1,0:T(8,128)(2,1)S(1)}, bf16[512,256]{1,0:T(8,128)(2,1)S(1)}, u32[]{:S(2)}, u32[]{:S(2)}) collective-permute-start(bf16[512,256]{1,0:T(8,128)(2,1)S(1)} %get-tuple-element.53), channel_id=1, source_target_pairs={{0,6},{2,0},{4,2},{6,4},{1,7},{3,1},{5,3},{7,5},{8,14},{10,8},{12,... | collective-permute-start | bytes 786440 | tf_op jit(solution)/shard_map/ppermute | solution.py:26
  187.5 4.2 %collective-permute-done.25 = bf16[512,256]{1,0:T(8,128)(2,1)S(1)} collective-permute-done((bf16[512,256]{1,0:T(8,128)(2,1)S(1)}, bf16[512,256]{1,0:T(8,128)(2,1)S(1)}, u32[]{:S(2)}, u32[]{:S(2)}) %collective-permute-start.25) | collective-permute-done | bytes 262176 | tf_op jit(solution)/shard_map/ppermute | solution.py:26
  191.8 1.8 collective-permute-start.27
  194.2 2.5 %shard_map.68.refs_0_ = f32[64,2048]{1,0:T(8,128)} custom-call(s32[5]{0:T(128)} %copy-done.17, bf16[8,64,512]{2,1,0:T(8,128)(2,1)} %copy-done.21), custom_call_target="tpu_custom_call" | custom-call | flops 536870912 | bytes 1048576 | tf_op jit(solution)/shard_map/pallas_call | solution.py:392
  197.5 2.5 %shard_map.69 = f32[64,2048]{1,0:T(8,128)} custom-call(s32[5]{0:T(128)} %copy-done.17, bf16[8,64,512]{2,1,0:T(8,128)(2,1)} %copy-done.22, f32[64,2048]{1,0:T(8,128)} %shard_map.68.refs_0_), custom_call_target="tpu_custom_call", output_to_operand_aliasing={{}: (2, {})} | custom-call | flops 536870912 | bytes 1048576 | tf_op jit(solution)/shard_map/pallas_call | solution.py:392
  200.0 1.8 collective-permute-done.22
  (103 shorter events, 14.9 us)
Async XLA Ops:
  0.6 9.0 %collective-permute-start.5 = (bf16[512,256]{1,0:T(8,128)(2,1)}, bf16[512,256]{1,0:T(8,128)(2,1)S(1)}, u32[]{:S(2)}, u32[]{:S(2)}) collective-permute-start(bf16[512,256]{1,0:T(8,128)(2,1)} %refs_0_.6), channel_id=1, source_target_pairs={{0,2},{2,4},{4,6},{6,0},{1,3},{3,5},{5,7},{7,1},{8,10},{10,12},{12... | collective-permute-start | bytes 786440 | tf_op jit(solution)/shard_map/ppermute | solution.py:26
  2.7 14.0 %collective-permute-start.3 = (bf16[512,256]{1,0:T(8,128)(2,1)}, bf16[512,256]{1,0:T(8,128)(2,1)S(1)}, u32[]{:S(2)}, u32[]{:S(2)}) collective-permute-start(bf16[512,256]{1,0:T(8,128)(2,1)} %refs_0_.6), channel_id=1, source_target_pairs={{0,4},{2,6},{4,0},{6,2},{1,5},{3,7},{5,1},{7,3},{8,12},{10,14},{12... | collective-permute-start | bytes 786440 | tf_op jit(solution)/shard_map/ppermute | solution.py:26
  5.2 16.5 %collective-permute-start.1 = (bf16[512,256]{1,0:T(8,128)(2,1)}, bf16[512,256]{1,0:T(8,128)(2,1)S(1)}, u32[]{:S(2)}, u32[]{:S(2)}) collective-permute-start(bf16[512,256]{1,0:T(8,128)(2,1)} %refs_0_.6), channel_id=1, source_target_pairs={{0,6},{2,0},{4,2},{6,4},{1,7},{3,1},{5,3},{7,5},{8,14},{10,8},{12,... | collective-permute-start | bytes 786440 | tf_op jit(solution)/shard_map/ppermute | solution.py:26
  6.3 17.1 %collective-permute-start = (bf16[512,256]{1,0:T(8,128)(2,1)}, bf16[512,256]{1,0:T(8,128)(2,1)S(1)}, u32[]{:S(2)}, u32[]{:S(2)}) collective-permute-start(bf16[512,256]{1,0:T(8,128)(2,1)} %refs_0_.6), channel_id=1, source_target_pairs={{0,1},{1,0},{2,3},{3,2},{4,5},{5,4},{6,7},{7,6},{8,9},{9,8},{10,11... | collective-permute-start | bytes 786440 | tf_op jit(solution)/shard_map/ppermute | solution.py:30
  7.9 15.9 %collective-permute-start.7 = (bf16[512,256]{1,0:T(8,128)(2,1)}, bf16[512,256]{1,0:T(8,128)(2,1)S(1)}, u32[]{:S(2)}, u32[]{:S(2)}) collective-permute-start(bf16[512,256]{1,0:T(8,128)(2,1)} %refs_0_.6), channel_id=1, source_target_pairs={{0,8},{8,0},{1,9},{9,1},{2,10},{10,2},{3,11},{11,3},{4,12},{12,4},... | collective-permute-start | bytes 786440 | tf_op jit(solution)/shard_map/ppermute | solution.py:30
  9.6 171.0 %copy-start.17 = (s32[5]{0:T(128)}, s32[5]{0:T(128)S(1)}, u32[]{:S(2)}) copy-start(s32[5]{0:T(128)S(1)} %stack.23.where) | copy-start | bytes 64
  9.6 30.3 %copy-start = (bf16[512,256]{1,0:T(8,128)(2,1)S(1)}, bf16[512,256]{1,0:T(8,128)(2,1)}, u32[]{:S(2)}) copy-start(bf16[512,256]{1,0:T(8,128)(2,1)} %refs_0_.6) | copy-start | bytes 786436
  9.6 14.2 %collective-permute-start.6 = (bf16[512,256]{1,0:T(8,128)(2,1)S(1)}, bf16[512,256]{1,0:T(8,128)(2,1)S(1)}, u32[]{:S(2)}, u32[]{:S(2)}) collective-permute-start(bf16[512,256]{1,0:T(8,128)(2,1)S(1)} %collective-permute-done.5.refs_6_), channel_id=1, source_target_pairs={{0,1},{1,0},{2,3},{3,2},{4,5},{5,4},{6,7},{7,6},{8,9},{9,8},{10,11... | collective-permute-start | bytes 786440 | tf_op jit(solution)/shard_map/ppermute | solution.py:30
  16.7 7.6 %collective-permute-start.4 = (bf16[512,256]{1,0:T(8,128)(2,1)S(1)}, bf16[512,256]{1,0:T(8,128)(2,1)S(1)}, u32[]{:S(2)}, u32[]{:S(2)}) collective-permute-start(bf16[512,256]{1,0:T(8,128)(2,1)S(1)} %collective-permute-done.3.refs_4_), channel_id=1, source_target_pairs={{0,1},{1,0},{2,3},{3,2},{4,5},{5,4},{6,7},{7,6},{8,9},{9,8},{10,11... | collective-permute-start | bytes 786440 | tf_op jit(solution)/shard_map/ppermute | solution.py:30
  21.7 32.0 %collective-permute-start.15 = (bf16[512,1024]{1,0:T(8,128)(2,1)}, bf16[512,1024]{1,0:T(8,128)(2,1)S(1)}, u32[]{:S(2)}, u32[]{:S(2)}) collective-permute-start(bf16[512,1024]{1,0:T(8,128)(2,1)} %get-tuple-element.35), channel_id=1, source_target_pairs={{0,8},{8,0},{1,9},{9,1},{2,10},{10,2},{3,11},{11,3},{4,12},{12,4},... | collective-permute-start | bytes 3145736 | tf_op jit(solution)/shard_map/ppermute | solution.py:30
  23.5 3.1 %collective-permute-start.2 = (bf16[512,256]{1,0:T(8,128)(2,1)S(1)}, bf16[512,256]{1,0:T(8,128)(2,1)S(1)}, u32[]{:S(2)}, u32[]{:S(2)}) collective-permute-start(bf16[512,256]{1,0:T(8,128)(2,1)S(1)} %collective-permute-done.1.refs_2_), channel_id=1, source_target_pairs={{0,1},{1,0},{2,3},{3,2},{4,5},{5,4},{6,7},{7,6},{8,9},{9,8},{10,11... | collective-permute-start | bytes 786440 | tf_op jit(solution)/shard_map/ppermute | solution.py:30
  23.7 14.5 %collective-permute-start.13 = (bf16[512,256]{1,0:T(8,128)(2,1)S(1)}, bf16[512,256]{1,0:T(8,128)(2,1)S(1)}, u32[]{:S(2)}, u32[]{:S(2)}) collective-permute-start(bf16[512,256]{1,0:T(8,128)(2,1)S(1)} %collective-permute-done.7.refs_8_.refs_0_), channel_id=1, source_target_pairs={{0,2},{2,4},{4,6},{6,0},{1,3},{3,5},{5,7},{7,1},{8,10},{10,12},{12... | collective-permute-start | bytes 786440 | tf_op jit(solution)/shard_map/ppermute | solution.py:26
  23.7 15.5 %collective-permute-start.11 = (bf16[512,256]{1,0:T(8,128)(2,1)S(1)}, bf16[512,256]{1,0:T(8,128)(2,1)S(1)}, u32[]{:S(2)}, u32[]{:S(2)}) collective-permute-start(bf16[512,256]{1,0:T(8,128)(2,1)S(1)} %collective-permute-done.7.refs_8_.refs_0_), channel_id=1, source_target_pairs={{0,4},{2,6},{4,0},{6,2},{1,5},{3,7},{5,1},{7,3},{8,12},{10,14},{12... | collective-permute-start | bytes 786440 | tf_op jit(solution)/shard_map/ppermute | solution.py:26
  24.4 15.0 %collective-permute-start.9 = (bf16[512,256]{1,0:T(8,128)(2,1)S(1)}, bf16[512,256]{1,0:T(8,128)(2,1)S(1)}, u32[]{:S(2)}, u32[]{:S(2)}) collective-permute-start(bf16[512,256]{1,0:T(8,128)(2,1)S(1)} %collective-permute-done.7.refs_8_.refs_0_), channel_id=1, source_target_pairs={{0,6},{2,0},{4,2},{6,4},{1,7},{3,1},{5,3},{7,5},{8,14},{10,8},{12,... | collective-permute-start | bytes 786440 | tf_op jit(solution)/shard_map/ppermute | solution.py:26
  26.5 20.6 %copy-start.1 = (bf16[512,256]{1,0:T(8,128)(2,1)}, bf16[512,256]{1,0:T(8,128)(2,1)S(1)}, u32[]{:S(2)}) copy-start(bf16[512,256]{1,0:T(8,128)(2,1)S(1)} %collective-permute-done.2.refs_3_) | copy-start | bytes 786436
  26.5 20.6 %collective-permute-start.8 = (bf16[512,256]{1,0:T(8,128)(2,1)S(1)}, bf16[512,256]{1,0:T(8,128)(2,1)S(1)}, u32[]{:S(2)}, u32[]{:S(2)}) collective-permute-start(bf16[512,256]{1,0:T(8,128)(2,1)S(1)} %collective-permute-done.7.refs_8_.refs_0_), channel_id=1, source_target_pairs={{0,1},{1,0},{2,3},{3,2},{4,5},{5,4},{6,7},{7,6},{8,9},{9,8},{10,11... | collective-permute-start | bytes 786440 | tf_op jit(solution)/shard_map/ppermute | solution.py:30
  38.2 9.1 %copy-start.3 = (bf16[512,256]{1,0:T(8,128)(2,1)}, bf16[512,256]{1,0:T(8,128)(2,1)S(1)}, u32[]{:S(2)}) copy-start(bf16[512,256]{1,0:T(8,128)(2,1)S(1)} %collective-permute-done.13.refs_14_.refs_6_) | copy-start | bytes 786436
  38.2 9.0 %collective-permute-start.14 = (bf16[512,256]{1,0:T(8,128)(2,1)S(1)}, bf16[512,256]{1,0:T(8,128)(2,1)S(1)}, u32[]{:S(2)}, u32[]{:S(2)}) collective-permute-start(bf16[512,256]{1,0:T(8,128)(2,1)S(1)} %collective-permute-done.13.refs_14_.refs_6_), channel_id=1, source_target_pairs={{0,1},{1,0},{2,3},{3,2},{4,5},{5,4},{6,7},{7,6},{8,9},{9,8},{10,11... | collective-permute-start | bytes 786440 | tf_op jit(solution)/shard_map/ppermute | solution.py:30
  39.3 8.0 %copy-start.5 = (bf16[512,256]{1,0:T(8,128)(2,1)}, bf16[512,256]{1,0:T(8,128)(2,1)S(1)}, u32[]{:S(2)}) copy-start(bf16[512,256]{1,0:T(8,128)(2,1)S(1)} %collective-permute-done.11.refs_12_.refs_4_) | copy-start | bytes 786436
  39.3 7.9 %collective-permute-start.12 = (bf16[512,256]{1,0:T(8,128)(2,1)S(1)}, bf16[512,256]{1,0:T(8,128)(2,1)S(1)}, u32[]{:S(2)}, u32[]{:S(2)}) collective-permute-start(bf16[512,256]{1,0:T(8,128)(2,1)S(1)} %collective-permute-done.11.refs_12_.refs_4_), channel_id=1, source_target_pairs={{0,1},{1,0},{2,3},{3,2},{4,5},{5,4},{6,7},{7,6},{8,9},{9,8},{10,11... | collective-permute-start | bytes 786440 | tf_op jit(solution)/shard_map/ppermute | solution.py:30
  39.4 7.9 %copy-start.7 = (bf16[512,256]{1,0:T(8,128)(2,1)}, bf16[512,256]{1,0:T(8,128)(2,1)S(1)}, u32[]{:S(2)}) copy-start(bf16[512,256]{1,0:T(8,128)(2,1)S(1)} %collective-permute-done.9.refs_10_.refs_2_) | copy-start | bytes 786436
  39.4 7.8 %collective-permute-start.10 = (bf16[512,256]{1,0:T(8,128)(2,1)S(1)}, bf16[512,256]{1,0:T(8,128)(2,1)S(1)}, u32[]{:S(2)}, u32[]{:S(2)}) collective-permute-start(bf16[512,256]{1,0:T(8,128)(2,1)S(1)} %collective-permute-done.9.refs_10_.refs_2_), channel_id=1, source_target_pairs={{0,1},{1,0},{2,3},{3,2},{4,5},{5,4},{6,7},{7,6},{8,9},{9,8},{10,11... | collective-permute-start | bytes 786440 | tf_op jit(solution)/shard_map/ppermute | solution.py:30
  47.1 6.5 %copy-start.9 = (bf16[512,256]{1,0:T(8,128)(2,1)}, bf16[512,256]{1,0:T(8,128)(2,1)S(1)}, u32[]{:S(2)}) copy-start(bf16[512,256]{1,0:T(8,128)(2,1)S(1)} %collective-permute-done.8.refs_9_.refs_1_) | copy-start | bytes 786436
  47.1 6.6 %collective-permute-start.16 = (f32[2,512]{1,0:T(2,128)S(1)}, f32[2,512]{1,0:T(2,128)S(1)}, u32[]{:S(2)}, u32[]{:S(2)}) collective-permute-start(f32[2,512]{1,0:T(2,128)S(1)} %get-tuple-element.31.refs_13_), channel_id=1, source_target_pairs={{0,8},{8,0},{1,9},{9,1},{2,10},{10,2},{3,11},{11,3},{4,12},{12,4},... | collective-permute-start | bytes 12296 | tf_op jit(solution)/shard_map/ppermute | solution.py:30
  47.2 6.4 %copy-start.11 = (bf16[512,256]{1,0:T(8,128)(2,1)}, bf16[512,256]{1,0:T(8,128)(2,1)S(1)}, u32[]{:S(2)}) copy-start(bf16[512,256]{1,0:T(8,128)(2,1)S(1)} %collective-permute-done.14.refs_15_.refs_7_) | copy-start | bytes 786436
  47.2 6.4 %copy-start.13 = (bf16[512,256]{1,0:T(8,128)(2,1)}, bf16[512,256]{1,0:T(8,128)(2,1)S(1)}, u32[]{:S(2)}) copy-start(bf16[512,256]{1,0:T(8,128)(2,1)S(1)} %collective-permute-done.12.refs_13_.refs_5_) | copy-start | bytes 786436
  58.2 15.7 %all-to-all-start = ((f32[16,4,1024]{2,1,0:T(4,128)}), f32[16,4,1024]{2,1,0:T(4,128)S(1)}, u32[]{:S(2)}, u32[]{:S(2)}) async-start(f32[16,4,1024]{2,1,0:T(4,128)} %broadcast_in_dim.3), calls=%async_computation | async-start | bytes 524288 | tf_op jit(solution)/shard_map/all_to_all | solution.py:35
  81.4 43.4 %collective-permute-start.19 = (bf16[512,512]{1,0:T(8,128)(2,1)S(1)}, bf16[512,512]{1,0:T(8,128)(2,1)S(1)}, u32[]{:S(2)}, u32[]{:S(2)}) collective-permute-start(bf16[512,512]{1,0:T(8,128)(2,1)S(1)} %convolution_convert_fusion.5), channel_id=1, source_target_pairs={{0,192},{64,0},{128,64},{192,128},{1,193},{65,1},{129,65},{193,129... | collective-permute-start | bytes 1572872 | tf_op jit(solution)/shard_map/ppermute | solution.py:26
  90.4 7.0 %copy-start.19 = (bf16[1024,512]{1,0:T(8,128)(2,1)S(1)}, bf16[1024,512]{1,0:T(8,128)(2,1)}, u32[]{:S(2)}) copy-start(bf16[1024,512]{1,0:T(8,128)(2,1)} %shard_map.63.first) | copy-start | bytes 3145732
  90.4 7.0 %copy-start.25 = (bf16[1024,512]{1,0:T(8,128)(2,1)S(1)}, bf16[1024,512]{1,0:T(8,128)(2,1)}, u32[]{:S(2)}) copy-start(bf16[1024,512]{1,0:T(8,128)(2,1)} %get-tuple-element.45) | copy-start | bytes 3145732
  97.0 74.1 %collective-permute-start.20 = (bf16[4,1024,256]{2,1,0:T(8,128)(2,1)}, bf16[4,1024,256]{2,1,0:T(8,128)(2,1)}, u32[]{:S(2)}, u32[]{:S(2)}) collective-permute-start(bf16[4,1024,256]{2,1,0:T(8,128)(2,1)} %shard_map.65), channel_id=1, source_target_pairs={{0,1},{1,0},{2,3},{3,2},{4,5},{5,4},{6,7},{7,6},{8,9},{9,8},{10,11... | collective-permute-start | bytes 6291464 | tf_op jit(solution)/shard_map/ppermute | solution.py:30
  98.1 15.0 %collective-permute-start.17 = (bf16[512,512]{1,0:T(8,128)(2,1)S(1)}, bf16[512,512]{1,0:T(8,128)(2,1)S(1)}, u32[]{:S(2)}, u32[]{:S(2)}) collective-permute-start(bf16[512,512]{1,0:T(8,128)(2,1)S(1)} %convolution_convert_fusion.4), channel_id=1, source_target_pairs={{0,128},{64,192},{128,0},{192,64},{1,129},{65,193},{129,1},{193,65... | collective-permute-start | bytes 1572872 | tf_op jit(solution)/shard_map/ppermute | solution.py:26
  98.6 26.2 %collective-permute-start.18 = (bf16[512,512]{1,0:T(8,128)(2,1)S(1)}, bf16[512,512]{1,0:T(8,128)(2,1)S(1)}, u32[]{:S(2)}, u32[]{:S(2)}) collective-permute-start(bf16[512,512]{1,0:T(8,128)(2,1)S(1)} %convolution_convert_fusion.3), channel_id=1, source_target_pairs={{0,64},{64,128},{128,192},{192,0},{1,65},{65,129},{129,193},{193,1... | collective-permute-start | bytes 1572872 | tf_op jit(solution)/shard_map/ppermute | solution.py:26
  100.0 24.8 %copy-start.23 = (bf16[1024,512]{1,0:T(8,128)(2,1)S(1)}, bf16[1024,512]{1,0:T(8,128)(2,1)}, u32[]{:S(2)}) copy-start(bf16[1024,512]{1,0:T(8,128)(2,1)} %get-tuple-element.44) | copy-start | bytes 3145732
  126.4 38.0 %all-to-all-start.2 = ((bf16[8,64,512]{2,1,0:T(8,128)(2,1)}), bf16[8,64,512]{2,1,0:T(8,128)(2,1)S(1)}, u32[]{:S(2)}, u32[]{:S(2)}) async-start(bf16[8,64,512]{2,1,0:T(8,128)(2,1)} %bitcast.6), calls=%async_computation.2 | async-start | bytes 1048576 | tf_op jit(solution)/shard_map/all_to_all | solution.py:498
  134.1 28.7 %copy-start.24 = (bf16[1024,512]{1,0:T(8,128)(2,1)S(1)}, bf16[1024,512]{1,0:T(8,128)(2,1)}, u32[]{:S(2)}) copy-start(bf16[1024,512]{1,0:T(8,128)(2,1)} %get-tuple-element.44) | copy-start | bytes 3145732
  136.2 14.4 %collective-permute-start.28 = (bf16[512,512]{1,0:T(8,128)(2,1)S(1)}, bf16[512,512]{1,0:T(8,128)(2,1)S(1)}, u32[]{:S(2)}, u32[]{:S(2)}) collective-permute-start(bf16[512,512]{1,0:T(8,128)(2,1)S(1)} %convolution_convert_fusion.2), channel_id=1, source_target_pairs={{0,128},{64,192},{128,0},{192,64},{1,129},{65,193},{129,1},{193,65... | collective-permute-start | bytes 1572872 | tf_op jit(solution)/shard_map/ppermute | solution.py:26
  136.7 26.2 %collective-permute-start.29 = (bf16[512,512]{1,0:T(8,128)(2,1)S(1)}, bf16[512,512]{1,0:T(8,128)(2,1)S(1)}, u32[]{:S(2)}, u32[]{:S(2)}) collective-permute-start(bf16[512,512]{1,0:T(8,128)(2,1)S(1)} %convolution_convert_fusion.1), channel_id=1, source_target_pairs={{0,64},{64,128},{128,192},{192,0},{1,65},{65,129},{129,193},{193,1... | collective-permute-start | bytes 1572872 | tf_op jit(solution)/shard_map/ppermute | solution.py:26
  136.8 26.1 %collective-permute-start.30 = (bf16[512,512]{1,0:T(8,128)(2,1)S(1)}, bf16[512,512]{1,0:T(8,128)(2,1)S(1)}, u32[]{:S(2)}, u32[]{:S(2)}) collective-permute-start(bf16[512,512]{1,0:T(8,128)(2,1)S(1)} %convolution_convert_fusion), channel_id=1, source_target_pairs={{0,192},{64,0},{128,64},{192,128},{1,193},{65,1},{129,65},{193,129... | collective-permute-start | bytes 1572872 | tf_op jit(solution)/shard_map/ppermute | solution.py:26
  164.4 10.7 %copy-start.21 = (bf16[8,64,512]{2,1,0:T(8,128)(2,1)}, bf16[8,64,512]{2,1,0:T(8,128)(2,1)S(1)}, u32[]{:S(2)}) copy-start(bf16[8,64,512]{2,1,0:T(8,128)(2,1)S(1)} %all-to-all-done.2.piece) | copy-start | bytes 1572868
  164.4 32.3 %all-to-all-start.1 = ((bf16[8,64,512]{2,1,0:T(8,128)(2,1)}), bf16[8,64,512]{2,1,0:T(8,128)(2,1)S(1)}, u32[]{:S(2)}, u32[]{:S(2)}) async-start(bf16[8,64,512]{2,1,0:T(8,128)(2,1)} %bitcast.7), calls=%async_computation.1 | async-start | bytes 1048576 | tf_op jit(solution)/shard_map/all_to_all | solution.py:498
  175.1 10.2 %collective-permute-start.24 = (bf16[512,256]{1,0:T(8,128)(2,1)S(1)}, bf16[512,256]{1,0:T(8,128)(2,1)S(1)}, u32[]{:S(2)}, u32[]{:S(2)}) collective-permute-start(bf16[512,256]{1,0:T(8,128)(2,1)S(1)} %get-tuple-element.54), channel_id=1, source_target_pairs={{0,4},{2,6},{4,0},{6,2},{1,5},{3,7},{5,1},{7,3},{8,12},{10,14},{12... | collective-permute-start | bytes 786440 | tf_op jit(solution)/shard_map/ppermute | solution.py:26
  177.9 13.7 %collective-permute-start.25 = (bf16[512,256]{1,0:T(8,128)(2,1)S(1)}, bf16[512,256]{1,0:T(8,128)(2,1)S(1)}, u32[]{:S(2)}, u32[]{:S(2)}) collective-permute-start(bf16[512,256]{1,0:T(8,128)(2,1)S(1)} %get-tuple-element.55), channel_id=1, source_target_pairs={{0,2},{2,4},{4,6},{6,0},{1,3},{3,5},{5,7},{7,1},{8,10},{10,12},{12... | collective-permute-start | bytes 786440 | tf_op jit(solution)/shard_map/ppermute | solution.py:26
  178.2 13.4 %collective-permute-start.26 = (bf16[512,256]{1,0:T(8,128)(2,1)S(1)}, bf16[512,256]{1,0:T(8,128)(2,1)S(1)}, u32[]{:S(2)}, u32[]{:S(2)}) collective-permute-start(bf16[512,256]{1,0:T(8,128)(2,1)S(1)} %get-tuple-element.56), channel_id=1, source_target_pairs={{0,6},{2,0},{4,2},{6,4},{1,7},{3,1},{5,3},{7,5},{8,14},{10,8},{12,... | collective-permute-start | bytes 786440 | tf_op jit(solution)/shard_map/ppermute | solution.py:26
  184.6 15.4 %collective-permute-start.21 = (bf16[512,256]{1,0:T(8,128)(2,1)S(1)}, bf16[512,256]{1,0:T(8,128)(2,1)S(1)}, u32[]{:S(2)}, u32[]{:S(2)}) collective-permute-start(bf16[512,256]{1,0:T(8,128)(2,1)S(1)} %get-tuple-element.51), channel_id=1, source_target_pairs={{0,4},{2,6},{4,0},{6,2},{1,5},{3,7},{5,1},{7,3},{8,12},{10,14},{12... | collective-permute-start | bytes 786440 | tf_op jit(solution)/shard_map/ppermute | solution.py:26
  184.7 17.1 %collective-permute-start.22 = (bf16[512,256]{1,0:T(8,128)(2,1)S(1)}, bf16[512,256]{1,0:T(8,128)(2,1)S(1)}, u32[]{:S(2)}, u32[]{:S(2)}) collective-permute-start(bf16[512,256]{1,0:T(8,128)(2,1)S(1)} %get-tuple-element.52), channel_id=1, source_target_pairs={{0,2},{2,4},{4,6},{6,0},{1,3},{3,5},{5,7},{7,1},{8,10},{10,12},{12... | collective-permute-start | bytes 786440 | tf_op jit(solution)/shard_map/ppermute | solution.py:26
  185.3 16.5 %collective-permute-start.23 = (bf16[512,256]{1,0:T(8,128)(2,1)S(1)}, bf16[512,256]{1,0:T(8,128)(2,1)S(1)}, u32[]{:S(2)}, u32[]{:S(2)}) collective-permute-start(bf16[512,256]{1,0:T(8,128)(2,1)S(1)} %get-tuple-element.53), channel_id=1, source_target_pairs={{0,6},{2,0},{4,2},{6,4},{1,7},{3,1},{5,3},{7,5},{8,14},{10,8},{12,... | collective-permute-start | bytes 786440 | tf_op jit(solution)/shard_map/ppermute | solution.py:26
  191.8 8.2 %collective-permute-start.27 = (bf16[512,256]{1,0:T(8,128)(2,1)S(1)}, bf16[512,256]{1,0:T(8,128)(2,1)S(1)}, u32[]{:S(2)}, u32[]{:S(2)}) collective-permute-start(bf16[512,256]{1,0:T(8,128)(2,1)S(1)} %add_convert_fusion.1), channel_id=1, source_target_pairs={{0,8},{8,0},{1,9},{9,1},{2,10},{10,2},{3,11},{11,3},{4,12},{12,4},... | collective-permute-start | bytes 786440 | tf_op jit(solution)/shard_map/ppermute | solution.py:30
  (14 other events, 31.9 us)
